TPU v7x, 32 devices: a whole 2x2x4 slice. The times are simulated.
32 devices in a mesh: dp: 2 (over core), tensor: 16 (over z, y, x).
Axes of the slice: x: 2, y: 2, z: 4, core: 2. Of those that a mesh axis runs over, the one named last changes fastest.
Arguments:
- gradient: float32 [2, 8192, 512], P('dp', 'tensor'), may hold values from -80 to 80
Outputs:
- update: bfloat16 [2, 8192, 512], P(None, 'tensor')
All inputs are finite; a program needn't handle non-finite values.
Results may differ from a plain program's by a relative error of at most 0.001.
Values may be sent and summed in bfloat16 or wider, within the bound.
No kernel may reach another device: no remote copies, remote signals or barrier semaphores. Data moves between devices by JAX's collectives and lax.ppermute only.
A program may use at most 64 MiB of HBM per device.

v0:
```python
import functools
import math

import jax
import jax.numpy as jnp
from jax import lax
from jax.experimental import pallas as pl
from jax.experimental.pallas import tpu as pltpu
from jax.sharding import PartitionSpec as P

FEATURES = 8192
OUTPUTS = 512
ITERS = 3

linear_term = 3.4445
cubic_term = -4.775
quintic_term = 2.0315
norm_floor = 1e-07
update_gain = 0.2

LANES = 128
GRAM_VMEM = 16 << 20
UPDATE_VMEM = 32 << 20
PLACE_VMEM = 4 << 20
SUBLANES = 8


GROUP = 8
SOUTH = (3, 4, 2, 0)
NORTH = (7, 6, 5, 1)


def split(value):
    high = value.astype(jnp.bfloat16)
    low = (value - high.astype(jnp.float32)).astype(jnp.bfloat16)
    return high, low


def wide(value, axis):
    high, low = split(value)
    return jnp.concatenate([high, high, low] if axis == 1 else [high, low, high], axis=axis)


def dot(first, second, contract=(1, 0)):
    return lax.dot_general(
        first, second, (((contract[0],), (contract[1],)), ((), ())), preferred_element_type=jnp.float32
    )


def grid_pair(half):
    shape = (half, half)
    return lax.broadcasted_iota(jnp.int32, shape, 0), lax.broadcasted_iota(jnp.int32, shape, 1)


def block_starts(rows):
    me = lax.rem(lax.axis_index("tensor"), GROUP)
    north = lax.rem(lax.axis_index("dp"), 2) == 1
    own, other = [], []
    for first, second in zip(SOUTH, NORTH):
        own.append(pl.multiple_of((me ^ jnp.where(north, second, first)) * rows, rows))
        other.append(pl.multiple_of((me ^ jnp.where(north, first, second)) * rows, rows))
    return own, other


def gram_kernel(gradient_ref, *refs):
    slots = len(SOUTH)
    chunks, send, (mixed, cross) = refs[:slots], refs[slots], refs[slots + 1 :]
    half = mixed.shape[0]
    rows = half // GROUP
    size = chunks[0].shape[0]
    high, low = split(gradient_ref[0])
    left = jnp.concatenate([high, high, low], axis=0)
    right = jnp.concatenate([high, low, high], axis=0)
    first = dot(left[:, :half], right[:, :half], (0, 0))
    cross[...] = dot(left[:, :half], right[:, half:], (0, 0))
    second = dot(left[:, half:], right[:, half:], (0, 0))
    row, column = grid_pair(half)
    mixed[...] = jnp.where(row <= column, first, second)
    diagonal = jnp.sum(jnp.where(row == column, second, 0.0), axis=0, keepdims=True)
    which = lax.broadcasted_iota(jnp.int32, (SUBLANES, LANES), 0)
    tile = jnp.zeros((SUBLANES, LANES), jnp.float32)
    for index in range(half // LANES):
        part = diagonal[:, index * LANES : (index + 1) * LANES]
        tile = jnp.where(which == index, jnp.broadcast_to(part, (SUBLANES, LANES)), tile)

    def write(out, at, start):
        for source in (cross, mixed):
            for lane in range(0, half, LANES):
                out[at : at + rows, :] = source[pl.ds(start, rows), lane : lane + LANES]
                at += rows
        out[at : at + SUBLANES, :] = tile

    own, other = block_starts(rows)
    for slot in range(slots):
        write(send, slot * size, other[slot])
    for slot in range(slots):
        write(chunks[slot], 0, own[slot])


def update_kernel(gain, *refs):
    slots = len(SOUTH)
    own_chunks, other_chunks = refs[:slots], refs[slots : 2 * slots]
    gradient_ref, update_ref, whole_hbm, mixed, cross, store_sem = refs[2 * slots :]
    half = mixed.shape[0]
    rows = half // GROUP
    own, other = block_starts(rows)
    for source, start in zip((*own_chunks, *other_chunks), own + other):
        at = 0
        for target in (cross, mixed):
            for lane in range(0, half, LANES):
                target[pl.ds(start, rows), lane : lane + LANES] = source[at : at + rows, :]
                at += rows
    diagonal = jnp.concatenate([own_chunks[0][at + i : at + i + 1, :] for i in range(half // LANES)], axis=1)
    row, column = grid_pair(half)
    packed = mixed[...]
    flipped = packed.T
    first = jnp.where(row <= column, packed, flipped)
    second = jnp.where(row > column, packed, flipped)
    on_diagonal = row == column
    second = jnp.where(on_diagonal, jnp.broadcast_to(diagonal, (half, half)), second)
    corner = cross[...]
    norm = jnp.sum(jnp.where(on_diagonal, first + second, 0.0), keepdims=True)
    divisor = jnp.sqrt(norm) + norm_floor
    scale = 1.0 / (divisor * divisor)
    gram = jnp.concatenate(
        [jnp.concatenate([first, corner], axis=1), jnp.concatenate([corner.T, second], axis=1)], axis=0
    )
    gram = gram * scale
    row, column = grid_pair(2 * half)
    identity = jnp.where(row == column, linear_term, 0.0)
    total = None
    for turn in range(ITERS):
        gram_left, gram_right = wide(gram, 1), wide(gram, 0)
        squared = dot(gram_left, gram_right)
        polynomial = identity + cubic_term * gram + quintic_term * squared
        polynomial_right = wide(polynomial, 0)
        total = polynomial if total is None else dot(wide(total, 1), polynomial_right)
        if turn + 1 < ITERS:
            gram = dot(wide(dot(gram_left, polynomial_right), 1), polynomial_right)
    polished = dot(wide(gradient_ref[0], 1), wide(total, 0))
    update_ref[0] = ((gain / divisor) * polished).astype(jnp.bfloat16)
    store = pltpu.make_async_copy(update_ref.at[0], whole_hbm.at[lax.axis_index("dp")], store_sem)
    store.start()
    store.wait()


def place_kernel(other_ref, whole_in, whole_hbm, sem):
    del whole_in
    copy = pltpu.make_async_copy(other_ref.at[0], whole_hbm.at[1 - lax.axis_index("dp")], sem)
    copy.start()
    copy.wait()


def on_device(mesh, gradient):
    pairs, size = mesh.shape["dp"], mesh.shape["tensor"]
    assert pairs % 2 == 0 and size % GROUP == 0 and size & (size - 1) == 0
    _, features, outputs = gradient.shape
    half, slots = outputs // 2, len(SOUTH)
    assert half // LANES <= SUBLANES
    length = 2 * half // GROUP * (half // LANES) + SUBLANES
    chunk = jax.ShapeDtypeStruct((length, LANES), jnp.float32)
    vmem = pl.BlockSpec(memory_space=pltpu.VMEM)
    anywhere = pl.BlockSpec(memory_space=pl.ANY)

    def flip(value):
        return lax.ppermute(value, "dp", [(d, d ^ 1) for d in range(pairs)])

    def far(value, step):
        return lax.ppermute(value, "tensor", [(i, i ^ step) for i in range(size)])

    def near(value, slot):
        partner = (SOUTH[slot], NORTH[slot])
        moves = [(d * size + i, d * size + (i ^ partner[d % 2])) for d in range(pairs) for i in range(size)]
        return lax.ppermute(value, ("dp", "tensor"), moves)

    *own, send = pl.pallas_call(
        gram_kernel,
        out_shape=[chunk] * slots + [jax.ShapeDtypeStruct((slots * length, LANES), jnp.float32)],
        in_specs=[vmem],
        out_specs=[vmem] * (slots + 1),
        scratch_shapes=[pltpu.VMEM((half, half), jnp.float32)] * 2,
        compiler_params=pltpu.CompilerParams(vmem_limit_bytes=GRAM_VMEM),
        name="gram",
    )(gradient)
    held = flip(send)
    arrived = []
    for slot in range(slots):
        message = jnp.concatenate([own[slot], held[slot * length : (slot + 1) * length]])
        arrived.append(near(message, slot))
    partial = functools.reduce(jnp.add, arrived)
    mine = partial[:length] + flip(partial[length:])
    step = GROUP
    while step < size:
        mine = mine + far(mine, step)
        step *= 2
    both = jnp.concatenate([mine, flip(mine)])
    gathered = [near(both, slot) for slot in range(slots)]
    passed = [flip(value[length:]) for value in gathered]
    gain = update_gain * math.sqrt(max(FEATURES, OUTPUTS))
    whole = jax.ShapeDtypeStruct((pairs, features, outputs), jnp.bfloat16)
    update, placed = pl.pallas_call(
        functools.partial(update_kernel, gain),
        out_shape=[jax.ShapeDtypeStruct(gradient.shape, jnp.bfloat16), whole],
        in_specs=[vmem] * (2 * slots + 1),
        out_specs=[vmem, anywhere],
        scratch_shapes=[
            pltpu.VMEM((half, half), jnp.float32),
            pltpu.VMEM((half, half), jnp.float32),
            pltpu.SemaphoreType.DMA,
        ],
        compiler_params=pltpu.CompilerParams(vmem_limit_bytes=UPDATE_VMEM),
        name="update",
    )(*gathered, *passed, gradient)
    if pairs != 2:
        return lax.all_gather(update, "dp", axis=0, tiled=True)
    other = lax.ppermute(update, "dp", [(0, 1), (1, 0)])
    return pl.pallas_call(
        place_kernel,
        out_shape=whole,
        in_specs=[vmem, anywhere],
        out_specs=anywhere,
        scratch_shapes=[pltpu.SemaphoreType.DMA],
        input_output_aliases={1: 0},
        compiler_params=pltpu.CompilerParams(vmem_limit_bytes=PLACE_VMEM),
        name="place",
    )(other, placed)


def solution(mesh):
    placed = (P("dp", "tensor", None),)
    return jax.shard_map(
        functools.partial(on_device, mesh), mesh=mesh, in_specs=placed, out_specs=P(None, "tensor", None), check_vma=False
    )
```

profile of v0, /device:TPU:0, one launch (start us, length us, event | category | flops | bytes accessed | tf_op | source)
XLA Modules:
  0.0 51.9 jit_solution(12136630998452157776)
XLA Ops:
  0.0 1.2 %copy-done = f32[1,512,512]{2,1,0:T(8,128)S(1)} copy-done((f32[1,512,512]{2,1,0:T(8,128)S(1)}, f32[1,512,512]{2,1,0:T(8,128)}, u32[]{:S(2)}) %copy-start) | copy-done | bytes 1048600
  1.2 0.9 %gram.1 = (f32[136,128]{1,0:T(8,128)S(1)}, f32[136,128]{1,0:T(8,128)S(1)}, f32[136,128]{1,0:T(8,128)S(1)}, f32[136,128]{1,0:T(8,128)S(1)}, f32[544,128]{1,0:T(8,128)S(1)}) custom-call(f32[1,512,512]{2,1,0:T(8,128)S(1)} %copy-done), custom_call_target="tpu_custom_call" | custom-call | tf_op jit(solution)/shard_map/gram/pallas_call | solution.py:176
  2.6 1.2 %collective-permute-done = f32[544,128]{1,0:T(8,128)S(1)} collective-permute-done((f32[544,128]{1,0:T(8,128)S(1)}, f32[544,128]{1,0:T(8,128)S(1)}, u32[]{:S(2)}, u32[]{:S(2)}) %collective-permute-start) | collective-permute-done | bytes 278560 | tf_op jit(solution)/shard_map/ppermute | solution.py:166
  3.9 3.9 %collective-permute-start.1 = (f32[272,128]{1,0:T(8,128)S(1)}, f32[272,128]{1,0:T(8,128)S(1)}, u32[]{:S(2)}, u32[]{:S(2)}) collective-permute-start(f32[272,128]{1,0:T(8,128)S(1)} %pad_maximum_fusion), channel_id=1, source_target_pairs={{0,3},{1,2},{2,1},{3,0},{4,7},{5,6},{6,5},{7,4},{8,11},{9,10},{10,... | collective-permute-start | bytes 417800 | tf_op jit(solution)/shard_map/ppermute | solution.py:174
  8.3 0.7 %collective-permute-start.4 = (f32[272,128]{1,0:T(8,128)S(1)}, f32[272,128]{1,0:T(8,128)S(1)}, u32[]{:S(2)}, u32[]{:S(2)}) collective-permute-start(f32[272,128]{1,0:T(8,128)S(1)} %pad_maximum_fusion.3), channel_id=1, source_target_pairs={{0,0},{1,1},{2,2},{3,3},{4,4},{5,5},{6,6},{7,7},{8,8},{9,9},{10,10... | collective-permute-start | bytes 417800 | tf_op jit(solution)/shard_map/ppermute | solution.py:174
  9.1 1.6 %collective-permute-start.2 = (f32[272,128]{1,0:T(8,128)S(1)}, f32[272,128]{1,0:T(8,128)S(1)}, u32[]{:S(2)}, u32[]{:S(2)}) collective-permute-start(f32[272,128]{1,0:T(8,128)S(1)} %pad_maximum_fusion.1), channel_id=1, source_target_pairs={{0,4},{1,5},{2,6},{3,7},{4,0},{5,1},{6,2},{7,3},{8,12},{9,13},{10,... | collective-permute-start | bytes 417800 | tf_op jit(solution)/shard_map/ppermute | solution.py:174
  10.7 3.7 %collective-permute-done.1 = f32[272,128]{1,0:T(8,128)S(1)} collective-permute-done((f32[272,128]{1,0:T(8,128)S(1)}, f32[272,128]{1,0:T(8,128)S(1)}, u32[]{:S(2)}, u32[]{:S(2)}) %collective-permute-start.1) | collective-permute-done | bytes 139296 | tf_op jit(solution)/shard_map/ppermute | solution.py:174
  14.5 2.5 %collective-permute-start.5 = (f32[136,128]{1,0:T(8,128)S(1)}, f32[136,128]{1,0:T(8,128)S(1)}, u32[]{:S(2)}, u32[]{:S(2)}) collective-permute-start(f32[136,128]{1,0:T(8,128)S(1)} %slice.45), channel_id=1, source_target_pairs={{0,16},{16,0},{1,17},{17,1},{2,18},{18,2},{3,19},{19,3},{4,20},{20... | collective-permute-start | bytes 208904 | tf_op jit(solution)/shard_map/ppermute | solution.py:166
  17.0 0.9 %collective-permute-done.5 = f32[136,128]{1,0:T(8,128)S(1)} collective-permute-done((f32[136,128]{1,0:T(8,128)S(1)}, f32[136,128]{1,0:T(8,128)S(1)}, u32[]{:S(2)}, u32[]{:S(2)}) %collective-permute-start.5) | collective-permute-done | bytes 69664 | tf_op jit(solution)/shard_map/ppermute | solution.py:166
  17.9 2.6 %collective-permute-start.6 = (f32[136,128]{1,0:T(8,128)S(1)}, f32[136,128]{1,0:T(8,128)S(1)}, u32[]{:S(2)}, u32[]{:S(2)}) collective-permute-start(f32[136,128]{1,0:T(8,128)S(1)} %slice_add_fusion), channel_id=1, source_target_pairs={{0,8},{1,9},{2,10},{3,11},{4,12},{5,13},{6,14},{7,15},{8,0},{9,1},... | collective-permute-start | bytes 208904 | tf_op jit(solution)/shard_map/ppermute | solution.py:169
  20.6 4.2 %collective-permute-done.6 = f32[136,128]{1,0:T(8,128)S(1)} collective-permute-done((f32[136,128]{1,0:T(8,128)S(1)}, f32[136,128]{1,0:T(8,128)S(1)}, u32[]{:S(2)}, u32[]{:S(2)}) %collective-permute-start.6) | collective-permute-done | bytes 69664 | tf_op jit(solution)/shard_map/ppermute | solution.py:169
  24.9 1.2 %collective-permute-done.7 = f32[136,128]{1,0:T(8,128)S(1)} collective-permute-done((f32[136,128]{1,0:T(8,128)S(1)}, f32[136,128]{1,0:T(8,128)S(1)}, u32[]{:S(2)}, u32[]{:S(2)}) %collective-permute-start.7) | collective-permute-done | bytes 69664 | tf_op jit(solution)/shard_map/ppermute | solution.py:166
  26.2 0.7 %collective-permute-start.11 = (f32[272,128]{1,0:T(8,128)S(1)}, f32[272,128]{1,0:T(8,128)S(1)}, u32[]{:S(2)}, u32[]{:S(2)}) collective-permute-start(f32[272,128]{1,0:T(8,128)S(1)} %pad_maximum_fusion.4), channel_id=1, source_target_pairs={{0,0},{1,1},{2,2},{3,3},{4,4},{5,5},{6,6},{7,7},{8,8},{9,9},{10,10... | collective-permute-start | bytes 417800 | tf_op jit(solution)/shard_map/ppermute | solution.py:174
  26.9 0.6 %collective-permute-start.10 = (f32[272,128]{1,0:T(8,128)S(1)}, f32[272,128]{1,0:T(8,128)S(1)}, u32[]{:S(2)}, u32[]{:S(2)}) collective-permute-start(f32[272,128]{1,0:T(8,128)S(1)} %pad_maximum_fusion.4), channel_id=1, source_target_pairs={{0,2},{1,3},{2,0},{3,1},{4,6},{5,7},{6,4},{7,5},{8,10},{9,11},{10,... | collective-permute-start | bytes 417800 | tf_op jit(solution)/shard_map/ppermute | solution.py:174
  27.4 0.7 %collective-permute-start.9 = (f32[272,128]{1,0:T(8,128)S(1)}, f32[272,128]{1,0:T(8,128)S(1)}, u32[]{:S(2)}, u32[]{:S(2)}) collective-permute-start(f32[272,128]{1,0:T(8,128)S(1)} %pad_maximum_fusion.4), channel_id=1, source_target_pairs={{0,4},{1,5},{2,6},{3,7},{4,0},{5,1},{6,2},{7,3},{8,12},{9,13},{10,... | collective-permute-start | bytes 417800 | tf_op jit(solution)/shard_map/ppermute | solution.py:174
  28.1 1.8 %collective-permute-start.8 = (f32[272,128]{1,0:T(8,128)S(1)}, f32[272,128]{1,0:T(8,128)S(1)}, u32[]{:S(2)}, u32[]{:S(2)}) collective-permute-start(f32[272,128]{1,0:T(8,128)S(1)} %pad_maximum_fusion.4), channel_id=1, source_target_pairs={{0,3},{1,2},{2,1},{3,0},{4,7},{5,6},{6,5},{7,4},{8,11},{9,10},{10,... | collective-permute-start | bytes 417800 | tf_op jit(solution)/shard_map/ppermute | solution.py:174
  29.9 2.7 %collective-permute-start.15 = (f32[136,128]{1,0:T(8,128)S(1)}, f32[136,128]{1,0:T(8,128)S(1)}, u32[]{:S(2)}, u32[]{:S(2)}) collective-permute-start(f32[136,128]{1,0:T(8,128)S(1)} %slice.49), channel_id=1, source_target_pairs={{0,16},{16,0},{1,17},{17,1},{2,18},{18,2},{3,19},{19,3},{4,20},{20... | collective-permute-start | bytes 208904 | tf_op jit(solution)/shard_map/ppermute | solution.py:166
  32.6 2.6 %collective-permute-start.14 = (f32[136,128]{1,0:T(8,128)S(1)}, f32[136,128]{1,0:T(8,128)S(1)}, u32[]{:S(2)}, u32[]{:S(2)}) collective-permute-start(f32[136,128]{1,0:T(8,128)S(1)} %slice.48), channel_id=1, source_target_pairs={{0,16},{16,0},{1,17},{17,1},{2,18},{18,2},{3,19},{19,3},{4,20},{20... | collective-permute-start | bytes 208904 | tf_op jit(solution)/shard_map/ppermute | solution.py:166
  35.2 1.3 %collective-permute-start.13 = (f32[136,128]{1,0:T(8,128)S(1)}, f32[136,128]{1,0:T(8,128)S(1)}, u32[]{:S(2)}, u32[]{:S(2)}) collective-permute-start(f32[136,128]{1,0:T(8,128)S(1)} %slice.47), channel_id=1, source_target_pairs={{0,16},{16,0},{1,17},{17,1},{2,18},{18,2},{3,19},{19,3},{4,20},{20... | collective-permute-start | bytes 208904 | tf_op jit(solution)/shard_map/ppermute | solution.py:166
  36.5 1.7 %collective-permute-start.12 = (f32[136,128]{1,0:T(8,128)S(1)}, f32[136,128]{1,0:T(8,128)S(1)}, u32[]{:S(2)}, u32[]{:S(2)}) collective-permute-start(f32[136,128]{1,0:T(8,128)S(1)} %slice.46), channel_id=1, source_target_pairs={{0,16},{16,0},{1,17},{17,1},{2,18},{18,2},{3,19},{19,3},{4,20},{20... | collective-permute-start | bytes 208904 | tf_op jit(solution)/shard_map/ppermute | solution.py:166
  38.2 0.9 %collective-permute-done.12.refs_4_ = f32[136,128]{1,0:T(8,128)S(1)} collective-permute-done((f32[136,128]{1,0:T(8,128)S(1)}, f32[136,128]{1,0:T(8,128)S(1)}, u32[]{:S(2)}, u32[]{:S(2)}) %collective-permute-start.12) | collective-permute-done | bytes 69664 | tf_op jit(solution)/shard_map/ppermute | solution.py:166
  39.1 10.0 %update.1 = (bf16[1,512,512]{2,1,0:T(8,128)(2,1)S(1)}, bf16[2,512,512]{2,1,0:T(8,128)(2,1)}) custom-call(f32[272,128]{1,0:T(8,128)S(1)} %collective-permute-done.8.refs_0_, f32[272,128]{1,0:T(8,128)S(1)} %collective-permute-done.9.refs_1_, f32[272,128]{1,0:T(8,128)S(1)} %collective-permute-done.10.refs_2_, f32[272,128]{1,0:T(8,128)S(1)} %collective-permute-done.11.refs_3_, ...), custom_call_target="tpu_custom_call" | custom-call | tf_op jit(solution)/shard_map/update/pallas_call | solution.py:201
  49.5 1.5 %collective-permute-done.16.other_ref = bf16[1,512,512]{2,1,0:T(8,128)(2,1)S(1)} collective-permute-done((bf16[1,512,512]{2,1,0:T(8,128)(2,1)S(1)}, bf16[1,512,512]{2,1,0:T(8,128)(2,1)S(1)}, u32[]{:S(2)}, u32[]{:S(2)}) %collective-permute-start.16) | collective-permute-done | bytes 524320 | tf_op jit(solution)/shard_map/ppermute | solution.py:216
  51.1 0.8 %place.1 = bf16[2,512,512]{2,1,0:T(8,128)(2,1)} custom-call(bf16[1,512,512]{2,1,0:T(8,128)(2,1)S(1)} %collective-permute-done.16.other_ref, bf16[2,512,512]{2,1,0:T(8,128)(2,1)} %get-tuple-element.18.whole_in), custom_call_target="tpu_custom_call", output_to_operand_aliasing={{}: (1, {})} | custom-call | tf_op jit(solution)/shard_map/place/pallas_call | solution.py:217
  (31 shorter events, 2.0 us)
Async XLA Ops:
  0.0 1.2 %copy-start = (f32[1,512,512]{2,1,0:T(8,128)S(1)}, f32[1,512,512]{2,1,0:T(8,128)}, u32[]{:S(2)}) copy-start(f32[1,512,512]{2,1,0:T(8,128)} %refs_8_.1) | copy-start | bytes 3145732
  2.1 1.7 %collective-permute-start = (f32[544,128]{1,0:T(8,128)S(1)}, f32[544,128]{1,0:T(8,128)S(1)}, u32[]{:S(2)}, u32[]{:S(2)}) collective-permute-start(f32[544,128]{1,0:T(8,128)S(1)} %get-tuple-element.13), channel_id=1, source_target_pairs={{0,16},{16,0},{1,17},{17,1},{2,18},{18,2},{3,19},{19,3},{4,20},{20... | collective-permute-start | bytes 835592 | tf_op jit(solution)/shard_map/ppermute | solution.py:166
  3.9 10.5 %collective-permute-start.1 = (f32[272,128]{1,0:T(8,128)S(1)}, f32[272,128]{1,0:T(8,128)S(1)}, u32[]{:S(2)}, u32[]{:S(2)}) collective-permute-start(f32[272,128]{1,0:T(8,128)S(1)} %pad_maximum_fusion), channel_id=1, source_target_pairs={{0,3},{1,2},{2,1},{3,0},{4,7},{5,6},{6,5},{7,4},{8,11},{9,10},{10,... | collective-permute-start | bytes 417800 | tf_op jit(solution)/shard_map/ppermute | solution.py:174
  7.8 6.6 %collective-permute-start.3 = (f32[272,128]{1,0:T(8,128)S(1)}, f32[272,128]{1,0:T(8,128)S(1)}, u32[]{:S(2)}, u32[]{:S(2)}) collective-permute-start(f32[272,128]{1,0:T(8,128)S(1)} %pad_maximum_fusion.2), channel_id=1, source_target_pairs={{0,2},{1,3},{2,0},{3,1},{4,6},{5,7},{6,4},{7,5},{8,10},{9,11},{10,... | collective-permute-start | bytes 417800 | tf_op jit(solution)/shard_map/ppermute | solution.py:174
  8.3 6.0 %collective-permute-start.4 = (f32[272,128]{1,0:T(8,128)S(1)}, f32[272,128]{1,0:T(8,128)S(1)}, u32[]{:S(2)}, u32[]{:S(2)}) collective-permute-start(f32[272,128]{1,0:T(8,128)S(1)} %pad_maximum_fusion.3), channel_id=1, source_target_pairs={{0,0},{1,1},{2,2},{3,3},{4,4},{5,5},{6,6},{7,7},{8,8},{9,9},{10,10... | collective-permute-start | bytes 417800 | tf_op jit(solution)/shard_map/ppermute | solution.py:174
  9.0 30.1 %copy-start.1 = (f32[1,512,512]{2,1,0:T(8,128)S(1)}, f32[1,512,512]{2,1,0:T(8,128)}, u32[]{:S(2)}) copy-start(f32[1,512,512]{2,1,0:T(8,128)} %refs_8_.1) | copy-start | bytes 3145732
  9.1 5.4 %collective-permute-start.2 = (f32[272,128]{1,0:T(8,128)S(1)}, f32[272,128]{1,0:T(8,128)S(1)}, u32[]{:S(2)}, u32[]{:S(2)}) collective-permute-start(f32[272,128]{1,0:T(8,128)S(1)} %pad_maximum_fusion.1), channel_id=1, source_target_pairs={{0,4},{1,5},{2,6},{3,7},{4,0},{5,1},{6,2},{7,3},{8,12},{9,13},{10,... | collective-permute-start | bytes 417800 | tf_op jit(solution)/shard_map/ppermute | solution.py:174
  14.5 3.4 %collective-permute-start.5 = (f32[136,128]{1,0:T(8,128)S(1)}, f32[136,128]{1,0:T(8,128)S(1)}, u32[]{:S(2)}, u32[]{:S(2)}) collective-permute-start(f32[136,128]{1,0:T(8,128)S(1)} %slice.45), channel_id=1, source_target_pairs={{0,16},{16,0},{1,17},{17,1},{2,18},{18,2},{3,19},{19,3},{4,20},{20... | collective-permute-start | bytes 208904 | tf_op jit(solution)/shard_map/ppermute | solution.py:166
  17.9 6.9 %collective-permute-start.6 = (f32[136,128]{1,0:T(8,128)S(1)}, f32[136,128]{1,0:T(8,128)S(1)}, u32[]{:S(2)}, u32[]{:S(2)}) collective-permute-start(f32[136,128]{1,0:T(8,128)S(1)} %slice_add_fusion), channel_id=1, source_target_pairs={{0,8},{1,9},{2,10},{3,11},{4,12},{5,13},{6,14},{7,15},{8,0},{9,1},... | collective-permute-start | bytes 208904 | tf_op jit(solution)/shard_map/ppermute | solution.py:169
  24.8 1.3 %collective-permute-start.7 = (f32[136,128]{1,0:T(8,128)S(1)}, f32[136,128]{1,0:T(8,128)S(1)}, u32[]{:S(2)}, u32[]{:S(2)}) collective-permute-start(f32[136,128]{1,0:T(8,128)S(1)} %add.19), channel_id=1, source_target_pairs={{0,16},{16,0},{1,17},{17,1},{2,18},{18,2},{3,19},{19,3},{4,20},{20... | collective-permute-start | bytes 208904 | tf_op jit(solution)/shard_map/ppermute | solution.py:166
  26.2 3.7 %collective-permute-start.11 = (f32[272,128]{1,0:T(8,128)S(1)}, f32[272,128]{1,0:T(8,128)S(1)}, u32[]{:S(2)}, u32[]{:S(2)}) collective-permute-start(f32[272,128]{1,0:T(8,128)S(1)} %pad_maximum_fusion.4), channel_id=1, source_target_pairs={{0,0},{1,1},{2,2},{3,3},{4,4},{5,5},{6,6},{7,7},{8,8},{9,9},{10,10... | collective-permute-start | bytes 417800 | tf_op jit(solution)/shard_map/ppermute | solution.py:174
  26.9 5.8 %collective-permute-start.10 = (f32[272,128]{1,0:T(8,128)S(1)}, f32[272,128]{1,0:T(8,128)S(1)}, u32[]{:S(2)}, u32[]{:S(2)}) collective-permute-start(f32[272,128]{1,0:T(8,128)S(1)} %pad_maximum_fusion.4), channel_id=1, source_target_pairs={{0,2},{1,3},{2,0},{3,1},{4,6},{5,7},{6,4},{7,5},{8,10},{9,11},{10,... | collective-permute-start | bytes 417800 | tf_op jit(solution)/shard_map/ppermute | solution.py:174
  27.4 7.8 %collective-permute-start.9 = (f32[272,128]{1,0:T(8,128)S(1)}, f32[272,128]{1,0:T(8,128)S(1)}, u32[]{:S(2)}, u32[]{:S(2)}) collective-permute-start(f32[272,128]{1,0:T(8,128)S(1)} %pad_maximum_fusion.4), channel_id=1, source_target_pairs={{0,4},{1,5},{2,6},{3,7},{4,0},{5,1},{6,2},{7,3},{8,12},{9,13},{10,... | collective-permute-start | bytes 417800 | tf_op jit(solution)/shard_map/ppermute | solution.py:174
  28.1 8.4 %collective-permute-start.8 = (f32[272,128]{1,0:T(8,128)S(1)}, f32[272,128]{1,0:T(8,128)S(1)}, u32[]{:S(2)}, u32[]{:S(2)}) collective-permute-start(f32[272,128]{1,0:T(8,128)S(1)} %pad_maximum_fusion.4), channel_id=1, source_target_pairs={{0,3},{1,2},{2,1},{3,0},{4,7},{5,6},{6,5},{7,4},{8,11},{9,10},{10,... | collective-permute-start | bytes 417800 | tf_op jit(solution)/shard_map/ppermute | solution.py:174
  29.9 8.3 %collective-permute-start.15 = (f32[136,128]{1,0:T(8,128)S(1)}, f32[136,128]{1,0:T(8,128)S(1)}, u32[]{:S(2)}, u32[]{:S(2)}) collective-permute-start(f32[136,128]{1,0:T(8,128)S(1)} %slice.49), channel_id=1, source_target_pairs={{0,16},{16,0},{1,17},{17,1},{2,18},{18,2},{3,19},{19,3},{4,20},{20... | collective-permute-start | bytes 208904 | tf_op jit(solution)/shard_map/ppermute | solution.py:166
  32.6 5.6 %collective-permute-start.14 = (f32[136,128]{1,0:T(8,128)S(1)}, f32[136,128]{1,0:T(8,128)S(1)}, u32[]{:S(2)}, u32[]{:S(2)}) collective-permute-start(f32[136,128]{1,0:T(8,128)S(1)} %slice.48), channel_id=1, source_target_pairs={{0,16},{16,0},{1,17},{17,1},{2,18},{18,2},{3,19},{19,3},{4,20},{20... | collective-permute-start | bytes 208904 | tf_op jit(solution)/shard_map/ppermute | solution.py:166
  35.2 3.0 %collective-permute-start.13 = (f32[136,128]{1,0:T(8,128)S(1)}, f32[136,128]{1,0:T(8,128)S(1)}, u32[]{:S(2)}, u32[]{:S(2)}) collective-permute-start(f32[136,128]{1,0:T(8,128)S(1)} %slice.47), channel_id=1, source_target_pairs={{0,16},{16,0},{1,17},{17,1},{2,18},{18,2},{3,19},{19,3},{4,20},{20... | collective-permute-start | bytes 208904 | tf_op jit(solution)/shard_map/ppermute | solution.py:166
  36.5 2.6 %collective-permute-start.12 = (f32[136,128]{1,0:T(8,128)S(1)}, f32[136,128]{1,0:T(8,128)S(1)}, u32[]{:S(2)}, u32[]{:S(2)}) collective-permute-start(f32[136,128]{1,0:T(8,128)S(1)} %slice.46), channel_id=1, source_target_pairs={{0,16},{16,0},{1,17},{17,1},{2,18},{18,2},{3,19},{19,3},{4,20},{20... | collective-permute-start | bytes 208904 | tf_op jit(solution)/shard_map/ppermute | solution.py:166
  49.1 2.0 %collective-permute-start.16 = (bf16[1,512,512]{2,1,0:T(8,128)(2,1)S(1)}, bf16[1,512,512]{2,1,0:T(8,128)(2,1)S(1)}, u32[]{:S(2)}, u32[]{:S(2)}) collective-permute-start(bf16[1,512,512]{2,1,0:T(8,128)(2,1)S(1)} %get-tuple-element.17), channel_id=1, source_target_pairs={{0,16},{16,0},{1,17},{17,1},{2,18},{18,2},{3,19},{19,3},{4,20},{20... | collective-permute-start | bytes 1572872 | tf_op jit(solution)/shard_map/ppermute | solution.py:216
where the time goes:
time: 52 us; the launch traced here: 51.9 us
  starting transfers between devices  24.9 us (48%)
  waiting for transfers between devices  13.8 us (27%)
  Pallas kernels  11.6 us (22%)
  local copies, waits for them, and re-layouts  1.28 us (2%)
    ppermute x7, starting transfers between devices, flip(): return lax.ppermute(value, 'dp', [(d, d ^ 1) for d in range(pairs)])  11.4 us
    ppermute x8, starting transfers between devices, near(): return lax.ppermute(value, ('dp', 'tensor'), moves)  10.5 us
    pallas_call x1, Pallas kernels, on_device(): pl.pallas_call(functools.partial(update_kernel, gain), out_shape=[jax.Sha...  9.95 us
    ppermute x1, waiting for transfers between devices, far(): return lax.ppermute(value, 'tensor', [(i, i ^ step) for i in range(size)])  4.25 us
    ppermute x7, waiting for transfers between devices, flip(): return lax.ppermute(value, 'dp', [(d, d ^ 1) for d in range(pairs)])  4.24 us
    ppermute x8, waiting for transfers between devices, near(): return lax.ppermute(value, ('dp', 'tensor'), moves)  3.79 us
    ppermute x1, starting transfers between devices, far(): return lax.ppermute(value, 'tensor', [(i, i ^ step) for i in range(size)])  2.65 us
    ppermute x1, waiting for transfers between devices, on_device(): other = lax.ppermute(update, 'dp', [(0, 1), (1, 0)])  1.54 us
  transfers between devices with their start and end apart: 17, of which 8 were waited for; matrix products, arithmetic and copies ran while one was open for 0% of the time, Pallas kernels for 0%

commit v1 on v0

--- a/solution.py
+++ b/solution.py
@@ -26,8 +26,7 @@
 
 
 GROUP = 8
-SOUTH = (3, 4, 2, 0)
-NORTH = (7, 6, 5, 1)
+PARTNERS = (0, 7, 6, 5, 3, 4, 1, 2)
 
 
 def split(value):
@@ -54,20 +53,13 @@
 
 def block_starts(rows):
     me = lax.rem(lax.axis_index("tensor"), GROUP)
-    north = lax.rem(lax.axis_index("dp"), 2) == 1
-    own, other = [], []
-    for first, second in zip(SOUTH, NORTH):
-        own.append(pl.multiple_of((me ^ jnp.where(north, second, first)) * rows, rows))
-        other.append(pl.multiple_of((me ^ jnp.where(north, first, second)) * rows, rows))
-    return own, other
+    return [pl.multiple_of((me ^ partner) * rows, rows) for partner in PARTNERS]
 
 
 def gram_kernel(gradient_ref, *refs):
-    slots = len(SOUTH)
-    chunks, send, (mixed, cross) = refs[:slots], refs[slots], refs[slots + 1 :]
+    chunks, (mixed, cross) = refs[:GROUP], refs[GROUP:]
     half = mixed.shape[0]
     rows = half // GROUP
-    size = chunks[0].shape[0]
     high, low = split(gradient_ref[0])
     left = jnp.concatenate([high, high, low], axis=0)
     right = jnp.concatenate([high, low, high], axis=0)
@@ -90,27 +82,25 @@
                 at += rows
         out[at : at + SUBLANES, :] = tile
 
-    own, other = block_starts(rows)
-    for slot in range(slots):
-        write(send, slot * size, other[slot])
-    for slot in range(slots):
-        write(chunks[slot], 0, own[slot])
+    for out, start in zip(chunks, block_starts(rows)):
+        write(out, 0, start)
 
 
 def update_kernel(gain, *refs):
-    slots = len(SOUTH)
-    own_chunks, other_chunks = refs[:slots], refs[slots : 2 * slots]
-    gradient_ref, update_ref, whole_hbm, mixed, cross, store_sem = refs[2 * slots :]
+    gathered, passed = refs[:GROUP], refs[GROUP : 2 * GROUP]
+    gradient_ref, update_ref, whole_hbm, mixed, cross, store_sem = refs[2 * GROUP :]
     half = mixed.shape[0]
     rows = half // GROUP
-    own, other = block_starts(rows)
-    for source, start in zip((*own_chunks, *other_chunks), own + other):
+    length = passed[0].shape[0]
+    north = lax.rem(lax.axis_index("dp"), 2) == 1
+    for direct, relayed, start in zip(gathered, passed, block_starts(rows)):
+        block = jnp.where(north, direct[length:, :], relayed[...])
         at = 0
         for target in (cross, mixed):
             for lane in range(0, half, LANES):
-                target[pl.ds(start, rows), lane : lane + LANES] = source[at : at + rows, :]
+                target[pl.ds(start, rows), lane : lane + LANES] = block[at : at + rows, :]
                 at += rows
-    diagonal = jnp.concatenate([own_chunks[0][at + i : at + i + 1, :] for i in range(half // LANES)], axis=1)
+    diagonal = jnp.concatenate([block[at + i : at + i + 1, :] for i in range(half // LANES)], axis=1)
     row, column = grid_pair(half)
     packed = mixed[...]
     flipped = packed.T
@@ -155,7 +145,7 @@
     pairs, size = mesh.shape["dp"], mesh.shape["tensor"]
     assert pairs % 2 == 0 and size % GROUP == 0 and size & (size - 1) == 0
     _, features, outputs = gradient.shape
-    half, slots = outputs // 2, len(SOUTH)
+    half = outputs // 2
     assert half // LANES <= SUBLANES
     length = 2 * half // GROUP * (half // LANES) + SUBLANES
     chunk = jax.ShapeDtypeStruct((length, LANES), jnp.float32)
@@ -165,43 +155,34 @@
     def flip(value):
         return lax.ppermute(value, "dp", [(d, d ^ 1) for d in range(pairs)])
 
-    def far(value, step):
-        return lax.ppermute(value, "tensor", [(i, i ^ step) for i in range(size)])
-
-    def near(value, slot):
-        partner = (SOUTH[slot], NORTH[slot])
-        moves = [(d * size + i, d * size + (i ^ partner[d % 2])) for d in range(pairs) for i in range(size)]
+    def chips(value, partner):
+        moves = [(d * size + i, d * size + (i ^ partner if d % 2 else i)) for d in range(pairs) for i in range(size)]
         return lax.ppermute(value, ("dp", "tensor"), moves)
 
-    *own, send = pl.pallas_call(
+    chunks = pl.pallas_call(
         gram_kernel,
-        out_shape=[chunk] * slots + [jax.ShapeDtypeStruct((slots * length, LANES), jnp.float32)],
+        out_shape=[chunk] * GROUP,
         in_specs=[vmem],
-        out_specs=[vmem] * (slots + 1),
+        out_specs=[vmem] * GROUP,
         scratch_shapes=[pltpu.VMEM((half, half), jnp.float32)] * 2,
         compiler_params=pltpu.CompilerParams(vmem_limit_bytes=GRAM_VMEM),
         name="gram",
     )(gradient)
-    held = flip(send)
-    arrived = []
-    for slot in range(slots):
-        message = jnp.concatenate([own[slot], held[slot * length : (slot + 1) * length]])
-        arrived.append(near(message, slot))
-    partial = functools.reduce(jnp.add, arrived)
-    mine = partial[:length] + flip(partial[length:])
+    messages = [jnp.concatenate([flip(value), value]) for value in chunks]
+    both = functools.reduce(jnp.add, [chips(value, k) for value, k in zip(messages[1:], PARTNERS[1:])], messages[0])
     step = GROUP
     while step < size:
-        mine = mine + far(mine, step)
+        both = both + chips(both, step)
         step *= 2
-    both = jnp.concatenate([mine, flip(mine)])
-    gathered = [near(both, slot) for slot in range(slots)]
-    passed = [flip(value[length:]) for value in gathered]
+    gathered = [chips(both, partner) for partner in reversed(PARTNERS[1:])]
+    gathered = [both] + gathered[::-1]
+    passed = [flip(value[:length]) for value in gathered]
     gain = update_gain * math.sqrt(max(FEATURES, OUTPUTS))
     whole = jax.ShapeDtypeStruct((pairs, features, outputs), jnp.bfloat16)
     update, placed = pl.pallas_call(
         functools.partial(update_kernel, gain),
         out_shape=[jax.ShapeDtypeStruct(gradient.shape, jnp.bfloat16), whole],
-        in_specs=[vmem] * (2 * slots + 1),
+        in_specs=[vmem] * (2 * GROUP + 1),
         out_specs=[vmem, anywhere],
         scratch_shapes=[
             pltpu.VMEM((half, half), jnp.float32),

time: 52 us -> 81.3 us (1.56)
  starting transfers between devices: 24.9 us -> 62.4 us
  waiting for transfers between devices: 13.8 us -> 4.91 us
    ppermute x7 -> x16, starting transfers between devices: 11.4 us -> 52 us  [flip(): return lax.ppermute(value, 'dp', [(d, d ^ 1) for d in range(pairs)])]
    ppermute x9 -> x15, waiting for transfers between devices: 8.04 us -> 0.04 us  [chips(): return lax.ppermute(value, ('dp', 'tensor'), moves)]
    ppermute x9 -> x15, starting transfers between devices: 13.1 us -> 10.2 us  [chips(): return lax.ppermute(value, ('dp', 'tensor'), moves)]
    ppermute x7 -> x16, waiting for transfers between devices: 4.24 us -> 3.13 us  [flip(): return lax.ppermute(value, 'dp', [(d, d ^ 1) for d in range(pairs)])]
  transfers between devices with their start and end apart: 17 -> 32, of which waited for: 8 -> 8; matrix products, arithmetic and copies ran while one was open for 0% -> 0% of each run, Pallas kernels for 0% -> 0%
where the time goes in v1:
time: 81.3 us; the launch traced here: 80.8 us
  starting transfers between devices  62.4 us (77%)
  Pallas kernels  11.6 us (14%)
  waiting for transfers between devices  4.91 us (6%)
  local copies, waits for them, and re-layouts  1.28 us (2%)
    ppermute x16, starting transfers between devices, flip(): return lax.ppermute(value, 'dp', [(d, d ^ 1) for d in range(pairs)])  52 us
    ppermute x15, starting transfers between devices, chips(): return lax.ppermute(value, ('dp', 'tensor'), moves)  10.2 us
    pallas_call x1, Pallas kernels, on_device(): pl.pallas_call(functools.partial(update_kernel, gain), out_shape=[jax.Sha...  9.98 us
    ppermute x16, waiting for transfers between devices, flip(): return lax.ppermute(value, 'dp', [(d, d ^ 1) for d in range(pairs)])  3.13 us
    ppermute x1, waiting for transfers between devices, on_device(): other = lax.ppermute(update, 'dp', [(0, 1), (1, 0)])  1.74 us
  transfers between devices with their start and end apart: 32, of which 8 were waited for; matrix products, arithmetic and copies ran while one was open for 0% of the time, Pallas kernels for 0%

profile of v1, /device:TPU:0, one launch (start us, length us, event | category | flops | bytes accessed | tf_op | source)
XLA Modules:
  0.0 80.8 jit_solution(11167993057359422319)
XLA Ops:
  0.0 1.2 %copy-done = f32[1,512,512]{2,1,0:T(8,128)S(1)} copy-done((f32[1,512,512]{2,1,0:T(8,128)S(1)}, f32[1,512,512]{2,1,0:T(8,128)}, u32[]{:S(2)}) %copy-start) | copy-done | bytes 1048600
  1.2 0.9 %gram.1 = (f32[136,128]{1,0:T(8,128)S(1)}, f32[136,128]{1,0:T(8,128)S(1)}, f32[136,128]{1,0:T(8,128)S(1)}, f32[136,128]{1,0:T(8,128)S(1)}, f32[136,128]{1,0:T(8,...) custom-call(f32[1,512,512]{2,1,0:T(8,128)S(1)} %copy-done), custom_call_target="tpu_custom_call" | custom-call | tf_op jit(solution)/shard_map/gram/pallas_call | solution.py:162
  4.4 0.9 %collective-permute-done.13 = f32[136,128]{1,0:T(8,128)S(1)} collective-permute-done((f32[136,128]{1,0:T(8,128)S(1)}, f32[136,128]{1,0:T(8,128)S(1)}, u32[]{:S(2)}, u32[]{:S(2)}) %collective-permute-start.13) | collective-permute-done | bytes 69664 | tf_op jit(solution)/shard_map/ppermute | solution.py:156
  5.7 0.9 %collective-permute-done.11 = f32[136,128]{1,0:T(8,128)S(1)} collective-permute-done((f32[136,128]{1,0:T(8,128)S(1)}, f32[136,128]{1,0:T(8,128)S(1)}, u32[]{:S(2)}, u32[]{:S(2)}) %collective-permute-start.11) | collective-permute-done | bytes 69664 | tf_op jit(solution)/shard_map/ppermute | solution.py:156
  6.6 0.7 collective-permute-start.14
  7.3 0.7 collective-permute-start.12
  8.0 0.7 collective-permute-start.10
  8.7 0.7 collective-permute-start.8
  9.4 0.7 collective-permute-start.6
  10.1 0.7 collective-permute-start.4
  10.8 0.7 collective-permute-start.2
  11.6 0.8 collective-permute-start.15
  12.5 0.7 collective-permute-start.22
  13.1 0.7 collective-permute-start.21
  13.8 0.7 collective-permute-start.20
  14.5 0.7 collective-permute-start.19
  15.2 0.7 collective-permute-start.18
  15.8 0.7 collective-permute-start.17
  16.5 0.7 collective-permute-start.16
  17.3 46.6 %collective-permute-start.23 = (f32[136,128]{1,0:T(8,128)S(1)}, f32[136,128]{1,0:T(8,128)S(1)}, u32[]{:S(2)}, u32[]{:S(2)}) collective-permute-start(f32[136,128]{1,0:T(8,128)S(1)} %slice.32), channel_id=1, source_target_pairs={{0,16},{16,0},{1,17},{17,1},{2,18},{18,2},{3,19},{19,3},{4,20},{20... | collective-permute-start | bytes 208904 | tf_op jit(solution)/shard_map/ppermute | solution.py:156
  64.6 1.6 %collective-permute-start.27 = (f32[136,128]{1,0:T(8,128)S(1)}, f32[136,128]{1,0:T(8,128)S(1)}, u32[]{:S(2)}, u32[]{:S(2)}) collective-permute-start(f32[136,128]{1,0:T(8,128)S(1)} %slice.36), channel_id=1, source_target_pairs={{0,16},{16,0},{1,17},{17,1},{2,18},{18,2},{3,19},{19,3},{4,20},{20... | collective-permute-start | bytes 208904 | tf_op jit(solution)/shard_map/ppermute | solution.py:156
  68.0 10.0 %update.1 = (bf16[1,512,512]{2,1,0:T(8,128)(2,1)S(1)}, bf16[2,512,512]{2,1,0:T(8,128)(2,1)}) custom-call(f32[272,128]{1,0:T(8,128)S(1)} %add.31.refs_0_, f32[272,128]{1,0:T(8,128)S(1)} %collective-permute-done.16.refs_1_, f32[272,128]{1,0:T(8,128)S(1)} %collective-permute-done.17.refs_2_, f32[272,128]{1,0:T(8,128)S(1)} %collective-permute-done.18.refs_3_, ...), custom_call_target="tpu_custom_call" | custom-call | tf_op jit(solution)/shard_map/update/pallas_call | solution.py:182
  78.3 1.7 %collective-permute-done.31.other_ref = bf16[1,512,512]{2,1,0:T(8,128)(2,1)S(1)} collective-permute-done((bf16[1,512,512]{2,1,0:T(8,128)(2,1)S(1)}, bf16[1,512,512]{2,1,0:T(8,128)(2,1)S(1)}, u32[]{:S(2)}, u32[]{:S(2)}) %collective-permute-start.31) | collective-permute-done | bytes 524320 | tf_op jit(solution)/shard_map/ppermute | solution.py:197
  80.0 0.8 place.1
  (64 shorter events, 5.7 us)
Async XLA Ops:
  2.1 1.6 %collective-permute-start.1 = (f32[136,128]{1,0:T(8,128)S(1)}, f32[136,128]{1,0:T(8,128)S(1)}, u32[]{:S(2)}, u32[]{:S(2)}) collective-permute-start(f32[136,128]{1,0:T(8,128)S(1)} %get-tuple-element.16), channel_id=1, source_target_pairs={{0,16},{16,0},{1,17},{17,1},{2,18},{18,2},{3,19},{19,3},{4,20},{20... | collective-permute-start | bytes 208904 | tf_op jit(solution)/shard_map/ppermute | solution.py:156
  2.6 6.8 %collective-permute-start = (f32[136,128]{1,0:T(8,128)S(1)}, f32[136,128]{1,0:T(8,128)S(1)}, u32[]{:S(2)}, u32[]{:S(2)}) collective-permute-start(f32[136,128]{1,0:T(8,128)S(1)} %get-tuple-element.15), channel_id=1, source_target_pairs={{0,16},{16,0},{1,17},{17,1},{2,18},{18,2},{3,19},{19,3},{4,20},{20... | collective-permute-start | bytes 208904 | tf_op jit(solution)/shard_map/ppermute | solution.py:156
  3.2 5.5 %collective-permute-start.5 = (f32[136,128]{1,0:T(8,128)S(1)}, f32[136,128]{1,0:T(8,128)S(1)}, u32[]{:S(2)}, u32[]{:S(2)}) collective-permute-start(f32[136,128]{1,0:T(8,128)S(1)} %get-tuple-element.18), channel_id=1, source_target_pairs={{0,16},{16,0},{1,17},{17,1},{2,18},{18,2},{3,19},{19,3},{4,20},{20... | collective-permute-start | bytes 208904 | tf_op jit(solution)/shard_map/ppermute | solution.py:156
  3.2 4.7 %collective-permute-start.7 = (f32[136,128]{1,0:T(8,128)S(1)}, f32[136,128]{1,0:T(8,128)S(1)}, u32[]{:S(2)}, u32[]{:S(2)}) collective-permute-start(f32[136,128]{1,0:T(8,128)S(1)} %get-tuple-element.19), channel_id=1, source_target_pairs={{0,16},{16,0},{1,17},{17,1},{2,18},{18,2},{3,19},{19,3},{4,20},{20... | collective-permute-start | bytes 208904 | tf_op jit(solution)/shard_map/ppermute | solution.py:156
  3.7 3.6 %collective-permute-start.9 = (f32[136,128]{1,0:T(8,128)S(1)}, f32[136,128]{1,0:T(8,128)S(1)}, u32[]{:S(2)}, u32[]{:S(2)}) collective-permute-start(f32[136,128]{1,0:T(8,128)S(1)} %get-tuple-element.20), channel_id=1, source_target_pairs={{0,16},{16,0},{1,17},{17,1},{2,18},{18,2},{3,19},{19,3},{4,20},{20... | collective-permute-start | bytes 208904 | tf_op jit(solution)/shard_map/ppermute | solution.py:156
  6.6 3.5 %collective-permute-start.14 = (f32[272,128]{1,0:T(8,128)S(1)}, f32[272,128]{1,0:T(8,128)S(1)}, u32[]{:S(2)}, u32[]{:S(2)}) collective-permute-start(f32[272,128]{1,0:T(8,128)S(1)} %pad_maximum_fusion.6), channel_id=1, source_target_pairs={{0,0},{1,1},{2,2},{3,3},{4,4},{5,5},{6,6},{7,7},{8,8},{9,9},{10,10... | collective-permute-start | bytes 417800 | tf_op jit(solution)/shard_map/ppermute | solution.py:160
  7.3 3.5 %collective-permute-start.12 = (f32[272,128]{1,0:T(8,128)S(1)}, f32[272,128]{1,0:T(8,128)S(1)}, u32[]{:S(2)}, u32[]{:S(2)}) collective-permute-start(f32[272,128]{1,0:T(8,128)S(1)} %pad_maximum_fusion.5), channel_id=1, source_target_pairs={{0,0},{1,1},{2,2},{3,3},{4,4},{5,5},{6,6},{7,7},{8,8},{9,9},{10,10... | collective-permute-start | bytes 417800 | tf_op jit(solution)/shard_map/ppermute | solution.py:160
  8.0 3.5 %collective-permute-start.10 = (f32[272,128]{1,0:T(8,128)S(1)}, f32[272,128]{1,0:T(8,128)S(1)}, u32[]{:S(2)}, u32[]{:S(2)}) collective-permute-start(f32[272,128]{1,0:T(8,128)S(1)} %pad_maximum_fusion.4), channel_id=1, source_target_pairs={{0,0},{1,1},{2,2},{3,3},{4,4},{5,5},{6,6},{7,7},{8,8},{9,9},{10,10... | collective-permute-start | bytes 417800 | tf_op jit(solution)/shard_map/ppermute | solution.py:160
  8.7 2.8 %collective-permute-start.8 = (f32[272,128]{1,0:T(8,128)S(1)}, f32[272,128]{1,0:T(8,128)S(1)}, u32[]{:S(2)}, u32[]{:S(2)}) collective-permute-start(f32[272,128]{1,0:T(8,128)S(1)} %pad_maximum_fusion.3), channel_id=1, source_target_pairs={{0,0},{1,1},{2,2},{3,3},{4,4},{5,5},{6,6},{7,7},{8,8},{9,9},{10,10... | collective-permute-start | bytes 417800 | tf_op jit(solution)/shard_map/ppermute | solution.py:160
  9.4 2.1 %collective-permute-start.6 = (f32[272,128]{1,0:T(8,128)S(1)}, f32[272,128]{1,0:T(8,128)S(1)}, u32[]{:S(2)}, u32[]{:S(2)}) collective-permute-start(f32[272,128]{1,0:T(8,128)S(1)} %pad_maximum_fusion.2), channel_id=1, source_target_pairs={{0,0},{1,1},{2,2},{3,3},{4,4},{5,5},{6,6},{7,7},{8,8},{9,9},{10,10... | collective-permute-start | bytes 417800 | tf_op jit(solution)/shard_map/ppermute | solution.py:160
  10.1 1.4 %collective-permute-start.4 = (f32[272,128]{1,0:T(8,128)S(1)}, f32[272,128]{1,0:T(8,128)S(1)}, u32[]{:S(2)}, u32[]{:S(2)}) collective-permute-start(f32[272,128]{1,0:T(8,128)S(1)} %pad_maximum_fusion.1), channel_id=1, source_target_pairs={{0,0},{1,1},{2,2},{3,3},{4,4},{5,5},{6,6},{7,7},{8,8},{9,9},{10,10... | collective-permute-start | bytes 417800 | tf_op jit(solution)/shard_map/ppermute | solution.py:160
  12.5 3.4 %collective-permute-start.22 = (f32[272,128]{1,0:T(8,128)S(1)}, f32[272,128]{1,0:T(8,128)S(1)}, u32[]{:S(2)}, u32[]{:S(2)}) collective-permute-start(f32[272,128]{1,0:T(8,128)S(1)} %add.31.refs_0_), channel_id=1, source_target_pairs={{0,0},{1,1},{2,2},{3,3},{4,4},{5,5},{6,6},{7,7},{8,8},{9,9},{10,10... | collective-permute-start | bytes 417800 | tf_op jit(solution)/shard_map/ppermute | solution.py:160
  13.1 3.4 %collective-permute-start.21 = (f32[272,128]{1,0:T(8,128)S(1)}, f32[272,128]{1,0:T(8,128)S(1)}, u32[]{:S(2)}, u32[]{:S(2)}) collective-permute-start(f32[272,128]{1,0:T(8,128)S(1)} %add.31.refs_0_), channel_id=1, source_target_pairs={{0,0},{1,1},{2,2},{3,3},{4,4},{5,5},{6,6},{7,7},{8,8},{9,9},{10,10... | collective-permute-start | bytes 417800 | tf_op jit(solution)/shard_map/ppermute | solution.py:160
  13.8 3.5 %collective-permute-start.20 = (f32[272,128]{1,0:T(8,128)S(1)}, f32[272,128]{1,0:T(8,128)S(1)}, u32[]{:S(2)}, u32[]{:S(2)}) collective-permute-start(f32[272,128]{1,0:T(8,128)S(1)} %add.31.refs_0_), channel_id=1, source_target_pairs={{0,0},{1,1},{2,2},{3,3},{4,4},{5,5},{6,6},{7,7},{8,8},{9,9},{10,10... | collective-permute-start | bytes 417800 | tf_op jit(solution)/shard_map/ppermute | solution.py:160
  14.5 49.4 %collective-permute-start.19 = (f32[272,128]{1,0:T(8,128)S(1)}, f32[272,128]{1,0:T(8,128)S(1)}, u32[]{:S(2)}, u32[]{:S(2)}) collective-permute-start(f32[272,128]{1,0:T(8,128)S(1)} %add.31.refs_0_), channel_id=1, source_target_pairs={{0,0},{1,1},{2,2},{3,3},{4,4},{5,5},{6,6},{7,7},{8,8},{9,9},{10,10... | collective-permute-start | bytes 417800 | tf_op jit(solution)/shard_map/ppermute | solution.py:160
  15.2 48.8 %collective-permute-start.18 = (f32[272,128]{1,0:T(8,128)S(1)}, f32[272,128]{1,0:T(8,128)S(1)}, u32[]{:S(2)}, u32[]{:S(2)}) collective-permute-start(f32[272,128]{1,0:T(8,128)S(1)} %add.31.refs_0_), channel_id=1, source_target_pairs={{0,0},{1,1},{2,2},{3,3},{4,4},{5,5},{6,6},{7,7},{8,8},{9,9},{10,10... | collective-permute-start | bytes 417800 | tf_op jit(solution)/shard_map/ppermute | solution.py:160
  15.8 48.6 %collective-permute-start.17 = (f32[272,128]{1,0:T(8,128)S(1)}, f32[272,128]{1,0:T(8,128)S(1)}, u32[]{:S(2)}, u32[]{:S(2)}) collective-permute-start(f32[272,128]{1,0:T(8,128)S(1)} %add.31.refs_0_), channel_id=1, source_target_pairs={{0,0},{1,1},{2,2},{3,3},{4,4},{5,5},{6,6},{7,7},{8,8},{9,9},{10,10... | collective-permute-start | bytes 417800 | tf_op jit(solution)/shard_map/ppermute | solution.py:160
  16.5 48.0 %collective-permute-start.16 = (f32[272,128]{1,0:T(8,128)S(1)}, f32[272,128]{1,0:T(8,128)S(1)}, u32[]{:S(2)}, u32[]{:S(2)}) collective-permute-start(f32[272,128]{1,0:T(8,128)S(1)} %add.31.refs_0_), channel_id=1, source_target_pairs={{0,0},{1,1},{2,2},{3,3},{4,4},{5,5},{6,6},{7,7},{8,8},{9,9},{10,10... | collective-permute-start | bytes 417800 | tf_op jit(solution)/shard_map/ppermute | solution.py:160
  17.3 48.9 %collective-permute-start.23 = (f32[136,128]{1,0:T(8,128)S(1)}, f32[136,128]{1,0:T(8,128)S(1)}, u32[]{:S(2)}, u32[]{:S(2)}) collective-permute-start(f32[136,128]{1,0:T(8,128)S(1)} %slice.32), channel_id=1, source_target_pairs={{0,16},{16,0},{1,17},{17,1},{2,18},{18,2},{3,19},{19,3},{4,20},{20... | collective-permute-start | bytes 208904 | tf_op jit(solution)/shard_map/ppermute | solution.py:156
  63.9 2.4 %collective-permute-start.30 = (f32[136,128]{1,0:T(8,128)S(1)}, f32[136,128]{1,0:T(8,128)S(1)}, u32[]{:S(2)}, u32[]{:S(2)}) collective-permute-start(f32[136,128]{1,0:T(8,128)S(1)} %slice.39), channel_id=1, source_target_pairs={{0,16},{16,0},{1,17},{17,1},{2,18},{18,2},{3,19},{19,3},{4,20},{20... | collective-permute-start | bytes 208904 | tf_op jit(solution)/shard_map/ppermute | solution.py:156
  64.0 2.8 %collective-permute-start.29 = (f32[136,128]{1,0:T(8,128)S(1)}, f32[136,128]{1,0:T(8,128)S(1)}, u32[]{:S(2)}, u32[]{:S(2)}) collective-permute-start(f32[136,128]{1,0:T(8,128)S(1)} %slice.38), channel_id=1, source_target_pairs={{0,16},{16,0},{1,17},{17,1},{2,18},{18,2},{3,19},{19,3},{4,20},{20... | collective-permute-start | bytes 208904 | tf_op jit(solution)/shard_map/ppermute | solution.py:156
  64.4 2.4 %collective-permute-start.28 = (f32[136,128]{1,0:T(8,128)S(1)}, f32[136,128]{1,0:T(8,128)S(1)}, u32[]{:S(2)}, u32[]{:S(2)}) collective-permute-start(f32[136,128]{1,0:T(8,128)S(1)} %slice.37), channel_id=1, source_target_pairs={{0,16},{16,0},{1,17},{17,1},{2,18},{18,2},{3,19},{19,3},{4,20},{20... | collective-permute-start | bytes 208904 | tf_op jit(solution)/shard_map/ppermute | solution.py:156
  64.6 2.5 %collective-permute-start.27 = (f32[136,128]{1,0:T(8,128)S(1)}, f32[136,128]{1,0:T(8,128)S(1)}, u32[]{:S(2)}, u32[]{:S(2)}) collective-permute-start(f32[136,128]{1,0:T(8,128)S(1)} %slice.36), channel_id=1, source_target_pairs={{0,16},{16,0},{1,17},{17,1},{2,18},{18,2},{3,19},{19,3},{4,20},{20... | collective-permute-start | bytes 208904 | tf_op jit(solution)/shard_map/ppermute | solution.py:156
  78.0 2.0 %collective-permute-start.31 = (bf16[1,512,512]{2,1,0:T(8,128)(2,1)S(1)}, bf16[1,512,512]{2,1,0:T(8,128)(2,1)S(1)}, u32[]{:S(2)}, u32[]{:S(2)}) collective-permute-start(bf16[1,512,512]{2,1,0:T(8,128)(2,1)S(1)} %get-tuple-element.23), channel_id=1, source_target_pairs={{0,16},{16,0},{1,17},{17,1},{2,18},{18,2},{3,19},{19,3},{4,20},{20... | collective-permute-start | bytes 1572872 | tf_op jit(solution)/shard_map/ppermute | solution.py:197
  (10 other events, 67.0 us)

commit v2 on v1

--- a/solution.py
+++ b/solution.py
@@ -26,7 +26,7 @@
 
 
 GROUP = 8
-PARTNERS = (0, 7, 6, 5, 3, 4, 1, 2)
+PARTNERS = (7, 3, 5, 6, 1, 2, 4, 0)
 
 
 def split(value):
@@ -87,20 +87,17 @@
 
 
 def update_kernel(gain, *refs):
-    gathered, passed = refs[:GROUP], refs[GROUP : 2 * GROUP]
-    gradient_ref, update_ref, whole_hbm, mixed, cross, store_sem = refs[2 * GROUP :]
+    chunks = refs[:GROUP]
+    gradient_ref, update_ref, whole_hbm, mixed, cross, store_sem = refs[GROUP:]
     half = mixed.shape[0]
     rows = half // GROUP
-    length = passed[0].shape[0]
-    north = lax.rem(lax.axis_index("dp"), 2) == 1
-    for direct, relayed, start in zip(gathered, passed, block_starts(rows)):
-        block = jnp.where(north, direct[length:, :], relayed[...])
+    for source, start in zip(chunks, block_starts(rows)):
         at = 0
         for target in (cross, mixed):
             for lane in range(0, half, LANES):
-                target[pl.ds(start, rows), lane : lane + LANES] = block[at : at + rows, :]
+                target[pl.ds(start, rows), lane : lane + LANES] = source[at : at + rows, :]
                 at += rows
-    diagonal = jnp.concatenate([block[at + i : at + i + 1, :] for i in range(half // LANES)], axis=1)
+    diagonal = jnp.concatenate([chunks[0][at + i : at + i + 1, :] for i in range(half // LANES)], axis=1)
     row, column = grid_pair(half)
     packed = mixed[...]
     flipped = packed.T
@@ -152,12 +149,12 @@
     vmem = pl.BlockSpec(memory_space=pltpu.VMEM)
     anywhere = pl.BlockSpec(memory_space=pl.ANY)
 
-    def flip(value):
-        return lax.ppermute(value, "dp", [(d, d ^ 1) for d in range(pairs)])
-
-    def chips(value, partner):
-        moves = [(d * size + i, d * size + (i ^ partner if d % 2 else i)) for d in range(pairs) for i in range(size)]
+    def across(value, partner):
+        moves = [(d * size + i, (d ^ 1) * size + (i ^ partner)) for d in range(pairs) for i in range(size)]
         return lax.ppermute(value, ("dp", "tensor"), moves)
+
+    def far(value, step):
+        return lax.ppermute(value, "tensor", [(i, i ^ step) for i in range(size)])
 
     chunks = pl.pallas_call(
         gram_kernel,
@@ -168,21 +165,18 @@
         compiler_params=pltpu.CompilerParams(vmem_limit_bytes=GRAM_VMEM),
         name="gram",
     )(gradient)
-    messages = [jnp.concatenate([flip(value), value]) for value in chunks]
-    both = functools.reduce(jnp.add, [chips(value, k) for value, k in zip(messages[1:], PARTNERS[1:])], messages[0])
+    owned = functools.reduce(jnp.add, [across(value, partner) for value, partner in zip(chunks, PARTNERS)])
     step = GROUP
     while step < size:
-        both = both + chips(both, step)
+        owned = owned + far(owned, step)
         step *= 2
-    gathered = [chips(both, partner) for partner in reversed(PARTNERS[1:])]
-    gathered = [both] + gathered[::-1]
-    passed = [flip(value[:length]) for value in gathered]
+    gathered = [across(owned, partner) for partner in reversed(PARTNERS)][::-1]
     gain = update_gain * math.sqrt(max(FEATURES, OUTPUTS))
     whole = jax.ShapeDtypeStruct((pairs, features, outputs), jnp.bfloat16)
     update, placed = pl.pallas_call(
         functools.partial(update_kernel, gain),
         out_shape=[jax.ShapeDtypeStruct(gradient.shape, jnp.bfloat16), whole],
-        in_specs=[vmem] * (2 * GROUP + 1),
+        in_specs=[vmem] * (GROUP + 1),
         out_specs=[vmem, anywhere],
         scratch_shapes=[
             pltpu.VMEM((half, half), jnp.float32),
@@ -191,7 +185,7 @@
         ],
         compiler_params=pltpu.CompilerParams(vmem_limit_bytes=UPDATE_VMEM),
         name="update",
-    )(*gathered, *passed, gradient)
+    )(*gathered, gradient)
     if pairs != 2:
         return lax.all_gather(update, "dp", axis=0, tiled=True)
     other = lax.ppermute(update, "dp", [(0, 1), (1, 0)])

time: 81.3 us -> 49.8 us (0.61)
  starting transfers between devices: 62.4 us -> 23.8 us
  waiting for transfers between devices: 4.91 us -> 12.9 us
    ppermute x31 -> x17, starting transfers between devices: 62.2 us -> 23.6 us  [the longest x16 20.9 us: across(): return lax.ppermute(value, ('dp', 'tensor'), moves)]
    ppermute x31 -> x17, waiting for transfers between devices: 3.17 us -> 11.1 us  [the longest x16 7.04 us: across(): return lax.ppermute(value, ('dp', 'tensor'), moves)]
  transfers between devices with their start and end apart: 32 -> 18, of which waited for: 8 -> 9; matrix products, arithmetic and copies ran while one was open for 0% -> 0% of each run, Pallas kernels for 0% -> 0%
where the time goes in v2:
time: 49.8 us; the launch traced here: 49.7 us
  starting transfers between devices  23.8 us (48%)
  waiting for transfers between devices  12.9 us (26%)
  Pallas kernels  11.6 us (23%)
  local copies, waits for them, and re-layouts  1.23 us (2%)
    ppermute x16, starting transfers between devices, across(): return lax.ppermute(value, ('dp', 'tensor'), moves)  20.9 us
    pallas_call x1, Pallas kernels, on_device(): pl.pallas_call(functools.partial(update_kernel, gain), out_shape=[jax.Sha...  9.97 us
    ppermute x16, waiting for transfers between devices, across(): return lax.ppermute(value, ('dp', 'tensor'), moves)  7.04 us
    ppermute x1, waiting for transfers between devices, far(): return lax.ppermute(value, 'tensor', [(i, i ^ step) for i in range(size)])  4.1 us
    ppermute x1, starting transfers between devices, far(): return lax.ppermute(value, 'tensor', [(i, i ^ step) for i in range(size)])  2.67 us
    ppermute x1, waiting for transfers between devices, on_device(): other = lax.ppermute(update, 'dp', [(0, 1), (1, 0)])  1.74 us
    unnamed x4, local copies, waits for them, and re-layouts  1.23 us
  transfers between devices with their start and end apart: 18, of which 9 were waited for; matrix products, arithmetic and copies ran while one was open for 0% of the time, Pallas kernels for 0%

profile of v2, /device:TPU:0, one launch (start us, length us, event | category | flops | bytes accessed | tf_op | source)
XLA Modules:
  0.0 49.7 jit_solution(8718684896194548024)
XLA Ops:
  0.0 1.2 %copy-done = f32[1,512,512]{2,1,0:T(8,128)S(1)} copy-done((f32[1,512,512]{2,1,0:T(8,128)S(1)}, f32[1,512,512]{2,1,0:T(8,128)}, u32[]{:S(2)}) %copy-start) | copy-done | bytes 1048600
  1.2 0.9 %gram.1 = (f32[136,128]{1,0:T(8,128)S(1)}, f32[136,128]{1,0:T(8,128)S(1)}, f32[136,128]{1,0:T(8,128)S(1)}, f32[136,128]{1,0:T(8,128)S(1)}, f32[136,128]{1,0:T(8,...) custom-call(f32[1,512,512]{2,1,0:T(8,128)S(1)} %copy-done), custom_call_target="tpu_custom_call" | custom-call | tf_op jit(solution)/shard_map/gram/pallas_call | solution.py:159
  2.1 4.4 %collective-permute-start = (f32[136,128]{1,0:T(8,128)S(1)}, f32[136,128]{1,0:T(8,128)S(1)}, u32[]{:S(2)}, u32[]{:S(2)}) collective-permute-start(f32[136,128]{1,0:T(8,128)S(1)} %get-tuple-element.15), channel_id=1, source_target_pairs={{0,23},{1,22},{2,21},{3,20},{4,19},{5,18},{6,17},{7,16},{8,31},{9,... | collective-permute-start | bytes 208904 | tf_op jit(solution)/shard_map/ppermute | solution.py:154
  6.5 0.8 %collective-permute-start.1 = (f32[136,128]{1,0:T(8,128)S(1)}, f32[136,128]{1,0:T(8,128)S(1)}, u32[]{:S(2)}, u32[]{:S(2)}) collective-permute-start(f32[136,128]{1,0:T(8,128)S(1)} %get-tuple-element.16), channel_id=1, source_target_pairs={{0,19},{1,18},{2,17},{3,16},{4,23},{5,22},{6,21},{7,20},{8,27},{9,... | collective-permute-start | bytes 208904 | tf_op jit(solution)/shard_map/ppermute | solution.py:154
  7.3 0.8 %collective-permute-start.2 = (f32[136,128]{1,0:T(8,128)S(1)}, f32[136,128]{1,0:T(8,128)S(1)}, u32[]{:S(2)}, u32[]{:S(2)}) collective-permute-start(f32[136,128]{1,0:T(8,128)S(1)} %get-tuple-element.17), channel_id=1, source_target_pairs={{0,21},{1,20},{2,23},{3,22},{4,17},{5,16},{6,19},{7,18},{8,29},{9,... | collective-permute-start | bytes 208904 | tf_op jit(solution)/shard_map/ppermute | solution.py:154
  8.1 2.8 %collective-permute-start.3 = (f32[136,128]{1,0:T(8,128)S(1)}, f32[136,128]{1,0:T(8,128)S(1)}, u32[]{:S(2)}, u32[]{:S(2)}) collective-permute-start(f32[136,128]{1,0:T(8,128)S(1)} %get-tuple-element.18), channel_id=1, source_target_pairs={{0,22},{1,23},{2,20},{3,21},{4,18},{5,19},{6,16},{7,17},{8,30},{9,... | collective-permute-start | bytes 208904 | tf_op jit(solution)/shard_map/ppermute | solution.py:154
  10.9 0.8 %collective-permute-start.5 = (f32[136,128]{1,0:T(8,128)S(1)}, f32[136,128]{1,0:T(8,128)S(1)}, u32[]{:S(2)}, u32[]{:S(2)}) collective-permute-start(f32[136,128]{1,0:T(8,128)S(1)} %get-tuple-element.20), channel_id=1, source_target_pairs={{0,18},{1,19},{2,16},{3,17},{4,22},{5,23},{6,20},{7,21},{8,26},{9,... | collective-permute-start | bytes 208904 | tf_op jit(solution)/shard_map/ppermute | solution.py:154
  11.7 2.7 %collective-permute-start.6 = (f32[136,128]{1,0:T(8,128)S(1)}, f32[136,128]{1,0:T(8,128)S(1)}, u32[]{:S(2)}, u32[]{:S(2)}) collective-permute-start(f32[136,128]{1,0:T(8,128)S(1)} %get-tuple-element.21), channel_id=1, source_target_pairs={{0,20},{1,21},{2,22},{3,23},{4,16},{5,17},{6,18},{7,19},{8,28},{9,... | collective-permute-start | bytes 208904 | tf_op jit(solution)/shard_map/ppermute | solution.py:154
  14.4 0.9 %collective-permute-done.3 = f32[136,128]{1,0:T(8,128)S(1)} collective-permute-done((f32[136,128]{1,0:T(8,128)S(1)}, f32[136,128]{1,0:T(8,128)S(1)}, u32[]{:S(2)}, u32[]{:S(2)}) %collective-permute-start.3) | collective-permute-done | bytes 69664 | tf_op jit(solution)/shard_map/ppermute | solution.py:154
  15.4 1.2 %collective-permute-done.5 = f32[136,128]{1,0:T(8,128)S(1)} collective-permute-done((f32[136,128]{1,0:T(8,128)S(1)}, f32[136,128]{1,0:T(8,128)S(1)}, u32[]{:S(2)}, u32[]{:S(2)}) %collective-permute-start.5) | collective-permute-done | bytes 69664 | tf_op jit(solution)/shard_map/ppermute | solution.py:154
  17.0 2.7 %collective-permute-start.8 = (f32[136,128]{1,0:T(8,128)S(1)}, f32[136,128]{1,0:T(8,128)S(1)}, u32[]{:S(2)}, u32[]{:S(2)}) collective-permute-start(f32[136,128]{1,0:T(8,128)S(1)} %add_add_fusion), channel_id=1, source_target_pairs={{0,8},{1,9},{2,10},{3,11},{4,12},{5,13},{6,14},{7,15},{8,0},{9,1},... | collective-permute-start | bytes 208904 | tf_op jit(solution)/shard_map/ppermute | solution.py:157
  19.7 4.1 %collective-permute-done.8 = f32[136,128]{1,0:T(8,128)S(1)} collective-permute-done((f32[136,128]{1,0:T(8,128)S(1)}, f32[136,128]{1,0:T(8,128)S(1)}, u32[]{:S(2)}, u32[]{:S(2)}) %collective-permute-start.8) | collective-permute-done | bytes 69664 | tf_op jit(solution)/shard_map/ppermute | solution.py:157
  23.9 0.6 %collective-permute-start.15 = (f32[136,128]{1,0:T(8,128)S(1)}, f32[136,128]{1,0:T(8,128)S(1)}, u32[]{:S(2)}, u32[]{:S(2)}) collective-permute-start(f32[136,128]{1,0:T(8,128)S(1)} %add.31), channel_id=1, source_target_pairs={{0,20},{1,21},{2,22},{3,23},{4,16},{5,17},{6,18},{7,19},{8,28},{9,... | collective-permute-start | bytes 208904 | tf_op jit(solution)/shard_map/ppermute | solution.py:154
  24.5 1.3 %collective-permute-start.14 = (f32[136,128]{1,0:T(8,128)S(1)}, f32[136,128]{1,0:T(8,128)S(1)}, u32[]{:S(2)}, u32[]{:S(2)}) collective-permute-start(f32[136,128]{1,0:T(8,128)S(1)} %add.31), channel_id=1, source_target_pairs={{0,18},{1,19},{2,16},{3,17},{4,22},{5,23},{6,20},{7,21},{8,26},{9,... | collective-permute-start | bytes 208904 | tf_op jit(solution)/shard_map/ppermute | solution.py:154
  25.8 1.1 %collective-permute-start.13 = (f32[136,128]{1,0:T(8,128)S(1)}, f32[136,128]{1,0:T(8,128)S(1)}, u32[]{:S(2)}, u32[]{:S(2)}) collective-permute-start(f32[136,128]{1,0:T(8,128)S(1)} %add.31), channel_id=1, source_target_pairs={{0,17},{1,16},{2,19},{3,18},{4,21},{5,20},{6,23},{7,22},{8,25},{9,... | collective-permute-start | bytes 208904 | tf_op jit(solution)/shard_map/ppermute | solution.py:154
  26.9 1.4 %collective-permute-start.12 = (f32[136,128]{1,0:T(8,128)S(1)}, f32[136,128]{1,0:T(8,128)S(1)}, u32[]{:S(2)}, u32[]{:S(2)}) collective-permute-start(f32[136,128]{1,0:T(8,128)S(1)} %add.31), channel_id=1, source_target_pairs={{0,22},{1,23},{2,20},{3,21},{4,18},{5,19},{6,16},{7,17},{8,30},{9,... | collective-permute-start | bytes 208904 | tf_op jit(solution)/shard_map/ppermute | solution.py:154
  28.9 2.1 %collective-permute-start.10 = (f32[136,128]{1,0:T(8,128)S(1)}, f32[136,128]{1,0:T(8,128)S(1)}, u32[]{:S(2)}, u32[]{:S(2)}) collective-permute-start(f32[136,128]{1,0:T(8,128)S(1)} %add.31), channel_id=1, source_target_pairs={{0,19},{1,18},{2,17},{3,16},{4,23},{5,22},{6,21},{7,20},{8,27},{9,... | collective-permute-start | bytes 208904 | tf_op jit(solution)/shard_map/ppermute | solution.py:154
  30.9 1.5 %collective-permute-start.9 = (f32[136,128]{1,0:T(8,128)S(1)}, f32[136,128]{1,0:T(8,128)S(1)}, u32[]{:S(2)}, u32[]{:S(2)}) collective-permute-start(f32[136,128]{1,0:T(8,128)S(1)} %add.31), channel_id=1, source_target_pairs={{0,23},{1,22},{2,21},{3,20},{4,19},{5,18},{6,17},{7,16},{8,31},{9,... | collective-permute-start | bytes 208904 | tf_op jit(solution)/shard_map/ppermute | solution.py:154
  32.5 0.9 %collective-permute-done.11.refs_2_ = f32[136,128]{1,0:T(8,128)S(1)} collective-permute-done((f32[136,128]{1,0:T(8,128)S(1)}, f32[136,128]{1,0:T(8,128)S(1)}, u32[]{:S(2)}, u32[]{:S(2)}) %collective-permute-start.11) | collective-permute-done | bytes 69664 | tf_op jit(solution)/shard_map/ppermute | solution.py:154
  33.3 2.1 %collective-permute-done.10.refs_1_ = f32[136,128]{1,0:T(8,128)S(1)} collective-permute-done((f32[136,128]{1,0:T(8,128)S(1)}, f32[136,128]{1,0:T(8,128)S(1)}, u32[]{:S(2)}, u32[]{:S(2)}) %collective-permute-start.10) | collective-permute-done | bytes 69664 | tf_op jit(solution)/shard_map/ppermute | solution.py:154
  35.5 1.4 %collective-permute-done.9.refs_0_ = f32[136,128]{1,0:T(8,128)S(1)} collective-permute-done((f32[136,128]{1,0:T(8,128)S(1)}, f32[136,128]{1,0:T(8,128)S(1)}, u32[]{:S(2)}, u32[]{:S(2)}) %collective-permute-start.9) | collective-permute-done | bytes 69664 | tf_op jit(solution)/shard_map/ppermute | solution.py:154
  36.9 10.0 %update.1 = (bf16[1,512,512]{2,1,0:T(8,128)(2,1)S(1)}, bf16[2,512,512]{2,1,0:T(8,128)(2,1)}) custom-call(f32[136,128]{1,0:T(8,128)S(1)} %collective-permute-done.9.refs_0_, f32[136,128]{1,0:T(8,128)S(1)} %collective-permute-done.10.refs_1_, f32[136,128]{1,0:T(8,128)S(1)} %collective-permute-done.11.refs_2_, f32[136,128]{1,0:T(8,128)S(1)} %collective-permute-done.12.refs_3_, ...), custom_call_target="tpu_custom_call" | custom-call | tf_op jit(solution)/shard_map/update/pallas_call | solution.py:176
  47.1 1.7 %collective-permute-done.17.other_ref = bf16[1,512,512]{2,1,0:T(8,128)(2,1)S(1)} collective-permute-done((bf16[1,512,512]{2,1,0:T(8,128)(2,1)S(1)}, bf16[1,512,512]{2,1,0:T(8,128)(2,1)S(1)}, u32[]{:S(2)}, u32[]{:S(2)}) %collective-permute-start.17) | collective-permute-done | bytes 524320 | tf_op jit(solution)/shard_map/ppermute | solution.py:191
  48.9 0.8 %place.1 = bf16[2,512,512]{2,1,0:T(8,128)(2,1)} custom-call(bf16[1,512,512]{2,1,0:T(8,128)(2,1)S(1)} %collective-permute-done.17.other_ref, bf16[2,512,512]{2,1,0:T(8,128)(2,1)} %get-tuple-element.24.whole_in), custom_call_target="tpu_custom_call", output_to_operand_aliasing={{}: (1, {})} | custom-call | tf_op jit(solution)/shard_map/place/pallas_call | solution.py:192
  (21 shorter events, 1.5 us)
Async XLA Ops:
  0.0 1.2 %copy-start = (f32[1,512,512]{2,1,0:T(8,128)S(1)}, f32[1,512,512]{2,1,0:T(8,128)}, u32[]{:S(2)}) copy-start(f32[1,512,512]{2,1,0:T(8,128)} %refs_8_.1) | copy-start | bytes 3145732
  1.2 35.7 %copy-start.1 = (f32[1,512,512]{2,1,0:T(8,128)S(1)}, f32[1,512,512]{2,1,0:T(8,128)}, u32[]{:S(2)}) copy-start(f32[1,512,512]{2,1,0:T(8,128)} %refs_8_.1) | copy-start | bytes 3145732
  2.1 8.8 %collective-permute-start = (f32[136,128]{1,0:T(8,128)S(1)}, f32[136,128]{1,0:T(8,128)S(1)}, u32[]{:S(2)}, u32[]{:S(2)}) collective-permute-start(f32[136,128]{1,0:T(8,128)S(1)} %get-tuple-element.15), channel_id=1, source_target_pairs={{0,23},{1,22},{2,21},{3,20},{4,19},{5,18},{6,17},{7,16},{8,31},{9,... | collective-permute-start | bytes 208904 | tf_op jit(solution)/shard_map/ppermute | solution.py:154
  6.5 5.2 %collective-permute-start.1 = (f32[136,128]{1,0:T(8,128)S(1)}, f32[136,128]{1,0:T(8,128)S(1)}, u32[]{:S(2)}, u32[]{:S(2)}) collective-permute-start(f32[136,128]{1,0:T(8,128)S(1)} %get-tuple-element.16), channel_id=1, source_target_pairs={{0,19},{1,18},{2,17},{3,16},{4,23},{5,22},{6,21},{7,20},{8,27},{9,... | collective-permute-start | bytes 208904 | tf_op jit(solution)/shard_map/ppermute | solution.py:154
  7.3 7.1 %collective-permute-start.2 = (f32[136,128]{1,0:T(8,128)S(1)}, f32[136,128]{1,0:T(8,128)S(1)}, u32[]{:S(2)}, u32[]{:S(2)}) collective-permute-start(f32[136,128]{1,0:T(8,128)S(1)} %get-tuple-element.17), channel_id=1, source_target_pairs={{0,21},{1,20},{2,23},{3,22},{4,17},{5,16},{6,19},{7,18},{8,29},{9,... | collective-permute-start | bytes 208904 | tf_op jit(solution)/shard_map/ppermute | solution.py:154
  8.1 7.1 %collective-permute-start.3 = (f32[136,128]{1,0:T(8,128)S(1)}, f32[136,128]{1,0:T(8,128)S(1)}, u32[]{:S(2)}, u32[]{:S(2)}) collective-permute-start(f32[136,128]{1,0:T(8,128)S(1)} %get-tuple-element.18), channel_id=1, source_target_pairs={{0,22},{1,23},{2,20},{3,21},{4,18},{5,19},{6,16},{7,17},{8,30},{9,... | collective-permute-start | bytes 208904 | tf_op jit(solution)/shard_map/ppermute | solution.py:154
  10.9 4.5 %collective-permute-start.4 = (f32[136,128]{1,0:T(8,128)S(1)}, f32[136,128]{1,0:T(8,128)S(1)}, u32[]{:S(2)}, u32[]{:S(2)}) collective-permute-start(f32[136,128]{1,0:T(8,128)S(1)} %get-tuple-element.19), channel_id=1, source_target_pairs={{0,17},{1,16},{2,19},{3,18},{4,21},{5,20},{6,23},{7,22},{8,25},{9,... | collective-permute-start | bytes 208904 | tf_op jit(solution)/shard_map/ppermute | solution.py:154
  10.9 5.6 %collective-permute-start.5 = (f32[136,128]{1,0:T(8,128)S(1)}, f32[136,128]{1,0:T(8,128)S(1)}, u32[]{:S(2)}, u32[]{:S(2)}) collective-permute-start(f32[136,128]{1,0:T(8,128)S(1)} %get-tuple-element.20), channel_id=1, source_target_pairs={{0,18},{1,19},{2,16},{3,17},{4,22},{5,23},{6,20},{7,21},{8,26},{9,... | collective-permute-start | bytes 208904 | tf_op jit(solution)/shard_map/ppermute | solution.py:154
  11.7 5.3 %collective-permute-start.6 = (f32[136,128]{1,0:T(8,128)S(1)}, f32[136,128]{1,0:T(8,128)S(1)}, u32[]{:S(2)}, u32[]{:S(2)}) collective-permute-start(f32[136,128]{1,0:T(8,128)S(1)} %get-tuple-element.21), channel_id=1, source_target_pairs={{0,20},{1,21},{2,22},{3,23},{4,16},{5,17},{6,18},{7,19},{8,28},{9,... | collective-permute-start | bytes 208904 | tf_op jit(solution)/shard_map/ppermute | solution.py:154
  14.4 2.6 %collective-permute-start.7 = (f32[136,128]{1,0:T(8,128)S(1)}, f32[136,128]{1,0:T(8,128)S(1)}, u32[]{:S(2)}, u32[]{:S(2)}) collective-permute-start(f32[136,128]{1,0:T(8,128)S(1)} %get-tuple-element.22), channel_id=1, source_target_pairs={{0,16},{1,17},{2,18},{3,19},{4,20},{5,21},{6,22},{7,23},{8,24},{9,... | collective-permute-start | bytes 208904 | tf_op jit(solution)/shard_map/ppermute | solution.py:154
  17.0 6.8 %collective-permute-start.8 = (f32[136,128]{1,0:T(8,128)S(1)}, f32[136,128]{1,0:T(8,128)S(1)}, u32[]{:S(2)}, u32[]{:S(2)}) collective-permute-start(f32[136,128]{1,0:T(8,128)S(1)} %add_add_fusion), channel_id=1, source_target_pairs={{0,8},{1,9},{2,10},{3,11},{4,12},{5,13},{6,14},{7,15},{8,0},{9,1},... | collective-permute-start | bytes 208904 | tf_op jit(solution)/shard_map/ppermute | solution.py:157
  23.8 4.5 %collective-permute-start.16 = (f32[136,128]{1,0:T(8,128)S(1)}, f32[136,128]{1,0:T(8,128)S(1)}, u32[]{:S(2)}, u32[]{:S(2)}) collective-permute-start(f32[136,128]{1,0:T(8,128)S(1)} %add.31), channel_id=1, source_target_pairs={{0,16},{1,17},{2,18},{3,19},{4,20},{5,21},{6,22},{7,23},{8,24},{9,... | collective-permute-start | bytes 208904 | tf_op jit(solution)/shard_map/ppermute | solution.py:154
  23.9 5.0 %collective-permute-start.15 = (f32[136,128]{1,0:T(8,128)S(1)}, f32[136,128]{1,0:T(8,128)S(1)}, u32[]{:S(2)}, u32[]{:S(2)}) collective-permute-start(f32[136,128]{1,0:T(8,128)S(1)} %add.31), channel_id=1, source_target_pairs={{0,20},{1,21},{2,22},{3,23},{4,16},{5,17},{6,18},{7,19},{8,28},{9,... | collective-permute-start | bytes 208904 | tf_op jit(solution)/shard_map/ppermute | solution.py:154
  24.5 6.5 %collective-permute-start.14 = (f32[136,128]{1,0:T(8,128)S(1)}, f32[136,128]{1,0:T(8,128)S(1)}, u32[]{:S(2)}, u32[]{:S(2)}) collective-permute-start(f32[136,128]{1,0:T(8,128)S(1)} %add.31), channel_id=1, source_target_pairs={{0,18},{1,19},{2,16},{3,17},{4,22},{5,23},{6,20},{7,21},{8,26},{9,... | collective-permute-start | bytes 208904 | tf_op jit(solution)/shard_map/ppermute | solution.py:154
  25.8 6.7 %collective-permute-start.13 = (f32[136,128]{1,0:T(8,128)S(1)}, f32[136,128]{1,0:T(8,128)S(1)}, u32[]{:S(2)}, u32[]{:S(2)}) collective-permute-start(f32[136,128]{1,0:T(8,128)S(1)} %add.31), channel_id=1, source_target_pairs={{0,17},{1,16},{2,19},{3,18},{4,21},{5,20},{6,23},{7,22},{8,25},{9,... | collective-permute-start | bytes 208904 | tf_op jit(solution)/shard_map/ppermute | solution.py:154
  26.9 5.6 %collective-permute-start.12 = (f32[136,128]{1,0:T(8,128)S(1)}, f32[136,128]{1,0:T(8,128)S(1)}, u32[]{:S(2)}, u32[]{:S(2)}) collective-permute-start(f32[136,128]{1,0:T(8,128)S(1)} %add.31), channel_id=1, source_target_pairs={{0,22},{1,23},{2,20},{3,21},{4,18},{5,19},{6,16},{7,17},{8,30},{9,... | collective-permute-start | bytes 208904 | tf_op jit(solution)/shard_map/ppermute | solution.py:154
  28.3 5.1 %collective-permute-start.11 = (f32[136,128]{1,0:T(8,128)S(1)}, f32[136,128]{1,0:T(8,128)S(1)}, u32[]{:S(2)}, u32[]{:S(2)}) collective-permute-start(f32[136,128]{1,0:T(8,128)S(1)} %add.31), channel_id=1, source_target_pairs={{0,21},{1,20},{2,23},{3,22},{4,17},{5,16},{6,19},{7,18},{8,29},{9,... | collective-permute-start | bytes 208904 | tf_op jit(solution)/shard_map/ppermute | solution.py:154
  28.9 6.6 %collective-permute-start.10 = (f32[136,128]{1,0:T(8,128)S(1)}, f32[136,128]{1,0:T(8,128)S(1)}, u32[]{:S(2)}, u32[]{:S(2)}) collective-permute-start(f32[136,128]{1,0:T(8,128)S(1)} %add.31), channel_id=1, source_target_pairs={{0,19},{1,18},{2,17},{3,16},{4,23},{5,22},{6,21},{7,20},{8,27},{9,... | collective-permute-start | bytes 208904 | tf_op jit(solution)/shard_map/ppermute | solution.py:154
  30.9 6.0 %collective-permute-start.9 = (f32[136,128]{1,0:T(8,128)S(1)}, f32[136,128]{1,0:T(8,128)S(1)}, u32[]{:S(2)}, u32[]{:S(2)}) collective-permute-start(f32[136,128]{1,0:T(8,128)S(1)} %add.31), channel_id=1, source_target_pairs={{0,23},{1,22},{2,21},{3,20},{4,19},{5,18},{6,17},{7,16},{8,31},{9,... | collective-permute-start | bytes 208904 | tf_op jit(solution)/shard_map/ppermute | solution.py:154
  46.9 2.0 %collective-permute-start.17 = (bf16[1,512,512]{2,1,0:T(8,128)(2,1)S(1)}, bf16[1,512,512]{2,1,0:T(8,128)(2,1)S(1)}, u32[]{:S(2)}, u32[]{:S(2)}) collective-permute-start(bf16[1,512,512]{2,1,0:T(8,128)(2,1)S(1)} %get-tuple-element.23), channel_id=1, source_target_pairs={{0,16},{16,0},{1,17},{17,1},{2,18},{18,2},{3,19},{19,3},{4,20},{20... | collective-permute-start | bytes 1572872 | tf_op jit(solution)/shard_map/ppermute | solution.py:191

commit v3 on v0

--- a/solution.py
+++ b/solution.py
@@ -26,8 +26,9 @@
 
 
 GROUP = 8
-SOUTH = (3, 4, 2, 0)
-NORTH = (7, 6, 5, 1)
+SOUTH = (3, 4, 2)
+NORTH = (7, 6, 5)
+DIRECT = 1
 
 
 def split(value):
@@ -55,16 +56,14 @@
 def block_starts(rows):
     me = lax.rem(lax.axis_index("tensor"), GROUP)
     north = lax.rem(lax.axis_index("dp"), 2) == 1
-    own, other = [], []
-    for first, second in zip(SOUTH, NORTH):
-        own.append(pl.multiple_of((me ^ jnp.where(north, second, first)) * rows, rows))
-        other.append(pl.multiple_of((me ^ jnp.where(north, first, second)) * rows, rows))
-    return own, other
+    own = [jnp.where(north, second, first) for first, second in zip(SOUTH, NORTH)]
+    other = [jnp.where(north, first, second) for first, second in zip(SOUTH, NORTH)]
+    return [pl.multiple_of((me ^ partner) * rows, rows) for partner in (0, DIRECT, *own, *other)]
 
 
 def gram_kernel(gradient_ref, *refs):
-    slots = len(SOUTH)
-    chunks, send, (mixed, cross) = refs[:slots], refs[slots], refs[slots + 1 :]
+    singles = 2 + len(SOUTH)
+    chunks, send, (mixed, cross) = refs[:singles], refs[singles], refs[singles + 1 :]
     half = mixed.shape[0]
     rows = half // GROUP
     size = chunks[0].shape[0]
@@ -90,27 +89,29 @@
                 at += rows
         out[at : at + SUBLANES, :] = tile
 
-    own, other = block_starts(rows)
-    for slot in range(slots):
-        write(send, slot * size, other[slot])
-    for slot in range(slots):
-        write(chunks[slot], 0, own[slot])
+    starts = block_starts(rows)
+    for slot, start in enumerate(starts[singles:]):
+        write(send, slot * size, start)
+    for out, start in zip(chunks, starts):
+        write(out, 0, start)
 
 
 def update_kernel(gain, *refs):
-    slots = len(SOUTH)
-    own_chunks, other_chunks = refs[:slots], refs[slots : 2 * slots]
-    gradient_ref, update_ref, whole_hbm, mixed, cross, store_sem = refs[2 * slots :]
+    chunks = refs[:GROUP]
+    gradient_ref, update_ref, whole_hbm, mixed, cross, store_sem = refs[GROUP:]
     half = mixed.shape[0]
     rows = half // GROUP
-    own, other = block_starts(rows)
-    for source, start in zip((*own_chunks, *other_chunks), own + other):
+    starts = block_starts(rows)
+    slots = len(SOUTH)
+    order = [1, 0, *range(1 + slots, 1, -1), *range(1 + 2 * slots, 1 + slots, -1)]
+    for source, index in zip(chunks, order):
+        start = starts[index]
         at = 0
         for target in (cross, mixed):
             for lane in range(0, half, LANES):
                 target[pl.ds(start, rows), lane : lane + LANES] = source[at : at + rows, :]
                 at += rows
-    diagonal = jnp.concatenate([own_chunks[0][at + i : at + i + 1, :] for i in range(half // LANES)], axis=1)
+    diagonal = jnp.concatenate([chunks[0][at + i : at + i + 1, :] for i in range(half // LANES)], axis=1)
     row, column = grid_pair(half)
     packed = mixed[...]
     flipped = packed.T
@@ -173,35 +174,37 @@
         moves = [(d * size + i, d * size + (i ^ partner[d % 2])) for d in range(pairs) for i in range(size)]
         return lax.ppermute(value, ("dp", "tensor"), moves)
 
-    *own, send = pl.pallas_call(
+    keep, direct, *own, send = pl.pallas_call(
         gram_kernel,
-        out_shape=[chunk] * slots + [jax.ShapeDtypeStruct((slots * length, LANES), jnp.float32)],
+        out_shape=[chunk] * (2 + slots) + [jax.ShapeDtypeStruct((slots * length, LANES), jnp.float32)],
         in_specs=[vmem],
-        out_specs=[vmem] * (slots + 1),
+        out_specs=[vmem] * (3 + slots),
         scratch_shapes=[pltpu.VMEM((half, half), jnp.float32)] * 2,
         compiler_params=pltpu.CompilerParams(vmem_limit_bytes=GRAM_VMEM),
         name="gram",
     )(gradient)
     held = flip(send)
+    mine = keep + far(direct, DIRECT)
     arrived = []
     for slot in range(slots):
         message = jnp.concatenate([own[slot], held[slot * length : (slot + 1) * length]])
         arrived.append(near(message, slot))
     partial = functools.reduce(jnp.add, arrived)
-    mine = partial[:length] + flip(partial[length:])
+    mine = mine + partial[:length] + flip(partial[length:])
     step = GROUP
     while step < size:
         mine = mine + far(mine, step)
         step *= 2
     both = jnp.concatenate([mine, flip(mine)])
-    gathered = [near(both, slot) for slot in range(slots)]
+    direct = far(mine, DIRECT)
+    gathered = [near(both, slot) for slot in range(slots)][::-1]
     passed = [flip(value[length:]) for value in gathered]
     gain = update_gain * math.sqrt(max(FEATURES, OUTPUTS))
     whole = jax.ShapeDtypeStruct((pairs, features, outputs), jnp.bfloat16)
     update, placed = pl.pallas_call(
         functools.partial(update_kernel, gain),
         out_shape=[jax.ShapeDtypeStruct(gradient.shape, jnp.bfloat16), whole],
-        in_specs=[vmem] * (2 * slots + 1),
+        in_specs=[vmem] * (GROUP + 1),
         out_specs=[vmem, anywhere],
         scratch_shapes=[
             pltpu.VMEM((half, half), jnp.float32),
@@ -210,7 +213,7 @@
         ],
         compiler_params=pltpu.CompilerParams(vmem_limit_bytes=UPDATE_VMEM),
         name="update",
-    )(*gathered, *passed, gradient)
+    )(direct, mine, *gathered, *passed, gradient)
     if pairs != 2:
         return lax.all_gather(update, "dp", axis=0, tiled=True)
     other = lax.ppermute(update, "dp", [(0, 1), (1, 0)])

time: 52 us -> 49.6 us (0.954)
  starting transfers between devices: 24.9 us -> 15.5 us
  waiting for transfers between devices: 13.8 us -> 20.9 us
    ppermute x7 -> x6, starting transfers between devices: 11.4 us -> 1.38 us  [flip(): return lax.ppermute(value, 'dp', [(d, d ^ 1) for d in range(pairs)])]
    ppermute x8 -> x6, waiting for transfers between devices: 3.79 us -> 10.7 us  [near(): return lax.ppermute(value, ('dp', 'tensor'), moves)]
    ppermute x1 -> x3, starting transfers between devices: 2.65 us -> 4.27 us  [far(): return lax.ppermute(value, 'tensor', [(i, i ^ step) for i in range(size)])]
    ppermute x8 -> x6, starting transfers between devices: 10.5 us -> 9.58 us  [near(): return lax.ppermute(value, ('dp', 'tensor'), moves)]
    ppermute x1 -> x3, waiting for transfers between devices: 4.25 us -> 4.06 us  [far(): return lax.ppermute(value, 'tensor', [(i, i ^ step) for i in range(size)])]
    ppermute x7 -> x6, waiting for transfers between devices: 4.24 us -> 4.41 us  [flip(): return lax.ppermute(value, 'dp', [(d, d ^ 1) for d in range(pairs)])]
  transfers between devices with their start and end apart: 17 -> 16, of which waited for: 8 -> 13; matrix products, arithmetic and copies ran while one was open for 0% -> 0% of each run, Pallas kernels for 0% -> 0%
where the time goes in v3:
time: 49.6 us; the launch traced here: 49.4 us
  waiting for transfers between devices  20.9 us (42%)
  starting transfers between devices  15.5 us (31%)
  Pallas kernels  11.6 us (23%)
  local copies, waits for them, and re-layouts  1.27 us (3%)
    ppermute x6, waiting for transfers between devices, near(): return lax.ppermute(value, ('dp', 'tensor'), moves)  10.7 us
    pallas_call x1, Pallas kernels, on_device(): pl.pallas_call(functools.partial(update_kernel, gain), out_shape=[jax.Sha...  9.97 us
    ppermute x6, starting transfers between devices, near(): return lax.ppermute(value, ('dp', 'tensor'), moves)  9.58 us
    ppermute x6, waiting for transfers between devices, flip(): return lax.ppermute(value, 'dp', [(d, d ^ 1) for d in range(pairs)])  4.41 us
    ppermute x3, starting transfers between devices, far(): return lax.ppermute(value, 'tensor', [(i, i ^ step) for i in range(size)])  4.27 us
    ppermute x3, waiting for transfers between devices, far(): return lax.ppermute(value, 'tensor', [(i, i ^ step) for i in range(size)])  4.06 us
    ppermute x1, waiting for transfers between devices, on_device(): other = lax.ppermute(update, 'dp', [(0, 1), (1, 0)])  1.74 us
    ppermute x6, starting transfers between devices, flip(): return lax.ppermute(value, 'dp', [(d, d ^ 1) for d in range(pairs)])  1.38 us
  transfers between devices with their start and end apart: 16, of which 13 were waited for; matrix products, arithmetic and copies ran while one was open for 0% of the time, Pallas kernels for 0%

profile of v3, /device:TPU:0, one launch (start us, length us, event | category | flops | bytes accessed | tf_op | source)
XLA Modules:
  0.0 49.4 jit_solution(1103789994878128588)
XLA Ops:
  0.0 1.2 %copy-done = f32[1,512,512]{2,1,0:T(8,128)S(1)} copy-done((f32[1,512,512]{2,1,0:T(8,128)S(1)}, f32[1,512,512]{2,1,0:T(8,128)}, u32[]{:S(2)}) %copy-start) | copy-done | bytes 1048600
  1.2 0.9 %gram.1 = (f32[136,128]{1,0:T(8,128)S(1)}, f32[136,128]{1,0:T(8,128)S(1)}, f32[136,128]{1,0:T(8,128)S(1)}, f32[136,128]{1,0:T(8,128)S(1)}, f32[136,128]{1,0:T(8,128)S(1)}, /*index=5*/f32[408,128]{1,0:T(8,128)S(1)}) custom-call(f32[1,512,512]{2,1,0:T(8,128)S(1)} %copy-done), custom_call_target="tpu_custom_call" | custom-call | tf_op jit(solution)/shard_map/gram/pallas_call | solution.py:177
  2.1 0.6 %collective-permute-start.1 = (f32[408,128]{1,0:T(8,128)S(1)}, f32[408,128]{1,0:T(8,128)S(1)}, u32[]{:S(2)}, u32[]{:S(2)}) collective-permute-start(f32[408,128]{1,0:T(8,128)S(1)} %get-tuple-element.16), channel_id=1, source_target_pairs={{0,16},{16,0},{1,17},{17,1},{2,18},{18,2},{3,19},{19,3},{4,20},{20... | collective-permute-start | bytes 626696 | tf_op jit(solution)/shard_map/ppermute | solution.py:167
  2.6 1.1 %collective-permute-done.1 = f32[408,128]{1,0:T(8,128)S(1)} collective-permute-done((f32[408,128]{1,0:T(8,128)S(1)}, f32[408,128]{1,0:T(8,128)S(1)}, u32[]{:S(2)}, u32[]{:S(2)}) %collective-permute-start.1) | collective-permute-done | bytes 208928 | tf_op jit(solution)/shard_map/ppermute | solution.py:167
  3.8 3.9 %collective-permute-start.2 = (f32[272,128]{1,0:T(8,128)S(1)}, f32[272,128]{1,0:T(8,128)S(1)}, u32[]{:S(2)}, u32[]{:S(2)}) collective-permute-start(f32[272,128]{1,0:T(8,128)S(1)} %pad_maximum_fusion), channel_id=1, source_target_pairs={{0,3},{1,2},{2,1},{3,0},{4,7},{5,6},{6,5},{7,4},{8,11},{9,10},{10,... | collective-permute-start | bytes 417800 | tf_op jit(solution)/shard_map/ppermute | solution.py:175
  7.7 0.6 %collective-permute-start.4 = (f32[272,128]{1,0:T(8,128)S(1)}, f32[272,128]{1,0:T(8,128)S(1)}, u32[]{:S(2)}, u32[]{:S(2)}) collective-permute-start(f32[272,128]{1,0:T(8,128)S(1)} %pad_maximum_fusion.2), channel_id=1, source_target_pairs={{0,2},{1,3},{2,0},{3,1},{4,6},{5,7},{6,4},{7,5},{8,10},{9,11},{10,... | collective-permute-start | bytes 417800 | tf_op jit(solution)/shard_map/ppermute | solution.py:175
  8.2 1.6 %collective-permute-start.3 = (f32[272,128]{1,0:T(8,128)S(1)}, f32[272,128]{1,0:T(8,128)S(1)}, u32[]{:S(2)}, u32[]{:S(2)}) collective-permute-start(f32[272,128]{1,0:T(8,128)S(1)} %pad_maximum_fusion.1), channel_id=1, source_target_pairs={{0,4},{1,5},{2,6},{3,7},{4,0},{5,1},{6,2},{7,3},{8,12},{9,13},{10,... | collective-permute-start | bytes 417800 | tf_op jit(solution)/shard_map/ppermute | solution.py:175
  10.4 3.6 %collective-permute-done.2 = f32[272,128]{1,0:T(8,128)S(1)} collective-permute-done((f32[272,128]{1,0:T(8,128)S(1)}, f32[272,128]{1,0:T(8,128)S(1)}, u32[]{:S(2)}, u32[]{:S(2)}) %collective-permute-start.2) | collective-permute-done | bytes 139296 | tf_op jit(solution)/shard_map/ppermute | solution.py:175
  14.0 0.6 %collective-permute-done.4 = f32[272,128]{1,0:T(8,128)S(1)} collective-permute-done((f32[272,128]{1,0:T(8,128)S(1)}, f32[272,128]{1,0:T(8,128)S(1)}, u32[]{:S(2)}, u32[]{:S(2)}) %collective-permute-start.4) | collective-permute-done | bytes 139296 | tf_op jit(solution)/shard_map/ppermute | solution.py:175
  14.9 0.7 %collective-permute-start.5 = (f32[136,128]{1,0:T(8,128)S(1)}, f32[136,128]{1,0:T(8,128)S(1)}, u32[]{:S(2)}, u32[]{:S(2)}) collective-permute-start(f32[136,128]{1,0:T(8,128)S(1)} %slice.36), channel_id=1, source_target_pairs={{0,16},{16,0},{1,17},{17,1},{2,18},{18,2},{3,19},{19,3},{4,20},{20... | collective-permute-start | bytes 208904 | tf_op jit(solution)/shard_map/ppermute | solution.py:167
  15.7 0.8 %collective-permute-done.5 = f32[136,128]{1,0:T(8,128)S(1)} collective-permute-done((f32[136,128]{1,0:T(8,128)S(1)}, f32[136,128]{1,0:T(8,128)S(1)}, u32[]{:S(2)}, u32[]{:S(2)}) %collective-permute-start.5) | collective-permute-done | bytes 69664 | tf_op jit(solution)/shard_map/ppermute | solution.py:167
  16.6 3.0 %collective-permute-start.6 = (f32[136,128]{1,0:T(8,128)S(1)}, f32[136,128]{1,0:T(8,128)S(1)}, u32[]{:S(2)}, u32[]{:S(2)}) collective-permute-start(f32[136,128]{1,0:T(8,128)S(1)} %fusion), channel_id=1, source_target_pairs={{0,8},{1,9},{2,10},{3,11},{4,12},{5,13},{6,14},{7,15},{8,0},{9,1},... | collective-permute-start | bytes 208904 | tf_op jit(solution)/shard_map/ppermute | solution.py:170
  19.6 4.0 %collective-permute-done.6 = f32[136,128]{1,0:T(8,128)S(1)} collective-permute-done((f32[136,128]{1,0:T(8,128)S(1)}, f32[136,128]{1,0:T(8,128)S(1)}, u32[]{:S(2)}, u32[]{:S(2)}) %collective-permute-start.6) | collective-permute-done | bytes 69664 | tf_op jit(solution)/shard_map/ppermute | solution.py:170
  23.7 1.2 %collective-permute-done.8 = f32[136,128]{1,0:T(8,128)S(1)} collective-permute-done((f32[136,128]{1,0:T(8,128)S(1)}, f32[136,128]{1,0:T(8,128)S(1)}, u32[]{:S(2)}, u32[]{:S(2)}) %collective-permute-start.8) | collective-permute-done | bytes 69664 | tf_op jit(solution)/shard_map/ppermute | solution.py:167
  24.9 2.7 %collective-permute-start.11 = (f32[272,128]{1,0:T(8,128)S(1)}, f32[272,128]{1,0:T(8,128)S(1)}, u32[]{:S(2)}, u32[]{:S(2)}) collective-permute-start(f32[272,128]{1,0:T(8,128)S(1)} %pad_maximum_fusion.3), channel_id=1, source_target_pairs={{0,3},{1,2},{2,1},{3,0},{4,7},{5,6},{6,5},{7,4},{8,11},{9,10},{10,... | collective-permute-start | bytes 417800 | tf_op jit(solution)/shard_map/ppermute | solution.py:175
  27.6 0.6 %collective-permute-start.10 = (f32[272,128]{1,0:T(8,128)S(1)}, f32[272,128]{1,0:T(8,128)S(1)}, u32[]{:S(2)}, u32[]{:S(2)}) collective-permute-start(f32[272,128]{1,0:T(8,128)S(1)} %pad_maximum_fusion.3), channel_id=1, source_target_pairs={{0,4},{1,5},{2,6},{3,7},{4,0},{5,1},{6,2},{7,3},{8,12},{9,13},{10,... | collective-permute-start | bytes 417800 | tf_op jit(solution)/shard_map/ppermute | solution.py:175
  28.4 0.7 %collective-permute-start.7 = (f32[136,128]{1,0:T(8,128)S(1)}, f32[136,128]{1,0:T(8,128)S(1)}, u32[]{:S(2)}, u32[]{:S(2)}) collective-permute-start(f32[136,128]{1,0:T(8,128)S(1)} %add.23.refs_1_), channel_id=1, source_target_pairs={{0,1},{1,0},{2,3},{3,2},{4,5},{5,4},{6,7},{7,6},{8,9},{9,8},{10,11... | collective-permute-start | bytes 208904 | tf_op jit(solution)/shard_map/ppermute | solution.py:170
  29.2 4.1 %collective-permute-done.11.refs_4_ = f32[272,128]{1,0:T(8,128)S(1)} collective-permute-done((f32[272,128]{1,0:T(8,128)S(1)}, f32[272,128]{1,0:T(8,128)S(1)}, u32[]{:S(2)}, u32[]{:S(2)}) %collective-permute-start.11) | collective-permute-done | bytes 139296 | tf_op jit(solution)/shard_map/ppermute | solution.py:175
  33.3 0.9 %collective-permute-done.10.refs_3_ = f32[272,128]{1,0:T(8,128)S(1)} collective-permute-done((f32[272,128]{1,0:T(8,128)S(1)}, f32[272,128]{1,0:T(8,128)S(1)}, u32[]{:S(2)}, u32[]{:S(2)}) %collective-permute-start.10) | collective-permute-done | bytes 139296 | tf_op jit(solution)/shard_map/ppermute | solution.py:175
  34.2 1.2 %collective-permute-done.9.refs_2_ = f32[272,128]{1,0:T(8,128)S(1)} collective-permute-done((f32[272,128]{1,0:T(8,128)S(1)}, f32[272,128]{1,0:T(8,128)S(1)}, u32[]{:S(2)}, u32[]{:S(2)}) %collective-permute-start.9) | collective-permute-done | bytes 139296 | tf_op jit(solution)/shard_map/ppermute | solution.py:175
  35.5 1.2 %collective-permute-done.12.refs_5_ = f32[136,128]{1,0:T(8,128)S(1)} collective-permute-done((f32[136,128]{1,0:T(8,128)S(1)}, f32[136,128]{1,0:T(8,128)S(1)}, u32[]{:S(2)}, u32[]{:S(2)}) %collective-permute-start.12) | collective-permute-done | bytes 69664 | tf_op jit(solution)/shard_map/ppermute | solution.py:167
  36.7 10.0 %update.1 = (bf16[1,512,512]{2,1,0:T(8,128)(2,1)S(1)}, bf16[2,512,512]{2,1,0:T(8,128)(2,1)}) custom-call(f32[136,128]{1,0:T(8,128)S(1)} %collective-permute-done.7.refs_0_, f32[136,128]{1,0:T(8,128)S(1)} %add.23.refs_1_, f32[272,128]{1,0:T(8,128)S(1)} %collective-permute-done.9.refs_2_, f32[272,128]{1,0:T(8,128)S(1)} %collective-permute-done.10.refs_3_, ...), custom_call_target="tpu_custom_call" | custom-call | tf_op jit(solution)/shard_map/update/pallas_call | solution.py:204
  46.9 1.7 %collective-permute-done.15.other_ref = bf16[1,512,512]{2,1,0:T(8,128)(2,1)S(1)} collective-permute-done((bf16[1,512,512]{2,1,0:T(8,128)(2,1)S(1)}, bf16[1,512,512]{2,1,0:T(8,128)(2,1)S(1)}, u32[]{:S(2)}, u32[]{:S(2)}) %collective-permute-start.15) | collective-permute-done | bytes 524320 | tf_op jit(solution)/shard_map/ppermute | solution.py:219
  48.6 0.8 %place.1 = bf16[2,512,512]{2,1,0:T(8,128)(2,1)} custom-call(bf16[1,512,512]{2,1,0:T(8,128)(2,1)S(1)} %collective-permute-done.15.other_ref, bf16[2,512,512]{2,1,0:T(8,128)(2,1)} %get-tuple-element.20.whole_in), custom_call_target="tpu_custom_call", output_to_operand_aliasing={{}: (1, {})} | custom-call | tf_op jit(solution)/shard_map/place/pallas_call | solution.py:220
  (27 shorter events, 1.5 us)
Async XLA Ops:
  0.0 1.2 %copy-start = (f32[1,512,512]{2,1,0:T(8,128)S(1)}, f32[1,512,512]{2,1,0:T(8,128)}, u32[]{:S(2)}) copy-start(f32[1,512,512]{2,1,0:T(8,128)} %refs_8_.1) | copy-start | bytes 3145732
  2.1 1.6 %collective-permute-start.1 = (f32[408,128]{1,0:T(8,128)S(1)}, f32[408,128]{1,0:T(8,128)S(1)}, u32[]{:S(2)}, u32[]{:S(2)}) collective-permute-start(f32[408,128]{1,0:T(8,128)S(1)} %get-tuple-element.16), channel_id=1, source_target_pairs={{0,16},{16,0},{1,17},{17,1},{2,18},{18,2},{3,19},{19,3},{4,20},{20... | collective-permute-start | bytes 626696 | tf_op jit(solution)/shard_map/ppermute | solution.py:167
  3.8 10.2 %collective-permute-start.2 = (f32[272,128]{1,0:T(8,128)S(1)}, f32[272,128]{1,0:T(8,128)S(1)}, u32[]{:S(2)}, u32[]{:S(2)}) collective-permute-start(f32[272,128]{1,0:T(8,128)S(1)} %pad_maximum_fusion), channel_id=1, source_target_pairs={{0,3},{1,2},{2,1},{3,0},{4,7},{5,6},{6,5},{7,4},{8,11},{9,10},{10,... | collective-permute-start | bytes 417800 | tf_op jit(solution)/shard_map/ppermute | solution.py:175
  7.7 6.9 %collective-permute-start.4 = (f32[272,128]{1,0:T(8,128)S(1)}, f32[272,128]{1,0:T(8,128)S(1)}, u32[]{:S(2)}, u32[]{:S(2)}) collective-permute-start(f32[272,128]{1,0:T(8,128)S(1)} %pad_maximum_fusion.2), channel_id=1, source_target_pairs={{0,2},{1,3},{2,0},{3,1},{4,6},{5,7},{6,4},{7,5},{8,10},{9,11},{10,... | collective-permute-start | bytes 417800 | tf_op jit(solution)/shard_map/ppermute | solution.py:175
  8.2 28.5 %copy-start.1 = (f32[1,512,512]{2,1,0:T(8,128)S(1)}, f32[1,512,512]{2,1,0:T(8,128)}, u32[]{:S(2)}) copy-start(f32[1,512,512]{2,1,0:T(8,128)} %refs_8_.1) | copy-start | bytes 3145732
  8.2 6.6 %collective-permute-start.3 = (f32[272,128]{1,0:T(8,128)S(1)}, f32[272,128]{1,0:T(8,128)S(1)}, u32[]{:S(2)}, u32[]{:S(2)}) collective-permute-start(f32[272,128]{1,0:T(8,128)S(1)} %pad_maximum_fusion.1), channel_id=1, source_target_pairs={{0,4},{1,5},{2,6},{3,7},{4,0},{5,1},{6,2},{7,3},{8,12},{9,13},{10,... | collective-permute-start | bytes 417800 | tf_op jit(solution)/shard_map/ppermute | solution.py:175
  9.9 5.8 %collective-permute-start = (f32[136,128]{1,0:T(8,128)S(1)}, f32[136,128]{1,0:T(8,128)S(1)}, u32[]{:S(2)}, u32[]{:S(2)}) collective-permute-start(f32[136,128]{1,0:T(8,128)S(1)} %get-tuple-element.14), channel_id=1, source_target_pairs={{0,1},{1,0},{2,3},{3,2},{4,5},{5,4},{6,7},{7,6},{8,9},{9,8},{10,11... | collective-permute-start | bytes 208904 | tf_op jit(solution)/shard_map/ppermute | solution.py:170
  14.9 1.7 %collective-permute-start.5 = (f32[136,128]{1,0:T(8,128)S(1)}, f32[136,128]{1,0:T(8,128)S(1)}, u32[]{:S(2)}, u32[]{:S(2)}) collective-permute-start(f32[136,128]{1,0:T(8,128)S(1)} %slice.36), channel_id=1, source_target_pairs={{0,16},{16,0},{1,17},{17,1},{2,18},{18,2},{3,19},{19,3},{4,20},{20... | collective-permute-start | bytes 208904 | tf_op jit(solution)/shard_map/ppermute | solution.py:167
  16.6 7.0 %collective-permute-start.6 = (f32[136,128]{1,0:T(8,128)S(1)}, f32[136,128]{1,0:T(8,128)S(1)}, u32[]{:S(2)}, u32[]{:S(2)}) collective-permute-start(f32[136,128]{1,0:T(8,128)S(1)} %fusion), channel_id=1, source_target_pairs={{0,8},{1,9},{2,10},{3,11},{4,12},{5,13},{6,14},{7,15},{8,0},{9,1},... | collective-permute-start | bytes 208904 | tf_op jit(solution)/shard_map/ppermute | solution.py:170
  23.6 1.3 %collective-permute-start.8 = (f32[136,128]{1,0:T(8,128)S(1)}, f32[136,128]{1,0:T(8,128)S(1)}, u32[]{:S(2)}, u32[]{:S(2)}) collective-permute-start(f32[136,128]{1,0:T(8,128)S(1)} %add.23.refs_1_), channel_id=1, source_target_pairs={{0,16},{16,0},{1,17},{17,1},{2,18},{18,2},{3,19},{19,3},{4,20},{20... | collective-permute-start | bytes 208904 | tf_op jit(solution)/shard_map/ppermute | solution.py:167
  24.9 8.4 %collective-permute-start.11 = (f32[272,128]{1,0:T(8,128)S(1)}, f32[272,128]{1,0:T(8,128)S(1)}, u32[]{:S(2)}, u32[]{:S(2)}) collective-permute-start(f32[272,128]{1,0:T(8,128)S(1)} %pad_maximum_fusion.3), channel_id=1, source_target_pairs={{0,3},{1,2},{2,1},{3,0},{4,7},{5,6},{6,5},{7,4},{8,11},{9,10},{10,... | collective-permute-start | bytes 417800 | tf_op jit(solution)/shard_map/ppermute | solution.py:175
  27.6 6.5 %collective-permute-start.10 = (f32[272,128]{1,0:T(8,128)S(1)}, f32[272,128]{1,0:T(8,128)S(1)}, u32[]{:S(2)}, u32[]{:S(2)}) collective-permute-start(f32[272,128]{1,0:T(8,128)S(1)} %pad_maximum_fusion.3), channel_id=1, source_target_pairs={{0,4},{1,5},{2,6},{3,7},{4,0},{5,1},{6,2},{7,3},{8,12},{9,13},{10,... | collective-permute-start | bytes 417800 | tf_op jit(solution)/shard_map/ppermute | solution.py:175
  28.3 7.1 %collective-permute-start.9 = (f32[272,128]{1,0:T(8,128)S(1)}, f32[272,128]{1,0:T(8,128)S(1)}, u32[]{:S(2)}, u32[]{:S(2)}) collective-permute-start(f32[272,128]{1,0:T(8,128)S(1)} %pad_maximum_fusion.3), channel_id=1, source_target_pairs={{0,2},{1,3},{2,0},{3,1},{4,6},{5,7},{6,4},{7,5},{8,10},{9,11},{10,... | collective-permute-start | bytes 417800 | tf_op jit(solution)/shard_map/ppermute | solution.py:175
  28.4 7.0 %collective-permute-start.7 = (f32[136,128]{1,0:T(8,128)S(1)}, f32[136,128]{1,0:T(8,128)S(1)}, u32[]{:S(2)}, u32[]{:S(2)}) collective-permute-start(f32[136,128]{1,0:T(8,128)S(1)} %add.23.refs_1_), channel_id=1, source_target_pairs={{0,1},{1,0},{2,3},{3,2},{4,5},{5,4},{6,7},{7,6},{8,9},{9,8},{10,11... | collective-permute-start | bytes 208904 | tf_op jit(solution)/shard_map/ppermute | solution.py:170
  33.3 2.1 %collective-permute-start.14 = (f32[136,128]{1,0:T(8,128)S(1)}, f32[136,128]{1,0:T(8,128)S(1)}, u32[]{:S(2)}, u32[]{:S(2)}) collective-permute-start(f32[136,128]{1,0:T(8,128)S(1)} %slice.39), channel_id=1, source_target_pairs={{0,16},{16,0},{1,17},{17,1},{2,18},{18,2},{3,19},{19,3},{4,20},{20... | collective-permute-start | bytes 208904 | tf_op jit(solution)/shard_map/ppermute | solution.py:167
  34.2 1.3 %collective-permute-start.13 = (f32[136,128]{1,0:T(8,128)S(1)}, f32[136,128]{1,0:T(8,128)S(1)}, u32[]{:S(2)}, u32[]{:S(2)}) collective-permute-start(f32[136,128]{1,0:T(8,128)S(1)} %slice.38), channel_id=1, source_target_pairs={{0,16},{16,0},{1,17},{17,1},{2,18},{18,2},{3,19},{19,3},{4,20},{20... | collective-permute-start | bytes 208904 | tf_op jit(solution)/shard_map/ppermute | solution.py:167
  35.4 1.3 %collective-permute-start.12 = (f32[136,128]{1,0:T(8,128)S(1)}, f32[136,128]{1,0:T(8,128)S(1)}, u32[]{:S(2)}, u32[]{:S(2)}) collective-permute-start(f32[136,128]{1,0:T(8,128)S(1)} %slice.37), channel_id=1, source_target_pairs={{0,16},{16,0},{1,17},{17,1},{2,18},{18,2},{3,19},{19,3},{4,20},{20... | collective-permute-start | bytes 208904 | tf_op jit(solution)/shard_map/ppermute | solution.py:167
  46.7 2.0 %collective-permute-start.15 = (bf16[1,512,512]{2,1,0:T(8,128)(2,1)S(1)}, bf16[1,512,512]{2,1,0:T(8,128)(2,1)S(1)}, u32[]{:S(2)}, u32[]{:S(2)}) collective-permute-start(bf16[1,512,512]{2,1,0:T(8,128)(2,1)S(1)} %get-tuple-element.19), channel_id=1, source_target_pairs={{0,16},{16,0},{1,17},{17,1},{2,18},{18,2},{3,19},{19,3},{4,20},{20... | collective-permute-start | bytes 1572872 | tf_op jit(solution)/shard_map/ppermute | solution.py:219

commit v4 on v3

--- a/solution.py
+++ b/solution.py
@@ -46,6 +46,19 @@
     return lax.dot_general(
         first, second, (((contract[0],), (contract[1],)), ((), ())), preferred_element_type=jnp.float32
     )
+
+
+class Factor:
+    def __init__(self, blocks):
+        (high_a, low_a), (high_b, low_b), (high_c, low_c) = [split(block) for block in blocks]
+        turned_high, turned_low = high_b.T, low_b.T
+        rows = [((high_a, high_b), (low_a, low_b)), ((turned_high, high_c), (turned_low, low_c))]
+        columns = [((high_a, turned_high), (low_a, turned_low)), ((high_b, high_c), (low_b, low_c))]
+        self.left = [jnp.concatenate([*high, *high, *low], axis=1) for high, low in rows]
+        self.right = [jnp.concatenate([*high, *low, *high], axis=0) for high, low in columns]
+
+    def times(self, other):
+        return [dot(self.left[i], other.right[j]) for i, j in ((0, 0), (0, 1), (1, 1))]
 
 
 def grid_pair(half):
@@ -113,33 +126,31 @@
                 at += rows
     diagonal = jnp.concatenate([chunks[0][at + i : at + i + 1, :] for i in range(half // LANES)], axis=1)
     row, column = grid_pair(half)
+    on_diagonal = row == column
     packed = mixed[...]
     flipped = packed.T
     first = jnp.where(row <= column, packed, flipped)
     second = jnp.where(row > column, packed, flipped)
-    on_diagonal = row == column
     second = jnp.where(on_diagonal, jnp.broadcast_to(diagonal, (half, half)), second)
-    corner = cross[...]
     norm = jnp.sum(jnp.where(on_diagonal, first + second, 0.0), keepdims=True)
     divisor = jnp.sqrt(norm) + norm_floor
     scale = 1.0 / (divisor * divisor)
-    gram = jnp.concatenate(
-        [jnp.concatenate([first, corner], axis=1), jnp.concatenate([corner.T, second], axis=1)], axis=0
-    )
-    gram = gram * scale
-    row, column = grid_pair(2 * half)
-    identity = jnp.where(row == column, linear_term, 0.0)
+    gram = (first * scale, cross[...] * scale, second * scale)
+    identity = jnp.where(on_diagonal, linear_term, 0.0)
     total = None
     for turn in range(ITERS):
-        gram_left, gram_right = wide(gram, 1), wide(gram, 0)
-        squared = dot(gram_left, gram_right)
-        polynomial = identity + cubic_term * gram + quintic_term * squared
-        polynomial_right = wide(polynomial, 0)
-        total = polynomial if total is None else dot(wide(total, 1), polynomial_right)
+        factor = Factor(gram)
+        squared = factor.times(factor)
+        polynomial = [cubic_term * g + quintic_term * q for g, q in zip(gram, squared)]
+        polynomial = Factor((identity + polynomial[0], polynomial[1], identity + polynomial[2]))
+        total = polynomial if total is None else Factor(total.times(polynomial))
         if turn + 1 < ITERS:
-            gram = dot(wide(dot(gram_left, polynomial_right), 1), polynomial_right)
-    polished = dot(wide(gradient_ref[0], 1), wide(total, 0))
-    update_ref[0] = ((gain / divisor) * polished).astype(jnp.bfloat16)
+            gram = Factor(factor.times(polynomial)).times(polynomial)
+    left = wide(gradient_ref[0], 1)
+    for index in range(2):
+        polished = dot(left, total.right[index])
+        columns = slice(index * half, (index + 1) * half)
+        update_ref[0, :, columns] = ((gain / divisor) * polished).astype(jnp.bfloat16)
     store = pltpu.make_async_copy(update_ref.at[0], whole_hbm.at[lax.axis_index("dp")], store_sem)
     store.start()
     store.wait()

time: 49.6 us -> 47.9 us (0.966)
  Pallas kernels: 11.6 us -> 9.9 us
    pallas_call x1, Pallas kernels: 9.97 us -> 8.24 us  [on_device(): pl.pallas_call(functools.partial(update_kernel, gain), out_shape=[jax.Sha...]
where the time goes in v4:
time: 47.9 us; the launch traced here: 47.7 us
  waiting for transfers between devices  20.9 us (44%)
  starting transfers between devices  15.5 us (32%)
  Pallas kernels  9.9 us (21%)
  local copies, waits for them, and re-layouts  1.27 us (3%)
    ppermute x6, waiting for transfers between devices, near(): return lax.ppermute(value, ('dp', 'tensor'), moves)  10.7 us
    ppermute x6, starting transfers between devices, near(): return lax.ppermute(value, ('dp', 'tensor'), moves)  9.58 us
    pallas_call x1, Pallas kernels, on_device(): pl.pallas_call(functools.partial(update_kernel, gain), out_shape=[jax.Sha...  8.24 us
    ppermute x6, waiting for transfers between devices, flip(): return lax.ppermute(value, 'dp', [(d, d ^ 1) for d in range(pairs)])  4.41 us
    ppermute x3, starting transfers between devices, far(): return lax.ppermute(value, 'tensor', [(i, i ^ step) for i in range(size)])  4.27 us
    ppermute x3, waiting for transfers between devices, far(): return lax.ppermute(value, 'tensor', [(i, i ^ step) for i in range(size)])  4.06 us
    ppermute x1, waiting for transfers between devices, on_device(): other = lax.ppermute(update, 'dp', [(0, 1), (1, 0)])  1.75 us
    ppermute x6, starting transfers between devices, flip(): return lax.ppermute(value, 'dp', [(d, d ^ 1) for d in range(pairs)])  1.38 us
  transfers between devices with their start and end apart: 16, of which 13 were waited for; matrix products, arithmetic and copies ran while one was open for 0% of the time, Pallas kernels for 0%

profile of v4, /device:TPU:0, one launch (start us, length us, event | category | flops | bytes accessed | tf_op | source)
XLA Modules:
  0.0 47.7 jit_solution(4100768500818682090)
XLA Ops:
  0.0 1.2 %copy-done = f32[1,512,512]{2,1,0:T(8,128)S(1)} copy-done((f32[1,512,512]{2,1,0:T(8,128)S(1)}, f32[1,512,512]{2,1,0:T(8,128)}, u32[]{:S(2)}) %copy-start) | copy-done | bytes 1048600
  1.2 0.9 %gram.1 = (f32[136,128]{1,0:T(8,128)S(1)}, f32[136,128]{1,0:T(8,128)S(1)}, f32[136,128]{1,0:T(8,128)S(1)}, f32[136,128]{1,0:T(8,128)S(1)}, f32[136,128]{1,0:T(8,128)S(1)}, /*index=5*/f32[408,128]{1,0:T(8,128)S(1)}) custom-call(f32[1,512,512]{2,1,0:T(8,128)S(1)} %copy-done), custom_call_target="tpu_custom_call" | custom-call | tf_op jit(solution)/shard_map/gram/pallas_call | solution.py:188
  2.1 0.6 %collective-permute-start.1 = (f32[408,128]{1,0:T(8,128)S(1)}, f32[408,128]{1,0:T(8,128)S(1)}, u32[]{:S(2)}, u32[]{:S(2)}) collective-permute-start(f32[408,128]{1,0:T(8,128)S(1)} %get-tuple-element.16), channel_id=1, source_target_pairs={{0,16},{16,0},{1,17},{17,1},{2,18},{18,2},{3,19},{19,3},{4,20},{20... | collective-permute-start | bytes 626696 | tf_op jit(solution)/shard_map/ppermute | solution.py:178
  2.6 1.1 %collective-permute-done.1 = f32[408,128]{1,0:T(8,128)S(1)} collective-permute-done((f32[408,128]{1,0:T(8,128)S(1)}, f32[408,128]{1,0:T(8,128)S(1)}, u32[]{:S(2)}, u32[]{:S(2)}) %collective-permute-start.1) | collective-permute-done | bytes 208928 | tf_op jit(solution)/shard_map/ppermute | solution.py:178
  3.8 3.9 %collective-permute-start.2 = (f32[272,128]{1,0:T(8,128)S(1)}, f32[272,128]{1,0:T(8,128)S(1)}, u32[]{:S(2)}, u32[]{:S(2)}) collective-permute-start(f32[272,128]{1,0:T(8,128)S(1)} %pad_maximum_fusion), channel_id=1, source_target_pairs={{0,3},{1,2},{2,1},{3,0},{4,7},{5,6},{6,5},{7,4},{8,11},{9,10},{10,... | collective-permute-start | bytes 417800 | tf_op jit(solution)/shard_map/ppermute | solution.py:186
  7.7 0.6 %collective-permute-start.4 = (f32[272,128]{1,0:T(8,128)S(1)}, f32[272,128]{1,0:T(8,128)S(1)}, u32[]{:S(2)}, u32[]{:S(2)}) collective-permute-start(f32[272,128]{1,0:T(8,128)S(1)} %pad_maximum_fusion.2), channel_id=1, source_target_pairs={{0,2},{1,3},{2,0},{3,1},{4,6},{5,7},{6,4},{7,5},{8,10},{9,11},{10,... | collective-permute-start | bytes 417800 | tf_op jit(solution)/shard_map/ppermute | solution.py:186
  8.2 1.6 %collective-permute-start.3 = (f32[272,128]{1,0:T(8,128)S(1)}, f32[272,128]{1,0:T(8,128)S(1)}, u32[]{:S(2)}, u32[]{:S(2)}) collective-permute-start(f32[272,128]{1,0:T(8,128)S(1)} %pad_maximum_fusion.1), channel_id=1, source_target_pairs={{0,4},{1,5},{2,6},{3,7},{4,0},{5,1},{6,2},{7,3},{8,12},{9,13},{10,... | collective-permute-start | bytes 417800 | tf_op jit(solution)/shard_map/ppermute | solution.py:186
  10.4 3.6 %collective-permute-done.2 = f32[272,128]{1,0:T(8,128)S(1)} collective-permute-done((f32[272,128]{1,0:T(8,128)S(1)}, f32[272,128]{1,0:T(8,128)S(1)}, u32[]{:S(2)}, u32[]{:S(2)}) %collective-permute-start.2) | collective-permute-done | bytes 139296 | tf_op jit(solution)/shard_map/ppermute | solution.py:186
  14.0 0.6 %collective-permute-done.4 = f32[272,128]{1,0:T(8,128)S(1)} collective-permute-done((f32[272,128]{1,0:T(8,128)S(1)}, f32[272,128]{1,0:T(8,128)S(1)}, u32[]{:S(2)}, u32[]{:S(2)}) %collective-permute-start.4) | collective-permute-done | bytes 139296 | tf_op jit(solution)/shard_map/ppermute | solution.py:186
  14.9 0.7 %collective-permute-start.5 = (f32[136,128]{1,0:T(8,128)S(1)}, f32[136,128]{1,0:T(8,128)S(1)}, u32[]{:S(2)}, u32[]{:S(2)}) collective-permute-start(f32[136,128]{1,0:T(8,128)S(1)} %slice.36), channel_id=1, source_target_pairs={{0,16},{16,0},{1,17},{17,1},{2,18},{18,2},{3,19},{19,3},{4,20},{20... | collective-permute-start | bytes 208904 | tf_op jit(solution)/shard_map/ppermute | solution.py:178
  15.7 0.8 %collective-permute-done.5 = f32[136,128]{1,0:T(8,128)S(1)} collective-permute-done((f32[136,128]{1,0:T(8,128)S(1)}, f32[136,128]{1,0:T(8,128)S(1)}, u32[]{:S(2)}, u32[]{:S(2)}) %collective-permute-start.5) | collective-permute-done | bytes 69664 | tf_op jit(solution)/shard_map/ppermute | solution.py:178
  16.6 3.0 %collective-permute-start.6 = (f32[136,128]{1,0:T(8,128)S(1)}, f32[136,128]{1,0:T(8,128)S(1)}, u32[]{:S(2)}, u32[]{:S(2)}) collective-permute-start(f32[136,128]{1,0:T(8,128)S(1)} %fusion), channel_id=1, source_target_pairs={{0,8},{1,9},{2,10},{3,11},{4,12},{5,13},{6,14},{7,15},{8,0},{9,1},... | collective-permute-start | bytes 208904 | tf_op jit(solution)/shard_map/ppermute | solution.py:181
  19.6 4.0 %collective-permute-done.6 = f32[136,128]{1,0:T(8,128)S(1)} collective-permute-done((f32[136,128]{1,0:T(8,128)S(1)}, f32[136,128]{1,0:T(8,128)S(1)}, u32[]{:S(2)}, u32[]{:S(2)}) %collective-permute-start.6) | collective-permute-done | bytes 69664 | tf_op jit(solution)/shard_map/ppermute | solution.py:181
  23.7 1.2 %collective-permute-done.8 = f32[136,128]{1,0:T(8,128)S(1)} collective-permute-done((f32[136,128]{1,0:T(8,128)S(1)}, f32[136,128]{1,0:T(8,128)S(1)}, u32[]{:S(2)}, u32[]{:S(2)}) %collective-permute-start.8) | collective-permute-done | bytes 69664 | tf_op jit(solution)/shard_map/ppermute | solution.py:178
  24.9 2.7 %collective-permute-start.11 = (f32[272,128]{1,0:T(8,128)S(1)}, f32[272,128]{1,0:T(8,128)S(1)}, u32[]{:S(2)}, u32[]{:S(2)}) collective-permute-start(f32[272,128]{1,0:T(8,128)S(1)} %pad_maximum_fusion.3), channel_id=1, source_target_pairs={{0,3},{1,2},{2,1},{3,0},{4,7},{5,6},{6,5},{7,4},{8,11},{9,10},{10,... | collective-permute-start | bytes 417800 | tf_op jit(solution)/shard_map/ppermute | solution.py:186
  27.6 0.6 %collective-permute-start.10 = (f32[272,128]{1,0:T(8,128)S(1)}, f32[272,128]{1,0:T(8,128)S(1)}, u32[]{:S(2)}, u32[]{:S(2)}) collective-permute-start(f32[272,128]{1,0:T(8,128)S(1)} %pad_maximum_fusion.3), channel_id=1, source_target_pairs={{0,4},{1,5},{2,6},{3,7},{4,0},{5,1},{6,2},{7,3},{8,12},{9,13},{10,... | collective-permute-start | bytes 417800 | tf_op jit(solution)/shard_map/ppermute | solution.py:186
  28.4 0.7 %collective-permute-start.7 = (f32[136,128]{1,0:T(8,128)S(1)}, f32[136,128]{1,0:T(8,128)S(1)}, u32[]{:S(2)}, u32[]{:S(2)}) collective-permute-start(f32[136,128]{1,0:T(8,128)S(1)} %add.23.refs_1_), channel_id=1, source_target_pairs={{0,1},{1,0},{2,3},{3,2},{4,5},{5,4},{6,7},{7,6},{8,9},{9,8},{10,11... | collective-permute-start | bytes 208904 | tf_op jit(solution)/shard_map/ppermute | solution.py:181
  29.2 4.1 %collective-permute-done.11.refs_4_ = f32[272,128]{1,0:T(8,128)S(1)} collective-permute-done((f32[272,128]{1,0:T(8,128)S(1)}, f32[272,128]{1,0:T(8,128)S(1)}, u32[]{:S(2)}, u32[]{:S(2)}) %collective-permute-start.11) | collective-permute-done | bytes 139296 | tf_op jit(solution)/shard_map/ppermute | solution.py:186
  33.3 0.9 %collective-permute-done.10.refs_3_ = f32[272,128]{1,0:T(8,128)S(1)} collective-permute-done((f32[272,128]{1,0:T(8,128)S(1)}, f32[272,128]{1,0:T(8,128)S(1)}, u32[]{:S(2)}, u32[]{:S(2)}) %collective-permute-start.10) | collective-permute-done | bytes 139296 | tf_op jit(solution)/shard_map/ppermute | solution.py:186
  34.2 1.2 %collective-permute-done.9.refs_2_ = f32[272,128]{1,0:T(8,128)S(1)} collective-permute-done((f32[272,128]{1,0:T(8,128)S(1)}, f32[272,128]{1,0:T(8,128)S(1)}, u32[]{:S(2)}, u32[]{:S(2)}) %collective-permute-start.9) | collective-permute-done | bytes 139296 | tf_op jit(solution)/shard_map/ppermute | solution.py:186
  35.5 1.2 %collective-permute-done.12.refs_5_ = f32[136,128]{1,0:T(8,128)S(1)} collective-permute-done((f32[136,128]{1,0:T(8,128)S(1)}, f32[136,128]{1,0:T(8,128)S(1)}, u32[]{:S(2)}, u32[]{:S(2)}) %collective-permute-start.12) | collective-permute-done | bytes 69664 | tf_op jit(solution)/shard_map/ppermute | solution.py:178
  36.7 8.2 %update.1 = (bf16[1,512,512]{2,1,0:T(8,128)(2,1)S(1)}, bf16[2,512,512]{2,1,0:T(8,128)(2,1)}) custom-call(f32[136,128]{1,0:T(8,128)S(1)} %collective-permute-done.7.refs_0_, f32[136,128]{1,0:T(8,128)S(1)} %add.23.refs_1_, f32[272,128]{1,0:T(8,128)S(1)} %collective-permute-done.9.refs_2_, f32[272,128]{1,0:T(8,128)S(1)} %collective-permute-done.10.refs_3_, ...), custom_call_target="tpu_custom_call" | custom-call | tf_op jit(solution)/shard_map/update/pallas_call | solution.py:215
  45.2 1.8 %collective-permute-done.15.other_ref = bf16[1,512,512]{2,1,0:T(8,128)(2,1)S(1)} collective-permute-done((bf16[1,512,512]{2,1,0:T(8,128)(2,1)S(1)}, bf16[1,512,512]{2,1,0:T(8,128)(2,1)S(1)}, u32[]{:S(2)}, u32[]{:S(2)}) %collective-permute-start.15) | collective-permute-done | bytes 524320 | tf_op jit(solution)/shard_map/ppermute | solution.py:230
  46.9 0.8 %place.1 = bf16[2,512,512]{2,1,0:T(8,128)(2,1)} custom-call(bf16[1,512,512]{2,1,0:T(8,128)(2,1)S(1)} %collective-permute-done.15.other_ref, bf16[2,512,512]{2,1,0:T(8,128)(2,1)} %get-tuple-element.20.whole_in), custom_call_target="tpu_custom_call", output_to_operand_aliasing={{}: (1, {})} | custom-call | tf_op jit(solution)/shard_map/place/pallas_call | solution.py:231
  (27 shorter events, 1.5 us)
Async XLA Ops:
  0.0 1.2 %copy-start = (f32[1,512,512]{2,1,0:T(8,128)S(1)}, f32[1,512,512]{2,1,0:T(8,128)}, u32[]{:S(2)}) copy-start(f32[1,512,512]{2,1,0:T(8,128)} %refs_8_.1) | copy-start | bytes 3145732
  2.1 1.6 %collective-permute-start.1 = (f32[408,128]{1,0:T(8,128)S(1)}, f32[408,128]{1,0:T(8,128)S(1)}, u32[]{:S(2)}, u32[]{:S(2)}) collective-permute-start(f32[408,128]{1,0:T(8,128)S(1)} %get-tuple-element.16), channel_id=1, source_target_pairs={{0,16},{16,0},{1,17},{17,1},{2,18},{18,2},{3,19},{19,3},{4,20},{20... | collective-permute-start | bytes 626696 | tf_op jit(solution)/shard_map/ppermute | solution.py:178
  3.8 10.2 %collective-permute-start.2 = (f32[272,128]{1,0:T(8,128)S(1)}, f32[272,128]{1,0:T(8,128)S(1)}, u32[]{:S(2)}, u32[]{:S(2)}) collective-permute-start(f32[272,128]{1,0:T(8,128)S(1)} %pad_maximum_fusion), channel_id=1, source_target_pairs={{0,3},{1,2},{2,1},{3,0},{4,7},{5,6},{6,5},{7,4},{8,11},{9,10},{10,... | collective-permute-start | bytes 417800 | tf_op jit(solution)/shard_map/ppermute | solution.py:186
  7.7 6.9 %collective-permute-start.4 = (f32[272,128]{1,0:T(8,128)S(1)}, f32[272,128]{1,0:T(8,128)S(1)}, u32[]{:S(2)}, u32[]{:S(2)}) collective-permute-start(f32[272,128]{1,0:T(8,128)S(1)} %pad_maximum_fusion.2), channel_id=1, source_target_pairs={{0,2},{1,3},{2,0},{3,1},{4,6},{5,7},{6,4},{7,5},{8,10},{9,11},{10,... | collective-permute-start | bytes 417800 | tf_op jit(solution)/shard_map/ppermute | solution.py:186
  8.2 28.5 %copy-start.1 = (f32[1,512,512]{2,1,0:T(8,128)S(1)}, f32[1,512,512]{2,1,0:T(8,128)}, u32[]{:S(2)}) copy-start(f32[1,512,512]{2,1,0:T(8,128)} %refs_8_.1) | copy-start | bytes 3145732
  8.2 6.6 %collective-permute-start.3 = (f32[272,128]{1,0:T(8,128)S(1)}, f32[272,128]{1,0:T(8,128)S(1)}, u32[]{:S(2)}, u32[]{:S(2)}) collective-permute-start(f32[272,128]{1,0:T(8,128)S(1)} %pad_maximum_fusion.1), channel_id=1, source_target_pairs={{0,4},{1,5},{2,6},{3,7},{4,0},{5,1},{6,2},{7,3},{8,12},{9,13},{10,... | collective-permute-start | bytes 417800 | tf_op jit(solution)/shard_map/ppermute | solution.py:186
  9.9 5.8 %collective-permute-start = (f32[136,128]{1,0:T(8,128)S(1)}, f32[136,128]{1,0:T(8,128)S(1)}, u32[]{:S(2)}, u32[]{:S(2)}) collective-permute-start(f32[136,128]{1,0:T(8,128)S(1)} %get-tuple-element.14), channel_id=1, source_target_pairs={{0,1},{1,0},{2,3},{3,2},{4,5},{5,4},{6,7},{7,6},{8,9},{9,8},{10,11... | collective-permute-start | bytes 208904 | tf_op jit(solution)/shard_map/ppermute | solution.py:181
  14.9 1.7 %collective-permute-start.5 = (f32[136,128]{1,0:T(8,128)S(1)}, f32[136,128]{1,0:T(8,128)S(1)}, u32[]{:S(2)}, u32[]{:S(2)}) collective-permute-start(f32[136,128]{1,0:T(8,128)S(1)} %slice.36), channel_id=1, source_target_pairs={{0,16},{16,0},{1,17},{17,1},{2,18},{18,2},{3,19},{19,3},{4,20},{20... | collective-permute-start | bytes 208904 | tf_op jit(solution)/shard_map/ppermute | solution.py:178
  16.6 7.0 %collective-permute-start.6 = (f32[136,128]{1,0:T(8,128)S(1)}, f32[136,128]{1,0:T(8,128)S(1)}, u32[]{:S(2)}, u32[]{:S(2)}) collective-permute-start(f32[136,128]{1,0:T(8,128)S(1)} %fusion), channel_id=1, source_target_pairs={{0,8},{1,9},{2,10},{3,11},{4,12},{5,13},{6,14},{7,15},{8,0},{9,1},... | collective-permute-start | bytes 208904 | tf_op jit(solution)/shard_map/ppermute | solution.py:181
  23.6 1.3 %collective-permute-start.8 = (f32[136,128]{1,0:T(8,128)S(1)}, f32[136,128]{1,0:T(8,128)S(1)}, u32[]{:S(2)}, u32[]{:S(2)}) collective-permute-start(f32[136,128]{1,0:T(8,128)S(1)} %add.23.refs_1_), channel_id=1, source_target_pairs={{0,16},{16,0},{1,17},{17,1},{2,18},{18,2},{3,19},{19,3},{4,20},{20... | collective-permute-start | bytes 208904 | tf_op jit(solution)/shard_map/ppermute | solution.py:178
  24.9 8.4 %collective-permute-start.11 = (f32[272,128]{1,0:T(8,128)S(1)}, f32[272,128]{1,0:T(8,128)S(1)}, u32[]{:S(2)}, u32[]{:S(2)}) collective-permute-start(f32[272,128]{1,0:T(8,128)S(1)} %pad_maximum_fusion.3), channel_id=1, source_target_pairs={{0,3},{1,2},{2,1},{3,0},{4,7},{5,6},{6,5},{7,4},{8,11},{9,10},{10,... | collective-permute-start | bytes 417800 | tf_op jit(solution)/shard_map/ppermute | solution.py:186
  27.6 6.5 %collective-permute-start.10 = (f32[272,128]{1,0:T(8,128)S(1)}, f32[272,128]{1,0:T(8,128)S(1)}, u32[]{:S(2)}, u32[]{:S(2)}) collective-permute-start(f32[272,128]{1,0:T(8,128)S(1)} %pad_maximum_fusion.3), channel_id=1, source_target_pairs={{0,4},{1,5},{2,6},{3,7},{4,0},{5,1},{6,2},{7,3},{8,12},{9,13},{10,... | collective-permute-start | bytes 417800 | tf_op jit(solution)/shard_map/ppermute | solution.py:186
  28.3 7.1 %collective-permute-start.9 = (f32[272,128]{1,0:T(8,128)S(1)}, f32[272,128]{1,0:T(8,128)S(1)}, u32[]{:S(2)}, u32[]{:S(2)}) collective-permute-start(f32[272,128]{1,0:T(8,128)S(1)} %pad_maximum_fusion.3), channel_id=1, source_target_pairs={{0,2},{1,3},{2,0},{3,1},{4,6},{5,7},{6,4},{7,5},{8,10},{9,11},{10,... | collective-permute-start | bytes 417800 | tf_op jit(solution)/shard_map/ppermute | solution.py:186
  28.4 7.0 %collective-permute-start.7 = (f32[136,128]{1,0:T(8,128)S(1)}, f32[136,128]{1,0:T(8,128)S(1)}, u32[]{:S(2)}, u32[]{:S(2)}) collective-permute-start(f32[136,128]{1,0:T(8,128)S(1)} %add.23.refs_1_), channel_id=1, source_target_pairs={{0,1},{1,0},{2,3},{3,2},{4,5},{5,4},{6,7},{7,6},{8,9},{9,8},{10,11... | collective-permute-start | bytes 208904 | tf_op jit(solution)/shard_map/ppermute | solution.py:181
  33.3 2.1 %collective-permute-start.14 = (f32[136,128]{1,0:T(8,128)S(1)}, f32[136,128]{1,0:T(8,128)S(1)}, u32[]{:S(2)}, u32[]{:S(2)}) collective-permute-start(f32[136,128]{1,0:T(8,128)S(1)} %slice.39), channel_id=1, source_target_pairs={{0,16},{16,0},{1,17},{17,1},{2,18},{18,2},{3,19},{19,3},{4,20},{20... | collective-permute-start | bytes 208904 | tf_op jit(solution)/shard_map/ppermute | solution.py:178
  34.2 1.3 %collective-permute-start.13 = (f32[136,128]{1,0:T(8,128)S(1)}, f32[136,128]{1,0:T(8,128)S(1)}, u32[]{:S(2)}, u32[]{:S(2)}) collective-permute-start(f32[136,128]{1,0:T(8,128)S(1)} %slice.38), channel_id=1, source_target_pairs={{0,16},{16,0},{1,17},{17,1},{2,18},{18,2},{3,19},{19,3},{4,20},{20... | collective-permute-start | bytes 208904 | tf_op jit(solution)/shard_map/ppermute | solution.py:178
  35.4 1.3 %collective-permute-start.12 = (f32[136,128]{1,0:T(8,128)S(1)}, f32[136,128]{1,0:T(8,128)S(1)}, u32[]{:S(2)}, u32[]{:S(2)}) collective-permute-start(f32[136,128]{1,0:T(8,128)S(1)} %slice.37), channel_id=1, source_target_pairs={{0,16},{16,0},{1,17},{17,1},{2,18},{18,2},{3,19},{19,3},{4,20},{20... | collective-permute-start | bytes 208904 | tf_op jit(solution)/shard_map/ppermute | solution.py:178
  44.9 2.0 %collective-permute-start.15 = (bf16[1,512,512]{2,1,0:T(8,128)(2,1)S(1)}, bf16[1,512,512]{2,1,0:T(8,128)(2,1)S(1)}, u32[]{:S(2)}, u32[]{:S(2)}) collective-permute-start(bf16[1,512,512]{2,1,0:T(8,128)(2,1)S(1)} %get-tuple-element.19), channel_id=1, source_target_pairs={{0,16},{16,0},{1,17},{17,1},{2,18},{18,2},{3,19},{19,3},{4,20},{20... | collective-permute-start | bytes 1572872 | tf_op jit(solution)/shard_map/ppermute | solution.py:230

commit v5 on v4

--- a/solution.py
+++ b/solution.py
@@ -21,14 +21,14 @@
 LANES = 128
 GRAM_VMEM = 16 << 20
 UPDATE_VMEM = 32 << 20
+PLACE_COST = 1 << 20
 PLACE_VMEM = 4 << 20
 SUBLANES = 8
 
 
 GROUP = 8
-SOUTH = (3, 4, 2)
-NORTH = (7, 6, 5)
-DIRECT = 1
+PARTNERS = (0, 7, 6, 5, 3, 4, 2, 1)
+BACK = (1, 2, 4, 3, 5, 6, 7)
 
 
 def split(value):
@@ -66,20 +66,15 @@
     return lax.broadcasted_iota(jnp.int32, shape, 0), lax.broadcasted_iota(jnp.int32, shape, 1)
 
 
-def block_starts(rows):
+def block_starts(rows, order):
     me = lax.rem(lax.axis_index("tensor"), GROUP)
-    north = lax.rem(lax.axis_index("dp"), 2) == 1
-    own = [jnp.where(north, second, first) for first, second in zip(SOUTH, NORTH)]
-    other = [jnp.where(north, first, second) for first, second in zip(SOUTH, NORTH)]
-    return [pl.multiple_of((me ^ partner) * rows, rows) for partner in (0, DIRECT, *own, *other)]
+    return [pl.multiple_of((me ^ partner) * rows, rows) for partner in order]
 
 
 def gram_kernel(gradient_ref, *refs):
-    singles = 2 + len(SOUTH)
-    chunks, send, (mixed, cross) = refs[:singles], refs[singles], refs[singles + 1 :]
+    chunks, (mixed, cross) = refs[:GROUP], refs[GROUP:]
     half = mixed.shape[0]
     rows = half // GROUP
-    size = chunks[0].shape[0]
     high, low = split(gradient_ref[0])
     left = jnp.concatenate([high, high, low], axis=0)
     right = jnp.concatenate([high, low, high], axis=0)
@@ -102,23 +97,16 @@
                 at += rows
         out[at : at + SUBLANES, :] = tile
 
-    starts = block_starts(rows)
-    for slot, start in enumerate(starts[singles:]):
-        write(send, slot * size, start)
-    for out, start in zip(chunks, starts):
+    for out, start in zip(chunks, block_starts(rows, PARTNERS)):
         write(out, 0, start)
 
 
 def update_kernel(gain, *refs):
     chunks = refs[:GROUP]
-    gradient_ref, update_ref, whole_hbm, mixed, cross, store_sem = refs[GROUP:]
+    gradient_ref, update_ref, mixed, cross = refs[GROUP:]
     half = mixed.shape[0]
     rows = half // GROUP
-    starts = block_starts(rows)
-    slots = len(SOUTH)
-    order = [1, 0, *range(1 + slots, 1, -1), *range(1 + 2 * slots, 1 + slots, -1)]
-    for source, index in zip(chunks, order):
-        start = starts[index]
+    for source, start in zip(chunks, block_starts(rows, (0, *BACK))):
         at = 0
         for target in (cross, mixed):
             for lane in range(0, half, LANES):
@@ -151,14 +139,12 @@
         polished = dot(left, total.right[index])
         columns = slice(index * half, (index + 1) * half)
         update_ref[0, :, columns] = ((gain / divisor) * polished).astype(jnp.bfloat16)
-    store = pltpu.make_async_copy(update_ref.at[0], whole_hbm.at[lax.axis_index("dp")], store_sem)
-    store.start()
-    store.wait()
-
-
-def place_kernel(other_ref, whole_in, whole_hbm, sem):
-    del whole_in
-    copy = pltpu.make_async_copy(other_ref.at[0], whole_hbm.at[1 - lax.axis_index("dp")], sem)
+
+
+def place_kernel(flipped, value_ref, *refs):
+    whole_hbm, sem = refs[-2:]
+    index = lax.axis_index("dp")
+    copy = pltpu.make_async_copy(value_ref.at[0], whole_hbm.at[1 - index if flipped else index], sem)
     copy.start()
     copy.wait()
 
@@ -167,77 +153,59 @@
     pairs, size = mesh.shape["dp"], mesh.shape["tensor"]
     assert pairs % 2 == 0 and size % GROUP == 0 and size & (size - 1) == 0
     _, features, outputs = gradient.shape
-    half, slots = outputs // 2, len(SOUTH)
+    half = outputs // 2
     assert half // LANES <= SUBLANES
     length = 2 * half // GROUP * (half // LANES) + SUBLANES
     chunk = jax.ShapeDtypeStruct((length, LANES), jnp.float32)
     vmem = pl.BlockSpec(memory_space=pltpu.VMEM)
     anywhere = pl.BlockSpec(memory_space=pl.ANY)
 
-    def flip(value):
-        return lax.ppermute(value, "dp", [(d, d ^ 1) for d in range(pairs)])
-
-    def far(value, step):
-        return lax.ppermute(value, "tensor", [(i, i ^ step) for i in range(size)])
-
-    def near(value, slot):
-        partner = (SOUTH[slot], NORTH[slot])
-        moves = [(d * size + i, d * size + (i ^ partner[d % 2])) for d in range(pairs) for i in range(size)]
-        return lax.ppermute(value, ("dp", "tensor"), moves)
-
-    keep, direct, *own, send = pl.pallas_call(
+    def swap(value, partner):
+        return lax.ppermute(value, "tensor", [(i, i ^ partner) for i in range(size)])
+
+    chunks = pl.pallas_call(
         gram_kernel,
-        out_shape=[chunk] * (2 + slots) + [jax.ShapeDtypeStruct((slots * length, LANES), jnp.float32)],
+        out_shape=[chunk] * GROUP,
         in_specs=[vmem],
-        out_specs=[vmem] * (3 + slots),
+        out_specs=[vmem] * GROUP,
         scratch_shapes=[pltpu.VMEM((half, half), jnp.float32)] * 2,
         compiler_params=pltpu.CompilerParams(vmem_limit_bytes=GRAM_VMEM),
         name="gram",
     )(gradient)
-    held = flip(send)
-    mine = keep + far(direct, DIRECT)
-    arrived = []
-    for slot in range(slots):
-        message = jnp.concatenate([own[slot], held[slot * length : (slot + 1) * length]])
-        arrived.append(near(message, slot))
-    partial = functools.reduce(jnp.add, arrived)
-    mine = mine + partial[:length] + flip(partial[length:])
+    owned = functools.reduce(jnp.add, [swap(value, k) for value, k in zip(chunks[1:], PARTNERS[1:])], chunks[0])
     step = GROUP
     while step < size:
-        mine = mine + far(mine, step)
+        owned = owned + swap(owned, step)
         step *= 2
-    both = jnp.concatenate([mine, flip(mine)])
-    direct = far(mine, DIRECT)
-    gathered = [near(both, slot) for slot in range(slots)][::-1]
-    passed = [flip(value[length:]) for value in gathered]
+    gathered = [owned] + [swap(owned, partner) for partner in BACK]
     gain = update_gain * math.sqrt(max(FEATURES, OUTPUTS))
-    whole = jax.ShapeDtypeStruct((pairs, features, outputs), jnp.bfloat16)
-    update, placed = pl.pallas_call(
+    update = pl.pallas_call(
         functools.partial(update_kernel, gain),
-        out_shape=[jax.ShapeDtypeStruct(gradient.shape, jnp.bfloat16), whole],
+        out_shape=jax.ShapeDtypeStruct(gradient.shape, jnp.bfloat16),
         in_specs=[vmem] * (GROUP + 1),
-        out_specs=[vmem, anywhere],
-        scratch_shapes=[
-            pltpu.VMEM((half, half), jnp.float32),
-            pltpu.VMEM((half, half), jnp.float32),
-            pltpu.SemaphoreType.DMA,
-        ],
+        out_specs=vmem,
+        scratch_shapes=[pltpu.VMEM((half, half), jnp.float32)] * 2,
         compiler_params=pltpu.CompilerParams(vmem_limit_bytes=UPDATE_VMEM),
         name="update",
-    )(direct, mine, *gathered, *passed, gradient)
+    )(*gathered, gradient)
     if pairs != 2:
         return lax.all_gather(update, "dp", axis=0, tiled=True)
+
+    def place(flipped, *operands):
+        return pl.pallas_call(
+            functools.partial(place_kernel, flipped),
+            out_shape=jax.ShapeDtypeStruct((pairs, features, outputs), jnp.bfloat16),
+            in_specs=[vmem, anywhere][: len(operands)],
+            out_specs=anywhere,
+            scratch_shapes=[pltpu.SemaphoreType.DMA],
+            input_output_aliases={1: 0} if flipped else {},
+            compiler_params=pltpu.CompilerParams(vmem_limit_bytes=PLACE_VMEM),
+            cost_estimate=pl.CostEstimate(flops=PLACE_COST, bytes_accessed=2 * features * outputs, transcendentals=0),
+            name="place",
+        )(*operands)
+
     other = lax.ppermute(update, "dp", [(0, 1), (1, 0)])
-    return pl.pallas_call(
-        place_kernel,
-        out_shape=whole,
-        in_specs=[vmem, anywhere],
-        out_specs=anywhere,
-        scratch_shapes=[pltpu.SemaphoreType.DMA],
-        input_output_aliases={1: 0},
-        compiler_params=pltpu.CompilerParams(vmem_limit_bytes=PLACE_VMEM),
-        name="place",
-    )(other, placed)
+    return place(True, other, place(False, update))
 
 
 def solution(mesh):

time: 47.9 us -> 45.2 us (0.944)
  waiting for transfers between devices: 20.9 us -> 10.6 us
  starting transfers between devices: 15.5 us -> 23.3 us
    ppermute x15, waiting for transfers between devices: 19.1 us -> 9.49 us  [swap(): lax.ppermute(value, 'tensor', [(i, i ^ partner) for i in range(size)])]
    ppermute x15, starting transfers between devices: 15.2 us -> 23.2 us  [swap(): lax.ppermute(value, 'tensor', [(i, i ^ partner) for i in range(size)])]
    ppermute x1, waiting for transfers between devices: 1.75 us -> 1.08 us  [on_device(): other = lax.ppermute(update, 'dp', [(0, 1), (1, 0)])]
    pallas_call x3 -> x4, Pallas kernels: 9.9 us -> 9.91 us  [the longest x1 7.44 us: on_device(): pl.pallas_call(functools.partial(update_kernel, gain), out_shape=jax.Shap...]
  transfers between devices with their start and end apart: 16 -> 16, of which waited for: 13 -> 11; matrix products, arithmetic and copies ran while one was open for 0% -> 0% of each run, Pallas kernels for 0% -> 2%
where the time goes in v5:
time: 45.2 us; the launch traced here: 45.1 us
  starting transfers between devices  23.3 us (52%)
  waiting for transfers between devices  10.6 us (23%)
  Pallas kernels  9.91 us (22%)
  local copies, waits for them, and re-layouts  1.23 us (3%)
    ppermute x15, starting transfers between devices, swap(): lax.ppermute(value, 'tensor', [(i, i ^ partner) for i in range(size)])  23.2 us
    ppermute x15, waiting for transfers between devices, swap(): lax.ppermute(value, 'tensor', [(i, i ^ partner) for i in range(size)])  9.49 us
    pallas_call x1, Pallas kernels, on_device(): pl.pallas_call(functools.partial(update_kernel, gain), out_shape=jax.Shap...  7.44 us
    pallas_call x2, Pallas kernels, place(): pl.pallas_call(functools.partial(place_kernel, flipped), out_shape=jax.Sh...  1.61 us
    unnamed x4, local copies, waits for them, and re-layouts  1.23 us
    ppermute x1, waiting for transfers between devices, on_device(): other = lax.ppermute(update, 'dp', [(0, 1), (1, 0)])  1.08 us
  transfers between devices with their start and end apart: 16, of which 11 were waited for; matrix products, arithmetic and copies ran while one was open for 0% of the time, Pallas kernels for 2%

profile of v5, /device:TPU:0, one launch (start us, length us, event | category | flops | bytes accessed | tf_op | source)
XLA Modules:
  0.0 45.1 jit_solution(5703392370116226093)
XLA Ops:
  0.0 1.2 %copy-done = f32[1,512,512]{2,1,0:T(8,128)S(1)} copy-done((f32[1,512,512]{2,1,0:T(8,128)S(1)}, f32[1,512,512]{2,1,0:T(8,128)}, u32[]{:S(2)}) %copy-start) | copy-done | bytes 1048600
  1.2 0.9 %gram.1 = (f32[136,128]{1,0:T(8,128)S(1)}, f32[136,128]{1,0:T(8,128)S(1)}, f32[136,128]{1,0:T(8,128)S(1)}, f32[136,128]{1,0:T(8,128)S(1)}, f32[136,128]{1,0:T(8,...) custom-call(f32[1,512,512]{2,1,0:T(8,128)S(1)} %copy-done), custom_call_target="tpu_custom_call" | custom-call | tf_op jit(solution)/shard_map/gram/pallas_call | solution.py:166
  2.1 5.0 %collective-permute-start = (f32[136,128]{1,0:T(8,128)S(1)}, f32[136,128]{1,0:T(8,128)S(1)}, u32[]{:S(2)}, u32[]{:S(2)}) collective-permute-start(f32[136,128]{1,0:T(8,128)S(1)} %get-tuple-element.14), channel_id=1, source_target_pairs={{0,7},{1,6},{2,5},{3,4},{4,3},{5,2},{6,1},{7,0},{8,15},{9,14},{10,... | collective-permute-start | bytes 208904 | tf_op jit(solution)/shard_map/ppermute | solution.py:164
  7.5 1.5 %collective-permute-start.2 = (f32[136,128]{1,0:T(8,128)S(1)}, f32[136,128]{1,0:T(8,128)S(1)}, u32[]{:S(2)}, u32[]{:S(2)}) collective-permute-start(f32[136,128]{1,0:T(8,128)S(1)} %get-tuple-element.16), channel_id=1, source_target_pairs={{0,5},{1,4},{2,7},{3,6},{4,1},{5,0},{6,3},{7,2},{8,13},{9,12},{10,... | collective-permute-start | bytes 208904 | tf_op jit(solution)/shard_map/ppermute | solution.py:164
  9.0 2.5 %collective-permute-start.3 = (f32[136,128]{1,0:T(8,128)S(1)}, f32[136,128]{1,0:T(8,128)S(1)}, u32[]{:S(2)}, u32[]{:S(2)}) collective-permute-start(f32[136,128]{1,0:T(8,128)S(1)} %get-tuple-element.17), channel_id=1, source_target_pairs={{0,3},{1,2},{2,1},{3,0},{4,7},{5,6},{6,5},{7,4},{8,11},{9,10},{10,... | collective-permute-start | bytes 208904 | tf_op jit(solution)/shard_map/ppermute | solution.py:164
  12.7 0.8 %collective-permute-start.6 = (f32[136,128]{1,0:T(8,128)S(1)}, f32[136,128]{1,0:T(8,128)S(1)}, u32[]{:S(2)}, u32[]{:S(2)}) collective-permute-start(f32[136,128]{1,0:T(8,128)S(1)} %get-tuple-element.20), channel_id=1, source_target_pairs={{0,1},{1,0},{2,3},{3,2},{4,5},{5,4},{6,7},{7,6},{8,9},{9,8},{10,11... | collective-permute-start | bytes 208904 | tf_op jit(solution)/shard_map/ppermute | solution.py:164
  13.5 1.6 %collective-permute-done.3 = f32[136,128]{1,0:T(8,128)S(1)} collective-permute-done((f32[136,128]{1,0:T(8,128)S(1)}, f32[136,128]{1,0:T(8,128)S(1)}, u32[]{:S(2)}, u32[]{:S(2)}) %collective-permute-start.3) | collective-permute-done | bytes 69664 | tf_op jit(solution)/shard_map/ppermute | solution.py:164
  15.1 0.7 %collective-permute-done.4 = f32[136,128]{1,0:T(8,128)S(1)} collective-permute-done((f32[136,128]{1,0:T(8,128)S(1)}, f32[136,128]{1,0:T(8,128)S(1)}, u32[]{:S(2)}, u32[]{:S(2)}) %collective-permute-start.4) | collective-permute-done | bytes 69664 | tf_op jit(solution)/shard_map/ppermute | solution.py:164
  16.2 0.8 %collective-permute-done.6 = f32[136,128]{1,0:T(8,128)S(1)} collective-permute-done((f32[136,128]{1,0:T(8,128)S(1)}, f32[136,128]{1,0:T(8,128)S(1)}, u32[]{:S(2)}, u32[]{:S(2)}) %collective-permute-start.6) | collective-permute-done | bytes 69664 | tf_op jit(solution)/shard_map/ppermute | solution.py:164
  17.1 2.6 %collective-permute-start.7 = (f32[136,128]{1,0:T(8,128)S(1)}, f32[136,128]{1,0:T(8,128)S(1)}, u32[]{:S(2)}, u32[]{:S(2)}) collective-permute-start(f32[136,128]{1,0:T(8,128)S(1)} %add_add_fusion), channel_id=1, source_target_pairs={{0,8},{1,9},{2,10},{3,11},{4,12},{5,13},{6,14},{7,15},{8,0},{9,1},... | collective-permute-start | bytes 208904 | tf_op jit(solution)/shard_map/ppermute | solution.py:164
  19.7 2.6 %collective-permute-done.7 = f32[136,128]{1,0:T(8,128)S(1)} collective-permute-done((f32[136,128]{1,0:T(8,128)S(1)}, f32[136,128]{1,0:T(8,128)S(1)}, u32[]{:S(2)}, u32[]{:S(2)}) %collective-permute-start.7) | collective-permute-done | bytes 69664 | tf_op jit(solution)/shard_map/ppermute | solution.py:164
  22.4 2.3 %collective-permute-start.14 = (f32[136,128]{1,0:T(8,128)S(1)}, f32[136,128]{1,0:T(8,128)S(1)}, u32[]{:S(2)}, u32[]{:S(2)}) collective-permute-start(f32[136,128]{1,0:T(8,128)S(1)} %add.31.refs_0_), channel_id=1, source_target_pairs={{0,7},{1,6},{2,5},{3,4},{4,3},{5,2},{6,1},{7,0},{8,15},{9,14},{10,... | collective-permute-start | bytes 208904 | tf_op jit(solution)/shard_map/ppermute | solution.py:164
  24.7 0.9 %collective-permute-start.13 = (f32[136,128]{1,0:T(8,128)S(1)}, f32[136,128]{1,0:T(8,128)S(1)}, u32[]{:S(2)}, u32[]{:S(2)}) collective-permute-start(f32[136,128]{1,0:T(8,128)S(1)} %add.31.refs_0_), channel_id=1, source_target_pairs={{0,6},{1,7},{2,4},{3,5},{4,2},{5,3},{6,0},{7,1},{8,14},{9,15},{10,... | collective-permute-start | bytes 208904 | tf_op jit(solution)/shard_map/ppermute | solution.py:164
  25.6 2.0 %collective-permute-start.12 = (f32[136,128]{1,0:T(8,128)S(1)}, f32[136,128]{1,0:T(8,128)S(1)}, u32[]{:S(2)}, u32[]{:S(2)}) collective-permute-start(f32[136,128]{1,0:T(8,128)S(1)} %add.31.refs_0_), channel_id=1, source_target_pairs={{0,5},{1,4},{2,7},{3,6},{4,1},{5,0},{6,3},{7,2},{8,13},{9,12},{10,... | collective-permute-start | bytes 208904 | tf_op jit(solution)/shard_map/ppermute | solution.py:164
  27.6 1.5 %collective-permute-start.11 = (f32[136,128]{1,0:T(8,128)S(1)}, f32[136,128]{1,0:T(8,128)S(1)}, u32[]{:S(2)}, u32[]{:S(2)}) collective-permute-start(f32[136,128]{1,0:T(8,128)S(1)} %add.31.refs_0_), channel_id=1, source_target_pairs={{0,3},{1,2},{2,1},{3,0},{4,7},{5,6},{6,5},{7,4},{8,11},{9,10},{10,... | collective-permute-start | bytes 208904 | tf_op jit(solution)/shard_map/ppermute | solution.py:164
  29.5 1.0 %collective-permute-start.9 = (f32[136,128]{1,0:T(8,128)S(1)}, f32[136,128]{1,0:T(8,128)S(1)}, u32[]{:S(2)}, u32[]{:S(2)}) collective-permute-start(f32[136,128]{1,0:T(8,128)S(1)} %add.31.refs_0_), channel_id=1, source_target_pairs={{0,2},{1,3},{2,0},{3,1},{4,6},{5,7},{6,4},{7,5},{8,10},{9,11},{10,... | collective-permute-start | bytes 208904 | tf_op jit(solution)/shard_map/ppermute | solution.py:164
  30.5 1.2 %collective-permute-start.8 = (f32[136,128]{1,0:T(8,128)S(1)}, f32[136,128]{1,0:T(8,128)S(1)}, u32[]{:S(2)}, u32[]{:S(2)}) collective-permute-start(f32[136,128]{1,0:T(8,128)S(1)} %add.31.refs_0_), channel_id=1, source_target_pairs={{0,1},{1,0},{2,3},{3,2},{4,5},{5,4},{6,7},{7,6},{8,9},{9,8},{10,11... | collective-permute-start | bytes 208904 | tf_op jit(solution)/shard_map/ppermute | solution.py:164
  31.8 1.0 %collective-permute-done.11.refs_4_ = f32[136,128]{1,0:T(8,128)S(1)} collective-permute-done((f32[136,128]{1,0:T(8,128)S(1)}, f32[136,128]{1,0:T(8,128)S(1)}, u32[]{:S(2)}, u32[]{:S(2)}) %collective-permute-start.11) | collective-permute-done | bytes 69664 | tf_op jit(solution)/shard_map/ppermute | solution.py:164
  32.8 0.6 %collective-permute-done.10.refs_3_ = f32[136,128]{1,0:T(8,128)S(1)} collective-permute-done((f32[136,128]{1,0:T(8,128)S(1)}, f32[136,128]{1,0:T(8,128)S(1)}, u32[]{:S(2)}, u32[]{:S(2)}) %collective-permute-start.10) | collective-permute-done | bytes 69664 | tf_op jit(solution)/shard_map/ppermute | solution.py:164
  33.8 1.0 %collective-permute-done.8.refs_1_ = f32[136,128]{1,0:T(8,128)S(1)} collective-permute-done((f32[136,128]{1,0:T(8,128)S(1)}, f32[136,128]{1,0:T(8,128)S(1)}, u32[]{:S(2)}, u32[]{:S(2)}) %collective-permute-start.8) | collective-permute-done | bytes 69664 | tf_op jit(solution)/shard_map/ppermute | solution.py:164
  34.8 7.4 %update.1.value_ref = bf16[1,512,512]{2,1,0:T(8,128)(2,1)S(1)} custom-call(f32[136,128]{1,0:T(8,128)S(1)} %add.31.refs_0_, f32[136,128]{1,0:T(8,128)S(1)} %collective-permute-done.8.refs_1_, f32[136,128]{1,0:T(8,128)S(1)} %collective-permute-done.9.refs_2_, f32[136,128]{1,0:T(8,128)S(1)} %collective-permute-done.10.refs_3_, ...), custom_call_target="tpu_custom_call" | custom-call | tf_op jit(solution)/shard_map/update/pallas_call | solution.py:182
  42.4 0.8 %place.2.refs_0_ = bf16[2,512,512]{2,1,0:T(8,128)(2,1)} custom-call(bf16[1,512,512]{2,1,0:T(8,128)(2,1)S(1)} %update.1.value_ref), custom_call_target="tpu_custom_call" | custom-call | flops 1048576 | bytes 524288 | tf_op jit(solution)/shard_map/place/pallas_call | solution.py:195
  43.2 1.1 %collective-permute-done.15.value_ref = bf16[1,512,512]{2,1,0:T(8,128)(2,1)S(1)} collective-permute-done((bf16[1,512,512]{2,1,0:T(8,128)(2,1)S(1)}, bf16[1,512,512]{2,1,0:T(8,128)(2,1)S(1)}, u32[]{:S(2)}, u32[]{:S(2)}) %collective-permute-start.15) | collective-permute-done | bytes 524320 | tf_op jit(solution)/shard_map/ppermute | solution.py:207
  44.3 0.8 %place.3 = bf16[2,512,512]{2,1,0:T(8,128)(2,1)} custom-call(bf16[1,512,512]{2,1,0:T(8,128)(2,1)S(1)} %collective-permute-done.15.value_ref, bf16[2,512,512]{2,1,0:T(8,128)(2,1)} %place.2.refs_0_), custom_call_target="tpu_custom_call", output_to_operand_aliasing={{}: (1, {})} | custom-call | flops 1048576 | bytes 524288 | tf_op jit(solution)/shard_map/place/pallas_call | solution.py:195
  (18 shorter events, 3.1 us)
Async XLA Ops:
  0.0 1.2 %copy-start = (f32[1,512,512]{2,1,0:T(8,128)S(1)}, f32[1,512,512]{2,1,0:T(8,128)}, u32[]{:S(2)}) copy-start(f32[1,512,512]{2,1,0:T(8,128)} %refs_8_.1) | copy-start | bytes 3145732
  1.2 33.6 %copy-start.1 = (f32[1,512,512]{2,1,0:T(8,128)S(1)}, f32[1,512,512]{2,1,0:T(8,128)}, u32[]{:S(2)}) copy-start(f32[1,512,512]{2,1,0:T(8,128)} %refs_8_.1) | copy-start | bytes 3145732
  2.1 9.8 %collective-permute-start = (f32[136,128]{1,0:T(8,128)S(1)}, f32[136,128]{1,0:T(8,128)S(1)}, u32[]{:S(2)}, u32[]{:S(2)}) collective-permute-start(f32[136,128]{1,0:T(8,128)S(1)} %get-tuple-element.14), channel_id=1, source_target_pairs={{0,7},{1,6},{2,5},{3,4},{4,3},{5,2},{6,1},{7,0},{8,15},{9,14},{10,... | collective-permute-start | bytes 208904 | tf_op jit(solution)/shard_map/ppermute | solution.py:164
  7.1 5.6 %collective-permute-start.1 = (f32[136,128]{1,0:T(8,128)S(1)}, f32[136,128]{1,0:T(8,128)S(1)}, u32[]{:S(2)}, u32[]{:S(2)}) collective-permute-start(f32[136,128]{1,0:T(8,128)S(1)} %get-tuple-element.15), channel_id=1, source_target_pairs={{0,6},{1,7},{2,4},{3,5},{4,2},{5,3},{6,0},{7,1},{8,14},{9,15},{10,... | collective-permute-start | bytes 208904 | tf_op jit(solution)/shard_map/ppermute | solution.py:164
  7.5 6.0 %collective-permute-start.2 = (f32[136,128]{1,0:T(8,128)S(1)}, f32[136,128]{1,0:T(8,128)S(1)}, u32[]{:S(2)}, u32[]{:S(2)}) collective-permute-start(f32[136,128]{1,0:T(8,128)S(1)} %get-tuple-element.16), channel_id=1, source_target_pairs={{0,5},{1,4},{2,7},{3,6},{4,1},{5,0},{6,3},{7,2},{8,13},{9,12},{10,... | collective-permute-start | bytes 208904 | tf_op jit(solution)/shard_map/ppermute | solution.py:164
  9.0 6.1 %collective-permute-start.3 = (f32[136,128]{1,0:T(8,128)S(1)}, f32[136,128]{1,0:T(8,128)S(1)}, u32[]{:S(2)}, u32[]{:S(2)}) collective-permute-start(f32[136,128]{1,0:T(8,128)S(1)} %get-tuple-element.17), channel_id=1, source_target_pairs={{0,3},{1,2},{2,1},{3,0},{4,7},{5,6},{6,5},{7,4},{8,11},{9,10},{10,... | collective-permute-start | bytes 208904 | tf_op jit(solution)/shard_map/ppermute | solution.py:164
  11.5 4.3 %collective-permute-start.4 = (f32[136,128]{1,0:T(8,128)S(1)}, f32[136,128]{1,0:T(8,128)S(1)}, u32[]{:S(2)}, u32[]{:S(2)}) collective-permute-start(f32[136,128]{1,0:T(8,128)S(1)} %get-tuple-element.18), channel_id=1, source_target_pairs={{0,4},{1,5},{2,6},{3,7},{4,0},{5,1},{6,2},{7,3},{8,12},{9,13},{10,... | collective-permute-start | bytes 208904 | tf_op jit(solution)/shard_map/ppermute | solution.py:164
  11.9 4.3 %collective-permute-start.5 = (f32[136,128]{1,0:T(8,128)S(1)}, f32[136,128]{1,0:T(8,128)S(1)}, u32[]{:S(2)}, u32[]{:S(2)}) collective-permute-start(f32[136,128]{1,0:T(8,128)S(1)} %get-tuple-element.19), channel_id=1, source_target_pairs={{0,2},{1,3},{2,0},{3,1},{4,6},{5,7},{6,4},{7,5},{8,10},{9,11},{10,... | collective-permute-start | bytes 208904 | tf_op jit(solution)/shard_map/ppermute | solution.py:164
  12.7 4.3 %collective-permute-start.6 = (f32[136,128]{1,0:T(8,128)S(1)}, f32[136,128]{1,0:T(8,128)S(1)}, u32[]{:S(2)}, u32[]{:S(2)}) collective-permute-start(f32[136,128]{1,0:T(8,128)S(1)} %get-tuple-element.20), channel_id=1, source_target_pairs={{0,1},{1,0},{2,3},{3,2},{4,5},{5,4},{6,7},{7,6},{8,9},{9,8},{10,11... | collective-permute-start | bytes 208904 | tf_op jit(solution)/shard_map/ppermute | solution.py:164
  17.1 5.3 %collective-permute-start.7 = (f32[136,128]{1,0:T(8,128)S(1)}, f32[136,128]{1,0:T(8,128)S(1)}, u32[]{:S(2)}, u32[]{:S(2)}) collective-permute-start(f32[136,128]{1,0:T(8,128)S(1)} %add_add_fusion), channel_id=1, source_target_pairs={{0,8},{1,9},{2,10},{3,11},{4,12},{5,13},{6,14},{7,15},{8,0},{9,1},... | collective-permute-start | bytes 208904 | tf_op jit(solution)/shard_map/ppermute | solution.py:164
  22.4 7.1 %collective-permute-start.14 = (f32[136,128]{1,0:T(8,128)S(1)}, f32[136,128]{1,0:T(8,128)S(1)}, u32[]{:S(2)}, u32[]{:S(2)}) collective-permute-start(f32[136,128]{1,0:T(8,128)S(1)} %add.31.refs_0_), channel_id=1, source_target_pairs={{0,7},{1,6},{2,5},{3,4},{4,3},{5,2},{6,1},{7,0},{8,15},{9,14},{10,... | collective-permute-start | bytes 208904 | tf_op jit(solution)/shard_map/ppermute | solution.py:164
  24.7 5.9 %collective-permute-start.13 = (f32[136,128]{1,0:T(8,128)S(1)}, f32[136,128]{1,0:T(8,128)S(1)}, u32[]{:S(2)}, u32[]{:S(2)}) collective-permute-start(f32[136,128]{1,0:T(8,128)S(1)} %add.31.refs_0_), channel_id=1, source_target_pairs={{0,6},{1,7},{2,4},{3,5},{4,2},{5,3},{6,0},{7,1},{8,14},{9,15},{10,... | collective-permute-start | bytes 208904 | tf_op jit(solution)/shard_map/ppermute | solution.py:164
  25.6 6.2 %collective-permute-start.12 = (f32[136,128]{1,0:T(8,128)S(1)}, f32[136,128]{1,0:T(8,128)S(1)}, u32[]{:S(2)}, u32[]{:S(2)}) collective-permute-start(f32[136,128]{1,0:T(8,128)S(1)} %add.31.refs_0_), channel_id=1, source_target_pairs={{0,5},{1,4},{2,7},{3,6},{4,1},{5,0},{6,3},{7,2},{8,13},{9,12},{10,... | collective-permute-start | bytes 208904 | tf_op jit(solution)/shard_map/ppermute | solution.py:164
  27.6 5.2 %collective-permute-start.11 = (f32[136,128]{1,0:T(8,128)S(1)}, f32[136,128]{1,0:T(8,128)S(1)}, u32[]{:S(2)}, u32[]{:S(2)}) collective-permute-start(f32[136,128]{1,0:T(8,128)S(1)} %add.31.refs_0_), channel_id=1, source_target_pairs={{0,3},{1,2},{2,1},{3,0},{4,7},{5,6},{6,5},{7,4},{8,11},{9,10},{10,... | collective-permute-start | bytes 208904 | tf_op jit(solution)/shard_map/ppermute | solution.py:164
  29.0 4.3 %collective-permute-start.10 = (f32[136,128]{1,0:T(8,128)S(1)}, f32[136,128]{1,0:T(8,128)S(1)}, u32[]{:S(2)}, u32[]{:S(2)}) collective-permute-start(f32[136,128]{1,0:T(8,128)S(1)} %add.31.refs_0_), channel_id=1, source_target_pairs={{0,4},{1,5},{2,6},{3,7},{4,0},{5,1},{6,2},{7,3},{8,12},{9,13},{10,... | collective-permute-start | bytes 208904 | tf_op jit(solution)/shard_map/ppermute | solution.py:164
  29.5 4.3 %collective-permute-start.9 = (f32[136,128]{1,0:T(8,128)S(1)}, f32[136,128]{1,0:T(8,128)S(1)}, u32[]{:S(2)}, u32[]{:S(2)}) collective-permute-start(f32[136,128]{1,0:T(8,128)S(1)} %add.31.refs_0_), channel_id=1, source_target_pairs={{0,2},{1,3},{2,0},{3,1},{4,6},{5,7},{6,4},{7,5},{8,10},{9,11},{10,... | collective-permute-start | bytes 208904 | tf_op jit(solution)/shard_map/ppermute | solution.py:164
  30.5 4.3 %collective-permute-start.8 = (f32[136,128]{1,0:T(8,128)S(1)}, f32[136,128]{1,0:T(8,128)S(1)}, u32[]{:S(2)}, u32[]{:S(2)}) collective-permute-start(f32[136,128]{1,0:T(8,128)S(1)} %add.31.refs_0_), channel_id=1, source_target_pairs={{0,1},{1,0},{2,3},{3,2},{4,5},{5,4},{6,7},{7,6},{8,9},{9,8},{10,11... | collective-permute-start | bytes 208904 | tf_op jit(solution)/shard_map/ppermute | solution.py:164
  42.3 2.0 %collective-permute-start.15 = (bf16[1,512,512]{2,1,0:T(8,128)(2,1)S(1)}, bf16[1,512,512]{2,1,0:T(8,128)(2,1)S(1)}, u32[]{:S(2)}, u32[]{:S(2)}) collective-permute-start(bf16[1,512,512]{2,1,0:T(8,128)(2,1)S(1)} %update.1.value_ref), channel_id=1, source_target_pairs={{0,16},{16,0},{1,17},{17,1},{2,18},{18,2},{3,19},{19,3},{4,20},{20... | collective-permute-start | bytes 1572872 | tf_op jit(solution)/shard_map/ppermute | solution.py:207

commit v6 on v5

--- a/solution.py
+++ b/solution.py
@@ -28,7 +28,10 @@
 
 GROUP = 8
 PARTNERS = (0, 7, 6, 5, 3, 4, 2, 1)
-BACK = (1, 2, 4, 3, 5, 6, 7)
+RELAY = 4
+LONE = (3, 7)
+TWICE = (2, 1)
+BLOCKS = (0, *[block for partner in TWICE for block in (partner, partner ^ RELAY)], *LONE, RELAY)
 
 
 def split(value):
@@ -102,17 +105,19 @@
 
 
 def update_kernel(gain, *refs):
-    chunks = refs[:GROUP]
-    gradient_ref, update_ref, mixed, cross = refs[GROUP:]
+    *arrays, gradient_ref, update_ref, mixed, cross = refs
     half = mixed.shape[0]
     rows = half // GROUP
-    for source, start in zip(chunks, block_starts(rows, (0, *BACK))):
-        at = 0
-        for target in (cross, mixed):
-            for lane in range(0, half, LANES):
-                target[pl.ds(start, rows), lane : lane + LANES] = source[at : at + rows, :]
-                at += rows
-    diagonal = jnp.concatenate([chunks[0][at + i : at + i + 1, :] for i in range(half // LANES)], axis=1)
+    starts = iter(block_starts(rows, BLOCKS))
+    length = arrays[0].shape[0]
+    for source in arrays:
+        for base in range(0, source.shape[0], length):
+            start, at = next(starts), base
+            for target in (cross, mixed):
+                for lane in range(0, half, LANES):
+                    target[pl.ds(start, rows), lane : lane + LANES] = source[at : at + rows, :]
+                    at += rows
+    diagonal = jnp.concatenate([source[at + i : at + i + 1, :] for i in range(half // LANES)], axis=1)
     row, column = grid_pair(half)
     on_diagonal = row == column
     packed = mixed[...]
@@ -177,12 +182,16 @@
     while step < size:
         owned = owned + swap(owned, step)
         step *= 2
-    gathered = [owned] + [swap(owned, partner) for partner in BACK]
+    relayed = swap(owned, RELAY)
+    lone = [swap(owned, partner) for partner in LONE]
+    pair = jnp.concatenate([owned, relayed])
+    twice = [swap(pair, partner) for partner in TWICE]
+    gathered = [owned, *twice, *lone, relayed]
     gain = update_gain * math.sqrt(max(FEATURES, OUTPUTS))
     update = pl.pallas_call(
         functools.partial(update_kernel, gain),
         out_shape=jax.ShapeDtypeStruct(gradient.shape, jnp.bfloat16),
-        in_specs=[vmem] * (GROUP + 1),
+        in_specs=[vmem] * (len(gathered) + 1),
         out_specs=vmem,
         scratch_shapes=[pltpu.VMEM((half, half), jnp.float32)] * 2,
         compiler_params=pltpu.CompilerParams(vmem_limit_bytes=UPDATE_VMEM),
@@ -209,7 +218,8 @@
 
 
 def solution(mesh):
+    def body(gradient):
+        return on_device(mesh, gradient)
+
     placed = (P("dp", "tensor", None),)
-    return jax.shard_map(
-        functools.partial(on_device, mesh), mesh=mesh, in_specs=placed, out_specs=P(None, "tensor", None), check_vma=False
-    )
+    return jax.shard_map(body, mesh=mesh, in_specs=placed, out_specs=P(None, "tensor", None), check_vma=False)

time: 45.2 us -> 46.6 us (1.031)
  waiting for transfers between devices: 10.6 us -> 14.4 us
  starting transfers between devices: 23.3 us -> 20.8 us
    ppermute x15 -> x13, waiting for transfers between devices: 9.49 us -> 13.4 us  [swap(): lax.ppermute(value, 'tensor', [(i, i ^ partner) for i in range(size)])]
    ppermute x15 -> x13, starting transfers between devices: 23.2 us -> 20.7 us  [swap(): lax.ppermute(value, 'tensor', [(i, i ^ partner) for i in range(size)])]
  transfers between devices with their start and end apart: 16 -> 14, of which waited for: 11 -> 10; matrix products, arithmetic and copies ran while one was open for 0% -> 0% of each run, Pallas kernels for 2% -> 2%
where the time goes in v6:
time: 46.6 us; the launch traced here: 46.5 us
  starting transfers between devices  20.8 us (45%)
  waiting for transfers between devices  14.4 us (31%)
  Pallas kernels  9.91 us (21%)
  local copies, waits for them, and re-layouts  1.23 us (3%)
    ppermute x13, starting transfers between devices, swap(): lax.ppermute(value, 'tensor', [(i, i ^ partner) for i in range(size)])  20.7 us
    ppermute x13, waiting for transfers between devices, swap(): lax.ppermute(value, 'tensor', [(i, i ^ partner) for i in range(size)])  13.4 us
    pallas_call x1, Pallas kernels, on_device(): pl.pallas_call(functools.partial(update_kernel, gain), out_shape=jax.Shap...  7.44 us
    pallas_call x2, Pallas kernels, place(): pl.pallas_call(functools.partial(place_kernel, flipped), out_shape=jax.Sh...  1.61 us
    unnamed x4, local copies, waits for them, and re-layouts  1.23 us
    ppermute x1, waiting for transfers between devices, on_device(): other = lax.ppermute(update, 'dp', [(0, 1), (1, 0)])  1.08 us
  transfers between devices with their start and end apart: 14, of which 10 were waited for; matrix products, arithmetic and copies ran while one was open for 0% of the time, Pallas kernels for 2%

profile of v6, /device:TPU:0, one launch (start us, length us, event | category | flops | bytes accessed | tf_op | source)
XLA Modules:
  0.0 46.5 jit_solution(6707013579919005969)
XLA Ops:
  0.0 1.2 %copy-done = f32[1,512,512]{2,1,0:T(8,128)S(1)} copy-done((f32[1,512,512]{2,1,0:T(8,128)S(1)}, f32[1,512,512]{2,1,0:T(8,128)}, u32[]{:S(2)}) %copy-start) | copy-done | bytes 1048600
  1.2 0.9 %gram.1 = (f32[136,128]{1,0:T(8,128)S(1)}, f32[136,128]{1,0:T(8,128)S(1)}, f32[136,128]{1,0:T(8,128)S(1)}, f32[136,128]{1,0:T(8,128)S(1)}, f32[136,128]{1,0:T(8,...) custom-call(f32[1,512,512]{2,1,0:T(8,128)S(1)} %copy-done), custom_call_target="tpu_custom_call" | custom-call | tf_op jit(solution)/shard_map/gram/pallas_call | solution.py:171
  2.1 5.0 %collective-permute-start = (f32[136,128]{1,0:T(8,128)S(1)}, f32[136,128]{1,0:T(8,128)S(1)}, u32[]{:S(2)}, u32[]{:S(2)}) collective-permute-start(f32[136,128]{1,0:T(8,128)S(1)} %get-tuple-element.14), channel_id=1, source_target_pairs={{0,7},{1,6},{2,5},{3,4},{4,3},{5,2},{6,1},{7,0},{8,15},{9,14},{10,... | collective-permute-start | bytes 208904 | tf_op jit(solution)/shard_map/ppermute | solution.py:169
  7.5 1.5 %collective-permute-start.2 = (f32[136,128]{1,0:T(8,128)S(1)}, f32[136,128]{1,0:T(8,128)S(1)}, u32[]{:S(2)}, u32[]{:S(2)}) collective-permute-start(f32[136,128]{1,0:T(8,128)S(1)} %get-tuple-element.16), channel_id=1, source_target_pairs={{0,5},{1,4},{2,7},{3,6},{4,1},{5,0},{6,3},{7,2},{8,13},{9,12},{10,... | collective-permute-start | bytes 208904 | tf_op jit(solution)/shard_map/ppermute | solution.py:169
  9.0 2.5 %collective-permute-start.3 = (f32[136,128]{1,0:T(8,128)S(1)}, f32[136,128]{1,0:T(8,128)S(1)}, u32[]{:S(2)}, u32[]{:S(2)}) collective-permute-start(f32[136,128]{1,0:T(8,128)S(1)} %get-tuple-element.17), channel_id=1, source_target_pairs={{0,3},{1,2},{2,1},{3,0},{4,7},{5,6},{6,5},{7,4},{8,11},{9,10},{10,... | collective-permute-start | bytes 208904 | tf_op jit(solution)/shard_map/ppermute | solution.py:169
  11.9 0.5 %collective-permute-start.5 = (f32[136,128]{1,0:T(8,128)S(1)}, f32[136,128]{1,0:T(8,128)S(1)}, u32[]{:S(2)}, u32[]{:S(2)}) collective-permute-start(f32[136,128]{1,0:T(8,128)S(1)} %get-tuple-element.19), channel_id=1, source_target_pairs={{0,2},{1,3},{2,0},{3,1},{4,6},{5,7},{6,4},{7,5},{8,10},{9,11},{10,... | collective-permute-start | bytes 208904 | tf_op jit(solution)/shard_map/ppermute | solution.py:169
  12.7 0.8 %collective-permute-start.6 = (f32[136,128]{1,0:T(8,128)S(1)}, f32[136,128]{1,0:T(8,128)S(1)}, u32[]{:S(2)}, u32[]{:S(2)}) collective-permute-start(f32[136,128]{1,0:T(8,128)S(1)} %get-tuple-element.20), channel_id=1, source_target_pairs={{0,1},{1,0},{2,3},{3,2},{4,5},{5,4},{6,7},{7,6},{8,9},{9,8},{10,11... | collective-permute-start | bytes 208904 | tf_op jit(solution)/shard_map/ppermute | solution.py:169
  13.5 1.6 %collective-permute-done.3 = f32[136,128]{1,0:T(8,128)S(1)} collective-permute-done((f32[136,128]{1,0:T(8,128)S(1)}, f32[136,128]{1,0:T(8,128)S(1)}, u32[]{:S(2)}, u32[]{:S(2)}) %collective-permute-start.3) | collective-permute-done | bytes 69664 | tf_op jit(solution)/shard_map/ppermute | solution.py:169
  15.1 0.7 %collective-permute-done.4 = f32[136,128]{1,0:T(8,128)S(1)} collective-permute-done((f32[136,128]{1,0:T(8,128)S(1)}, f32[136,128]{1,0:T(8,128)S(1)}, u32[]{:S(2)}, u32[]{:S(2)}) %collective-permute-start.4) | collective-permute-done | bytes 69664 | tf_op jit(solution)/shard_map/ppermute | solution.py:169
  16.2 0.8 %collective-permute-done.6 = f32[136,128]{1,0:T(8,128)S(1)} collective-permute-done((f32[136,128]{1,0:T(8,128)S(1)}, f32[136,128]{1,0:T(8,128)S(1)}, u32[]{:S(2)}, u32[]{:S(2)}) %collective-permute-start.6) | collective-permute-done | bytes 69664 | tf_op jit(solution)/shard_map/ppermute | solution.py:169
  17.1 2.6 %collective-permute-start.7 = (f32[136,128]{1,0:T(8,128)S(1)}, f32[136,128]{1,0:T(8,128)S(1)}, u32[]{:S(2)}, u32[]{:S(2)}) collective-permute-start(f32[136,128]{1,0:T(8,128)S(1)} %add_add_fusion), channel_id=1, source_target_pairs={{0,8},{1,9},{2,10},{3,11},{4,12},{5,13},{6,14},{7,15},{8,0},{9,1},... | collective-permute-start | bytes 208904 | tf_op jit(solution)/shard_map/ppermute | solution.py:169
  19.7 2.7 %collective-permute-done.7 = f32[136,128]{1,0:T(8,128)S(1)} collective-permute-done((f32[136,128]{1,0:T(8,128)S(1)}, f32[136,128]{1,0:T(8,128)S(1)}, u32[]{:S(2)}, u32[]{:S(2)}) %collective-permute-start.7) | collective-permute-done | bytes 69664 | tf_op jit(solution)/shard_map/ppermute | solution.py:169
  22.5 1.3 %collective-permute-start.8 = (f32[136,128]{1,0:T(8,128)S(1)}, f32[136,128]{1,0:T(8,128)S(1)}, u32[]{:S(2)}, u32[]{:S(2)}) collective-permute-start(f32[136,128]{1,0:T(8,128)S(1)} %add.31.refs_0_), channel_id=1, source_target_pairs={{0,4},{1,5},{2,6},{3,7},{4,0},{5,1},{6,2},{7,3},{8,12},{9,13},{10,... | collective-permute-start | bytes 208904 | tf_op jit(solution)/shard_map/ppermute | solution.py:169
  23.7 3.1 %collective-permute-done.8.refs_5_ = f32[136,128]{1,0:T(8,128)S(1)} collective-permute-done((f32[136,128]{1,0:T(8,128)S(1)}, f32[136,128]{1,0:T(8,128)S(1)}, u32[]{:S(2)}, u32[]{:S(2)}) %collective-permute-start.8) | collective-permute-done | bytes 69664 | tf_op jit(solution)/shard_map/ppermute | solution.py:169
  26.9 0.8 %collective-permute-start.10 = (f32[272,128]{1,0:T(8,128)S(1)}, f32[272,128]{1,0:T(8,128)S(1)}, u32[]{:S(2)}, u32[]{:S(2)}) collective-permute-start(f32[272,128]{1,0:T(8,128)S(1)} %pad_maximum_fusion), channel_id=1, source_target_pairs={{0,1},{1,0},{2,3},{3,2},{4,5},{5,4},{6,7},{7,6},{8,9},{9,8},{10,11... | collective-permute-start | bytes 417800 | tf_op jit(solution)/shard_map/ppermute | solution.py:169
  27.6 1.0 %collective-permute-start.9 = (f32[272,128]{1,0:T(8,128)S(1)}, f32[272,128]{1,0:T(8,128)S(1)}, u32[]{:S(2)}, u32[]{:S(2)}) collective-permute-start(f32[272,128]{1,0:T(8,128)S(1)} %pad_maximum_fusion), channel_id=1, source_target_pairs={{0,2},{1,3},{2,0},{3,1},{4,6},{5,7},{6,4},{7,5},{8,10},{9,11},{10,... | collective-permute-start | bytes 417800 | tf_op jit(solution)/shard_map/ppermute | solution.py:169
  28.6 2.4 %collective-permute-start.12 = (f32[136,128]{1,0:T(8,128)S(1)}, f32[136,128]{1,0:T(8,128)S(1)}, u32[]{:S(2)}, u32[]{:S(2)}) collective-permute-start(f32[136,128]{1,0:T(8,128)S(1)} %add.31.refs_0_), channel_id=1, source_target_pairs={{0,7},{1,6},{2,5},{3,4},{4,3},{5,2},{6,1},{7,0},{8,15},{9,14},{10,... | collective-permute-start | bytes 208904 | tf_op jit(solution)/shard_map/ppermute | solution.py:169
  31.0 1.5 %collective-permute-start.11 = (f32[136,128]{1,0:T(8,128)S(1)}, f32[136,128]{1,0:T(8,128)S(1)}, u32[]{:S(2)}, u32[]{:S(2)}) collective-permute-start(f32[136,128]{1,0:T(8,128)S(1)} %add.31.refs_0_), channel_id=1, source_target_pairs={{0,3},{1,2},{2,1},{3,0},{4,7},{5,6},{6,5},{7,4},{8,11},{9,10},{10,... | collective-permute-start | bytes 208904 | tf_op jit(solution)/shard_map/ppermute | solution.py:169
  32.5 2.2 %collective-permute-done.12.refs_4_ = f32[136,128]{1,0:T(8,128)S(1)} collective-permute-done((f32[136,128]{1,0:T(8,128)S(1)}, f32[136,128]{1,0:T(8,128)S(1)}, u32[]{:S(2)}, u32[]{:S(2)}) %collective-permute-start.12) | collective-permute-done | bytes 69664 | tf_op jit(solution)/shard_map/ppermute | solution.py:169
  34.7 1.5 %collective-permute-done.11.refs_3_ = f32[136,128]{1,0:T(8,128)S(1)} collective-permute-done((f32[136,128]{1,0:T(8,128)S(1)}, f32[136,128]{1,0:T(8,128)S(1)}, u32[]{:S(2)}, u32[]{:S(2)}) %collective-permute-start.11) | collective-permute-done | bytes 69664 | tf_op jit(solution)/shard_map/ppermute | solution.py:169
  36.3 7.4 %update.1.value_ref = bf16[1,512,512]{2,1,0:T(8,128)(2,1)S(1)} custom-call(f32[136,128]{1,0:T(8,128)S(1)} %add.31.refs_0_, f32[272,128]{1,0:T(8,128)S(1)} %collective-permute-done.9.refs_1_, f32[272,128]{1,0:T(8,128)S(1)} %collective-permute-done.10.refs_2_, f32[136,128]{1,0:T(8,128)S(1)} %collective-permute-done.11.refs_3_, ...), custom_call_target="tpu_custom_call" | custom-call | tf_op jit(solution)/shard_map/update/pallas_call | solution.py:191
  43.8 0.8 %place.2.refs_0_ = bf16[2,512,512]{2,1,0:T(8,128)(2,1)} custom-call(bf16[1,512,512]{2,1,0:T(8,128)(2,1)S(1)} %update.1.value_ref), custom_call_target="tpu_custom_call" | custom-call | flops 1048576 | bytes 524288 | tf_op jit(solution)/shard_map/place/pallas_call | solution.py:204
  44.6 1.1 %collective-permute-done.13.value_ref = bf16[1,512,512]{2,1,0:T(8,128)(2,1)S(1)} collective-permute-done((bf16[1,512,512]{2,1,0:T(8,128)(2,1)S(1)}, bf16[1,512,512]{2,1,0:T(8,128)(2,1)S(1)}, u32[]{:S(2)}, u32[]{:S(2)}) %collective-permute-start.13) | collective-permute-done | bytes 524320 | tf_op jit(solution)/shard_map/ppermute | solution.py:216
  45.7 0.8 %place.3 = bf16[2,512,512]{2,1,0:T(8,128)(2,1)} custom-call(bf16[1,512,512]{2,1,0:T(8,128)(2,1)S(1)} %collective-permute-done.13.value_ref, bf16[2,512,512]{2,1,0:T(8,128)(2,1)} %place.2.refs_0_), custom_call_target="tpu_custom_call", output_to_operand_aliasing={{}: (1, {})} | custom-call | flops 1048576 | bytes 524288 | tf_op jit(solution)/shard_map/place/pallas_call | solution.py:204
  (15 shorter events, 1.7 us)
Async XLA Ops:
  0.0 1.2 %copy-start = (f32[1,512,512]{2,1,0:T(8,128)S(1)}, f32[1,512,512]{2,1,0:T(8,128)}, u32[]{:S(2)}) copy-start(f32[1,512,512]{2,1,0:T(8,128)} %refs_6_.1) | copy-start | bytes 3145732
  1.2 35.0 %copy-start.1 = (f32[1,512,512]{2,1,0:T(8,128)S(1)}, f32[1,512,512]{2,1,0:T(8,128)}, u32[]{:S(2)}) copy-start(f32[1,512,512]{2,1,0:T(8,128)} %refs_6_.1) | copy-start | bytes 3145732
  2.1 9.8 %collective-permute-start = (f32[136,128]{1,0:T(8,128)S(1)}, f32[136,128]{1,0:T(8,128)S(1)}, u32[]{:S(2)}, u32[]{:S(2)}) collective-permute-start(f32[136,128]{1,0:T(8,128)S(1)} %get-tuple-element.14), channel_id=1, source_target_pairs={{0,7},{1,6},{2,5},{3,4},{4,3},{5,2},{6,1},{7,0},{8,15},{9,14},{10,... | collective-permute-start | bytes 208904 | tf_op jit(solution)/shard_map/ppermute | solution.py:169
  7.1 5.6 %collective-permute-start.1 = (f32[136,128]{1,0:T(8,128)S(1)}, f32[136,128]{1,0:T(8,128)S(1)}, u32[]{:S(2)}, u32[]{:S(2)}) collective-permute-start(f32[136,128]{1,0:T(8,128)S(1)} %get-tuple-element.15), channel_id=1, source_target_pairs={{0,6},{1,7},{2,4},{3,5},{4,2},{5,3},{6,0},{7,1},{8,14},{9,15},{10,... | collective-permute-start | bytes 208904 | tf_op jit(solution)/shard_map/ppermute | solution.py:169
  7.5 6.0 %collective-permute-start.2 = (f32[136,128]{1,0:T(8,128)S(1)}, f32[136,128]{1,0:T(8,128)S(1)}, u32[]{:S(2)}, u32[]{:S(2)}) collective-permute-start(f32[136,128]{1,0:T(8,128)S(1)} %get-tuple-element.16), channel_id=1, source_target_pairs={{0,5},{1,4},{2,7},{3,6},{4,1},{5,0},{6,3},{7,2},{8,13},{9,12},{10,... | collective-permute-start | bytes 208904 | tf_op jit(solution)/shard_map/ppermute | solution.py:169
  9.0 6.1 %collective-permute-start.3 = (f32[136,128]{1,0:T(8,128)S(1)}, f32[136,128]{1,0:T(8,128)S(1)}, u32[]{:S(2)}, u32[]{:S(2)}) collective-permute-start(f32[136,128]{1,0:T(8,128)S(1)} %get-tuple-element.17), channel_id=1, source_target_pairs={{0,3},{1,2},{2,1},{3,0},{4,7},{5,6},{6,5},{7,4},{8,11},{9,10},{10,... | collective-permute-start | bytes 208904 | tf_op jit(solution)/shard_map/ppermute | solution.py:169
  11.5 4.3 %collective-permute-start.4 = (f32[136,128]{1,0:T(8,128)S(1)}, f32[136,128]{1,0:T(8,128)S(1)}, u32[]{:S(2)}, u32[]{:S(2)}) collective-permute-start(f32[136,128]{1,0:T(8,128)S(1)} %get-tuple-element.18), channel_id=1, source_target_pairs={{0,4},{1,5},{2,6},{3,7},{4,0},{5,1},{6,2},{7,3},{8,12},{9,13},{10,... | collective-permute-start | bytes 208904 | tf_op jit(solution)/shard_map/ppermute | solution.py:169
  11.9 4.3 %collective-permute-start.5 = (f32[136,128]{1,0:T(8,128)S(1)}, f32[136,128]{1,0:T(8,128)S(1)}, u32[]{:S(2)}, u32[]{:S(2)}) collective-permute-start(f32[136,128]{1,0:T(8,128)S(1)} %get-tuple-element.19), channel_id=1, source_target_pairs={{0,2},{1,3},{2,0},{3,1},{4,6},{5,7},{6,4},{7,5},{8,10},{9,11},{10,... | collective-permute-start | bytes 208904 | tf_op jit(solution)/shard_map/ppermute | solution.py:169
  12.7 4.3 %collective-permute-start.6 = (f32[136,128]{1,0:T(8,128)S(1)}, f32[136,128]{1,0:T(8,128)S(1)}, u32[]{:S(2)}, u32[]{:S(2)}) collective-permute-start(f32[136,128]{1,0:T(8,128)S(1)} %get-tuple-element.20), channel_id=1, source_target_pairs={{0,1},{1,0},{2,3},{3,2},{4,5},{5,4},{6,7},{7,6},{8,9},{9,8},{10,11... | collective-permute-start | bytes 208904 | tf_op jit(solution)/shard_map/ppermute | solution.py:169
  17.1 5.4 %collective-permute-start.7 = (f32[136,128]{1,0:T(8,128)S(1)}, f32[136,128]{1,0:T(8,128)S(1)}, u32[]{:S(2)}, u32[]{:S(2)}) collective-permute-start(f32[136,128]{1,0:T(8,128)S(1)} %add_add_fusion), channel_id=1, source_target_pairs={{0,8},{1,9},{2,10},{3,11},{4,12},{5,13},{6,14},{7,15},{8,0},{9,1},... | collective-permute-start | bytes 208904 | tf_op jit(solution)/shard_map/ppermute | solution.py:169
  22.5 4.4 %collective-permute-start.8 = (f32[136,128]{1,0:T(8,128)S(1)}, f32[136,128]{1,0:T(8,128)S(1)}, u32[]{:S(2)}, u32[]{:S(2)}) collective-permute-start(f32[136,128]{1,0:T(8,128)S(1)} %add.31.refs_0_), channel_id=1, source_target_pairs={{0,4},{1,5},{2,6},{3,7},{4,0},{5,1},{6,2},{7,3},{8,12},{9,13},{10,... | collective-permute-start | bytes 208904 | tf_op jit(solution)/shard_map/ppermute | solution.py:169
  26.9 9.4 %collective-permute-start.10 = (f32[272,128]{1,0:T(8,128)S(1)}, f32[272,128]{1,0:T(8,128)S(1)}, u32[]{:S(2)}, u32[]{:S(2)}) collective-permute-start(f32[272,128]{1,0:T(8,128)S(1)} %pad_maximum_fusion), channel_id=1, source_target_pairs={{0,1},{1,0},{2,3},{3,2},{4,5},{5,4},{6,7},{7,6},{8,9},{9,8},{10,11... | collective-permute-start | bytes 417800 | tf_op jit(solution)/shard_map/ppermute | solution.py:169
  27.6 8.7 %collective-permute-start.9 = (f32[272,128]{1,0:T(8,128)S(1)}, f32[272,128]{1,0:T(8,128)S(1)}, u32[]{:S(2)}, u32[]{:S(2)}) collective-permute-start(f32[272,128]{1,0:T(8,128)S(1)} %pad_maximum_fusion), channel_id=1, source_target_pairs={{0,2},{1,3},{2,0},{3,1},{4,6},{5,7},{6,4},{7,5},{8,10},{9,11},{10,... | collective-permute-start | bytes 417800 | tf_op jit(solution)/shard_map/ppermute | solution.py:169
  28.6 6.1 %collective-permute-start.12 = (f32[136,128]{1,0:T(8,128)S(1)}, f32[136,128]{1,0:T(8,128)S(1)}, u32[]{:S(2)}, u32[]{:S(2)}) collective-permute-start(f32[136,128]{1,0:T(8,128)S(1)} %add.31.refs_0_), channel_id=1, source_target_pairs={{0,7},{1,6},{2,5},{3,4},{4,3},{5,2},{6,1},{7,0},{8,15},{9,14},{10,... | collective-permute-start | bytes 208904 | tf_op jit(solution)/shard_map/ppermute | solution.py:169
  31.0 5.2 %collective-permute-start.11 = (f32[136,128]{1,0:T(8,128)S(1)}, f32[136,128]{1,0:T(8,128)S(1)}, u32[]{:S(2)}, u32[]{:S(2)}) collective-permute-start(f32[136,128]{1,0:T(8,128)S(1)} %add.31.refs_0_), channel_id=1, source_target_pairs={{0,3},{1,2},{2,1},{3,0},{4,7},{5,6},{6,5},{7,4},{8,11},{9,10},{10,... | collective-permute-start | bytes 208904 | tf_op jit(solution)/shard_map/ppermute | solution.py:169
  43.7 2.0 %collective-permute-start.13 = (bf16[1,512,512]{2,1,0:T(8,128)(2,1)S(1)}, bf16[1,512,512]{2,1,0:T(8,128)(2,1)S(1)}, u32[]{:S(2)}, u32[]{:S(2)}) collective-permute-start(bf16[1,512,512]{2,1,0:T(8,128)(2,1)S(1)} %update.1.value_ref), channel_id=1, source_target_pairs={{0,16},{16,0},{1,17},{17,1},{2,18},{18,2},{3,19},{19,3},{4,20},{20... | collective-permute-start | bytes 1572872 | tf_op jit(solution)/shard_map/ppermute | solution.py:216

commit v7 on v6

--- a/solution.py
+++ b/solution.py
@@ -27,11 +27,13 @@
 
 
 GROUP = 8
-PARTNERS = (0, 7, 6, 5, 3, 4, 2, 1)
 RELAY = 4
 LONE = (3, 7)
 TWICE = (2, 1)
 BLOCKS = (0, *[block for partner in TWICE for block in (partner, partner ^ RELAY)], *LONE, RELAY)
+OUT_TWICE = (2,)
+OUT_LONE = (7, 5, 3, 1)
+OUT_BLOCKS = (0, *[block for partner in OUT_TWICE for block in (partner, partner ^ RELAY)], *OUT_LONE, RELAY)
 
 
 def split(value):
@@ -75,7 +77,7 @@
 
 
 def gram_kernel(gradient_ref, *refs):
-    chunks, (mixed, cross) = refs[:GROUP], refs[GROUP:]
+    *arrays, mixed, cross = refs
     half = mixed.shape[0]
     rows = half // GROUP
     high, low = split(gradient_ref[0])
@@ -100,8 +102,11 @@
                 at += rows
         out[at : at + SUBLANES, :] = tile
 
-    for out, start in zip(chunks, block_starts(rows, PARTNERS)):
-        write(out, 0, start)
+    starts = iter(block_starts(rows, OUT_BLOCKS))
+    length = arrays[0].shape[0]
+    for out in arrays:
+        for base in range(0, out.shape[0], length):
+            write(out, base, next(starts))
 
 
 def update_kernel(gain, *refs):
@@ -168,16 +173,22 @@
     def swap(value, partner):
         return lax.ppermute(value, "tensor", [(i, i ^ partner) for i in range(size)])
 
-    chunks = pl.pallas_call(
+    double = jax.ShapeDtypeStruct((2 * length, LANES), jnp.float32)
+    shapes = [chunk] + [double] * len(OUT_TWICE) + [chunk] * (len(OUT_LONE) + 1)
+    keep, *chunks, relayed = pl.pallas_call(
         gram_kernel,
-        out_shape=[chunk] * GROUP,
+        out_shape=shapes,
         in_specs=[vmem],
-        out_specs=[vmem] * GROUP,
+        out_specs=[vmem] * len(shapes),
         scratch_shapes=[pltpu.VMEM((half, half), jnp.float32)] * 2,
         compiler_params=pltpu.CompilerParams(vmem_limit_bytes=GRAM_VMEM),
         name="gram",
     )(gradient)
-    owned = functools.reduce(jnp.add, [swap(value, k) for value, k in zip(chunks[1:], PARTNERS[1:])], chunks[0])
+    arrived = [swap(value, partner) for value, partner in zip(chunks, OUT_TWICE + OUT_LONE)]
+    twice, lone = arrived[: len(OUT_TWICE)], arrived[len(OUT_TWICE) :]
+    relayed = functools.reduce(jnp.add, [value[length:] for value in twice], relayed)
+    owned = functools.reduce(jnp.add, [value[:length] for value in twice] + lone, keep)
+    owned = owned + swap(relayed, RELAY)
     step = GROUP
     while step < size:
         owned = owned + swap(owned, step)

time: 46.6 us -> 45.3 us (0.972)
  waiting for transfers between devices: 14.4 us -> 12.4 us
  starting transfers between devices: 20.8 us -> 21.5 us
    ppermute x13 -> x12, waiting for transfers between devices: 13.4 us -> 11.3 us  [swap(): lax.ppermute(value, 'tensor', [(i, i ^ partner) for i in range(size)])]
    ppermute x13 -> x12, starting transfers between devices: 20.7 us -> 21.4 us  [swap(): lax.ppermute(value, 'tensor', [(i, i ^ partner) for i in range(size)])]
  transfers between devices with their start and end apart: 14 -> 13, of which waited for: 10 -> 9; matrix products, arithmetic and copies ran while one was open for 0% -> 0% of each run, Pallas kernels for 2% -> 2%
where the time goes in v7:
time: 45.3 us; the launch traced here: 45.1 us
  starting transfers between devices  21.5 us (47%)
  waiting for transfers between devices  12.4 us (27%)
  Pallas kernels  9.91 us (22%)
  local copies, waits for them, and re-layouts  1.23 us (3%)
    ppermute x12, starting transfers between devices, swap(): lax.ppermute(value, 'tensor', [(i, i ^ partner) for i in range(size)])  21.4 us
    ppermute x12, waiting for transfers between devices, swap(): lax.ppermute(value, 'tensor', [(i, i ^ partner) for i in range(size)])  11.3 us
    pallas_call x1, Pallas kernels, on_device(): pl.pallas_call(functools.partial(update_kernel, gain), out_shape=jax.Shap...  7.44 us
    pallas_call x2, Pallas kernels, place(): pl.pallas_call(functools.partial(place_kernel, flipped), out_shape=jax.Sh...  1.61 us
    unnamed x4, local copies, waits for them, and re-layouts  1.23 us
    ppermute x1, waiting for transfers between devices, on_device(): other = lax.ppermute(update, 'dp', [(0, 1), (1, 0)])  1.08 us
  transfers between devices with their start and end apart: 13, of which 9 were waited for; matrix products, arithmetic and copies ran while one was open for 0% of the time, Pallas kernels for 2%

profile of v7, /device:TPU:0, one launch (start us, length us, event | category | flops | bytes accessed | tf_op | source)
XLA Modules:
  0.0 45.1 jit_solution(7198308563875226247)
XLA Ops:
  0.0 1.2 %copy-done = f32[1,512,512]{2,1,0:T(8,128)S(1)} copy-done((f32[1,512,512]{2,1,0:T(8,128)S(1)}, f32[1,512,512]{2,1,0:T(8,128)}, u32[]{:S(2)}) %copy-start) | copy-done | bytes 1048600
  1.2 0.9 %gram.1 = (f32[136,128]{1,0:T(8,128)S(1)}, f32[272,128]{1,0:T(8,128)S(1)}, f32[136,128]{1,0:T(8,128)S(1)}, f32[136,128]{1,0:T(8,128)S(1)}, f32[136,128]{1,0:T(8,...) custom-call(f32[1,512,512]{2,1,0:T(8,128)S(1)} %copy-done), custom_call_target="tpu_custom_call" | custom-call | tf_op jit(solution)/shard_map/gram/pallas_call | solution.py:178
  2.1 3.1 %collective-permute-start = (f32[272,128]{1,0:T(8,128)S(1)}, f32[272,128]{1,0:T(8,128)S(1)}, u32[]{:S(2)}, u32[]{:S(2)}) collective-permute-start(f32[272,128]{1,0:T(8,128)S(1)} %get-tuple-element.13), channel_id=1, source_target_pairs={{0,2},{1,3},{2,0},{3,1},{4,6},{5,7},{6,4},{7,5},{8,10},{9,11},{10,... | collective-permute-start | bytes 417800 | tf_op jit(solution)/shard_map/ppermute | solution.py:174
  5.2 2.4 %collective-permute-start.1 = (f32[136,128]{1,0:T(8,128)S(1)}, f32[136,128]{1,0:T(8,128)S(1)}, u32[]{:S(2)}, u32[]{:S(2)}) collective-permute-start(f32[136,128]{1,0:T(8,128)S(1)} %get-tuple-element.14), channel_id=1, source_target_pairs={{0,7},{1,6},{2,5},{3,4},{4,3},{5,2},{6,1},{7,0},{8,15},{9,14},{10,... | collective-permute-start | bytes 208904 | tf_op jit(solution)/shard_map/ppermute | solution.py:174
  7.7 2.8 %collective-permute-start.3 = (f32[136,128]{1,0:T(8,128)S(1)}, f32[136,128]{1,0:T(8,128)S(1)}, u32[]{:S(2)}, u32[]{:S(2)}) collective-permute-start(f32[136,128]{1,0:T(8,128)S(1)} %get-tuple-element.16), channel_id=1, source_target_pairs={{0,3},{1,2},{2,1},{3,0},{4,7},{5,6},{6,5},{7,4},{8,11},{9,10},{10,... | collective-permute-start | bytes 208904 | tf_op jit(solution)/shard_map/ppermute | solution.py:174
  10.5 0.5 %collective-permute-start.4 = (f32[136,128]{1,0:T(8,128)S(1)}, f32[136,128]{1,0:T(8,128)S(1)}, u32[]{:S(2)}, u32[]{:S(2)}) collective-permute-start(f32[136,128]{1,0:T(8,128)S(1)} %get-tuple-element.17), channel_id=1, source_target_pairs={{0,1},{1,0},{2,3},{3,2},{4,5},{5,4},{6,7},{7,6},{8,9},{9,8},{10,11... | collective-permute-start | bytes 208904 | tf_op jit(solution)/shard_map/ppermute | solution.py:174
  11.0 1.6 %collective-permute-start.5 = (f32[136,128]{1,0:T(8,128)S(1)}, f32[136,128]{1,0:T(8,128)S(1)}, u32[]{:S(2)}, u32[]{:S(2)}) collective-permute-start(f32[136,128]{1,0:T(8,128)S(1)} %slice_add_fusion), channel_id=1, source_target_pairs={{0,4},{1,5},{2,6},{3,7},{4,0},{5,1},{6,2},{7,3},{8,12},{9,13},{10,... | collective-permute-start | bytes 208904 | tf_op jit(solution)/shard_map/ppermute | solution.py:174
  12.9 1.3 %collective-permute-done.3 = f32[136,128]{1,0:T(8,128)S(1)} collective-permute-done((f32[136,128]{1,0:T(8,128)S(1)}, f32[136,128]{1,0:T(8,128)S(1)}, u32[]{:S(2)}, u32[]{:S(2)}) %collective-permute-start.3) | collective-permute-done | bytes 69664 | tf_op jit(solution)/shard_map/ppermute | solution.py:174
  14.2 0.6 %collective-permute-done.4 = f32[136,128]{1,0:T(8,128)S(1)} collective-permute-done((f32[136,128]{1,0:T(8,128)S(1)}, f32[136,128]{1,0:T(8,128)S(1)}, u32[]{:S(2)}, u32[]{:S(2)}) %collective-permute-start.4) | collective-permute-done | bytes 69664 | tf_op jit(solution)/shard_map/ppermute | solution.py:174
  14.8 0.6 %collective-permute-done.5 = f32[136,128]{1,0:T(8,128)S(1)} collective-permute-done((f32[136,128]{1,0:T(8,128)S(1)}, f32[136,128]{1,0:T(8,128)S(1)}, u32[]{:S(2)}, u32[]{:S(2)}) %collective-permute-start.5) | collective-permute-done | bytes 69664 | tf_op jit(solution)/shard_map/ppermute | solution.py:174
  15.4 2.6 %collective-permute-start.6 = (f32[136,128]{1,0:T(8,128)S(1)}, f32[136,128]{1,0:T(8,128)S(1)}, u32[]{:S(2)}, u32[]{:S(2)}) collective-permute-start(f32[136,128]{1,0:T(8,128)S(1)} %fusion.4), channel_id=1, source_target_pairs={{0,8},{1,9},{2,10},{3,11},{4,12},{5,13},{6,14},{7,15},{8,0},{9,1},... | collective-permute-start | bytes 208904 | tf_op jit(solution)/shard_map/ppermute | solution.py:174
  18.1 2.6 %collective-permute-done.6 = f32[136,128]{1,0:T(8,128)S(1)} collective-permute-done((f32[136,128]{1,0:T(8,128)S(1)}, f32[136,128]{1,0:T(8,128)S(1)}, u32[]{:S(2)}, u32[]{:S(2)}) %collective-permute-start.6) | collective-permute-done | bytes 69664 | tf_op jit(solution)/shard_map/ppermute | solution.py:174
  20.7 1.6 %collective-permute-start.7 = (f32[136,128]{1,0:T(8,128)S(1)}, f32[136,128]{1,0:T(8,128)S(1)}, u32[]{:S(2)}, u32[]{:S(2)}) collective-permute-start(f32[136,128]{1,0:T(8,128)S(1)} %add.31.refs_0_), channel_id=1, source_target_pairs={{0,4},{1,5},{2,6},{3,7},{4,0},{5,1},{6,2},{7,3},{8,12},{9,13},{10,... | collective-permute-start | bytes 208904 | tf_op jit(solution)/shard_map/ppermute | solution.py:174
  22.4 2.7 %collective-permute-done.7.refs_5_ = f32[136,128]{1,0:T(8,128)S(1)} collective-permute-done((f32[136,128]{1,0:T(8,128)S(1)}, f32[136,128]{1,0:T(8,128)S(1)}, u32[]{:S(2)}, u32[]{:S(2)}) %collective-permute-start.7) | collective-permute-done | bytes 69664 | tf_op jit(solution)/shard_map/ppermute | solution.py:174
  25.1 1.6 %collective-permute-start.9 = (f32[272,128]{1,0:T(8,128)S(1)}, f32[272,128]{1,0:T(8,128)S(1)}, u32[]{:S(2)}, u32[]{:S(2)}) collective-permute-start(f32[272,128]{1,0:T(8,128)S(1)} %pad_maximum_fusion), channel_id=1, source_target_pairs={{0,1},{1,0},{2,3},{3,2},{4,5},{5,4},{6,7},{7,6},{8,9},{9,8},{10,11... | collective-permute-start | bytes 417800 | tf_op jit(solution)/shard_map/ppermute | solution.py:174
  26.7 1.0 %collective-permute-start.8 = (f32[272,128]{1,0:T(8,128)S(1)}, f32[272,128]{1,0:T(8,128)S(1)}, u32[]{:S(2)}, u32[]{:S(2)}) collective-permute-start(f32[272,128]{1,0:T(8,128)S(1)} %pad_maximum_fusion), channel_id=1, source_target_pairs={{0,2},{1,3},{2,0},{3,1},{4,6},{5,7},{6,4},{7,5},{8,10},{9,11},{10,... | collective-permute-start | bytes 417800 | tf_op jit(solution)/shard_map/ppermute | solution.py:174
  27.6 2.0 %collective-permute-start.11 = (f32[136,128]{1,0:T(8,128)S(1)}, f32[136,128]{1,0:T(8,128)S(1)}, u32[]{:S(2)}, u32[]{:S(2)}) collective-permute-start(f32[136,128]{1,0:T(8,128)S(1)} %add.31.refs_0_), channel_id=1, source_target_pairs={{0,7},{1,6},{2,5},{3,4},{4,3},{5,2},{6,1},{7,0},{8,15},{9,14},{10,... | collective-permute-start | bytes 208904 | tf_op jit(solution)/shard_map/ppermute | solution.py:174
  29.7 2.0 %collective-permute-start.10 = (f32[136,128]{1,0:T(8,128)S(1)}, f32[136,128]{1,0:T(8,128)S(1)}, u32[]{:S(2)}, u32[]{:S(2)}) collective-permute-start(f32[136,128]{1,0:T(8,128)S(1)} %add.31.refs_0_), channel_id=1, source_target_pairs={{0,3},{1,2},{2,1},{3,0},{4,7},{5,6},{6,5},{7,4},{8,11},{9,10},{10,... | collective-permute-start | bytes 208904 | tf_op jit(solution)/shard_map/ppermute | solution.py:174
  31.7 2.1 %collective-permute-done.11.refs_4_ = f32[136,128]{1,0:T(8,128)S(1)} collective-permute-done((f32[136,128]{1,0:T(8,128)S(1)}, f32[136,128]{1,0:T(8,128)S(1)}, u32[]{:S(2)}, u32[]{:S(2)}) %collective-permute-start.11) | collective-permute-done | bytes 69664 | tf_op jit(solution)/shard_map/ppermute | solution.py:174
  33.7 1.1 %collective-permute-done.10.refs_3_ = f32[136,128]{1,0:T(8,128)S(1)} collective-permute-done((f32[136,128]{1,0:T(8,128)S(1)}, f32[136,128]{1,0:T(8,128)S(1)}, u32[]{:S(2)}, u32[]{:S(2)}) %collective-permute-start.10) | collective-permute-done | bytes 69664 | tf_op jit(solution)/shard_map/ppermute | solution.py:174
  34.9 7.4 %update.1.value_ref = bf16[1,512,512]{2,1,0:T(8,128)(2,1)S(1)} custom-call(f32[136,128]{1,0:T(8,128)S(1)} %add.31.refs_0_, f32[272,128]{1,0:T(8,128)S(1)} %collective-permute-done.8.refs_1_, f32[272,128]{1,0:T(8,128)S(1)} %collective-permute-done.9.refs_2_, f32[136,128]{1,0:T(8,128)S(1)} %collective-permute-done.10.refs_3_, ...), custom_call_target="tpu_custom_call" | custom-call | tf_op jit(solution)/shard_map/update/pallas_call | solution.py:202
  42.4 0.8 %place.2.refs_0_ = bf16[2,512,512]{2,1,0:T(8,128)(2,1)} custom-call(bf16[1,512,512]{2,1,0:T(8,128)(2,1)S(1)} %update.1.value_ref), custom_call_target="tpu_custom_call" | custom-call | flops 1048576 | bytes 524288 | tf_op jit(solution)/shard_map/place/pallas_call | solution.py:215
  43.2 1.1 %collective-permute-done.12.value_ref = bf16[1,512,512]{2,1,0:T(8,128)(2,1)S(1)} collective-permute-done((bf16[1,512,512]{2,1,0:T(8,128)(2,1)S(1)}, bf16[1,512,512]{2,1,0:T(8,128)(2,1)S(1)}, u32[]{:S(2)}, u32[]{:S(2)}) %collective-permute-start.12) | collective-permute-done | bytes 524320 | tf_op jit(solution)/shard_map/ppermute | solution.py:227
  44.3 0.8 %place.3 = bf16[2,512,512]{2,1,0:T(8,128)(2,1)} custom-call(bf16[1,512,512]{2,1,0:T(8,128)(2,1)S(1)} %collective-permute-done.12.value_ref, bf16[2,512,512]{2,1,0:T(8,128)(2,1)} %place.2.refs_0_), custom_call_target="tpu_custom_call", output_to_operand_aliasing={{}: (1, {})} | custom-call | flops 1048576 | bytes 524288 | tf_op jit(solution)/shard_map/place/pallas_call | solution.py:215
  (14 shorter events, 0.5 us)
Async XLA Ops:
  0.0 1.2 %copy-start = (f32[1,512,512]{2,1,0:T(8,128)S(1)}, f32[1,512,512]{2,1,0:T(8,128)}, u32[]{:S(2)}) copy-start(f32[1,512,512]{2,1,0:T(8,128)} %refs_6_.1) | copy-start | bytes 3145732
  1.2 33.7 %copy-start.1 = (f32[1,512,512]{2,1,0:T(8,128)S(1)}, f32[1,512,512]{2,1,0:T(8,128)}, u32[]{:S(2)}) copy-start(f32[1,512,512]{2,1,0:T(8,128)} %refs_6_.1) | copy-start | bytes 3145732
  2.1 8.9 %collective-permute-start = (f32[272,128]{1,0:T(8,128)S(1)}, f32[272,128]{1,0:T(8,128)S(1)}, u32[]{:S(2)}, u32[]{:S(2)}) collective-permute-start(f32[272,128]{1,0:T(8,128)S(1)} %get-tuple-element.13), channel_id=1, source_target_pairs={{0,2},{1,3},{2,0},{3,1},{4,6},{5,7},{6,4},{7,5},{8,10},{9,11},{10,... | collective-permute-start | bytes 417800 | tf_op jit(solution)/shard_map/ppermute | solution.py:174
  5.2 7.5 %collective-permute-start.1 = (f32[136,128]{1,0:T(8,128)S(1)}, f32[136,128]{1,0:T(8,128)S(1)}, u32[]{:S(2)}, u32[]{:S(2)}) collective-permute-start(f32[136,128]{1,0:T(8,128)S(1)} %get-tuple-element.14), channel_id=1, source_target_pairs={{0,7},{1,6},{2,5},{3,4},{4,3},{5,2},{6,1},{7,0},{8,15},{9,14},{10,... | collective-permute-start | bytes 208904 | tf_op jit(solution)/shard_map/ppermute | solution.py:174
  7.6 5.3 %collective-permute-start.2 = (f32[136,128]{1,0:T(8,128)S(1)}, f32[136,128]{1,0:T(8,128)S(1)}, u32[]{:S(2)}, u32[]{:S(2)}) collective-permute-start(f32[136,128]{1,0:T(8,128)S(1)} %get-tuple-element.15), channel_id=1, source_target_pairs={{0,5},{1,4},{2,7},{3,6},{4,1},{5,0},{6,3},{7,2},{8,13},{9,12},{10,... | collective-permute-start | bytes 208904 | tf_op jit(solution)/shard_map/ppermute | solution.py:174
  7.7 6.5 %collective-permute-start.3 = (f32[136,128]{1,0:T(8,128)S(1)}, f32[136,128]{1,0:T(8,128)S(1)}, u32[]{:S(2)}, u32[]{:S(2)}) collective-permute-start(f32[136,128]{1,0:T(8,128)S(1)} %get-tuple-element.16), channel_id=1, source_target_pairs={{0,3},{1,2},{2,1},{3,0},{4,7},{5,6},{6,5},{7,4},{8,11},{9,10},{10,... | collective-permute-start | bytes 208904 | tf_op jit(solution)/shard_map/ppermute | solution.py:174
  10.5 4.4 %collective-permute-start.4 = (f32[136,128]{1,0:T(8,128)S(1)}, f32[136,128]{1,0:T(8,128)S(1)}, u32[]{:S(2)}, u32[]{:S(2)}) collective-permute-start(f32[136,128]{1,0:T(8,128)S(1)} %get-tuple-element.17), channel_id=1, source_target_pairs={{0,1},{1,0},{2,3},{3,2},{4,5},{5,4},{6,7},{7,6},{8,9},{9,8},{10,11... | collective-permute-start | bytes 208904 | tf_op jit(solution)/shard_map/ppermute | solution.py:174
  11.0 4.4 %collective-permute-start.5 = (f32[136,128]{1,0:T(8,128)S(1)}, f32[136,128]{1,0:T(8,128)S(1)}, u32[]{:S(2)}, u32[]{:S(2)}) collective-permute-start(f32[136,128]{1,0:T(8,128)S(1)} %slice_add_fusion), channel_id=1, source_target_pairs={{0,4},{1,5},{2,6},{3,7},{4,0},{5,1},{6,2},{7,3},{8,12},{9,13},{10,... | collective-permute-start | bytes 208904 | tf_op jit(solution)/shard_map/ppermute | solution.py:174
  15.4 5.3 %collective-permute-start.6 = (f32[136,128]{1,0:T(8,128)S(1)}, f32[136,128]{1,0:T(8,128)S(1)}, u32[]{:S(2)}, u32[]{:S(2)}) collective-permute-start(f32[136,128]{1,0:T(8,128)S(1)} %fusion.4), channel_id=1, source_target_pairs={{0,8},{1,9},{2,10},{3,11},{4,12},{5,13},{6,14},{7,15},{8,0},{9,1},... | collective-permute-start | bytes 208904 | tf_op jit(solution)/shard_map/ppermute | solution.py:174
  20.7 4.4 %collective-permute-start.7 = (f32[136,128]{1,0:T(8,128)S(1)}, f32[136,128]{1,0:T(8,128)S(1)}, u32[]{:S(2)}, u32[]{:S(2)}) collective-permute-start(f32[136,128]{1,0:T(8,128)S(1)} %add.31.refs_0_), channel_id=1, source_target_pairs={{0,4},{1,5},{2,6},{3,7},{4,0},{5,1},{6,2},{7,3},{8,12},{9,13},{10,... | collective-permute-start | bytes 208904 | tf_op jit(solution)/shard_map/ppermute | solution.py:174
  25.1 9.8 %collective-permute-start.9 = (f32[272,128]{1,0:T(8,128)S(1)}, f32[272,128]{1,0:T(8,128)S(1)}, u32[]{:S(2)}, u32[]{:S(2)}) collective-permute-start(f32[272,128]{1,0:T(8,128)S(1)} %pad_maximum_fusion), channel_id=1, source_target_pairs={{0,1},{1,0},{2,3},{3,2},{4,5},{5,4},{6,7},{7,6},{8,9},{9,8},{10,11... | collective-permute-start | bytes 417800 | tf_op jit(solution)/shard_map/ppermute | solution.py:174
  26.7 8.2 %collective-permute-start.8 = (f32[272,128]{1,0:T(8,128)S(1)}, f32[272,128]{1,0:T(8,128)S(1)}, u32[]{:S(2)}, u32[]{:S(2)}) collective-permute-start(f32[272,128]{1,0:T(8,128)S(1)} %pad_maximum_fusion), channel_id=1, source_target_pairs={{0,2},{1,3},{2,0},{3,1},{4,6},{5,7},{6,4},{7,5},{8,10},{9,11},{10,... | collective-permute-start | bytes 417800 | tf_op jit(solution)/shard_map/ppermute | solution.py:174
  27.6 6.1 %collective-permute-start.11 = (f32[136,128]{1,0:T(8,128)S(1)}, f32[136,128]{1,0:T(8,128)S(1)}, u32[]{:S(2)}, u32[]{:S(2)}) collective-permute-start(f32[136,128]{1,0:T(8,128)S(1)} %add.31.refs_0_), channel_id=1, source_target_pairs={{0,7},{1,6},{2,5},{3,4},{4,3},{5,2},{6,1},{7,0},{8,15},{9,14},{10,... | collective-permute-start | bytes 208904 | tf_op jit(solution)/shard_map/ppermute | solution.py:174
  29.7 5.2 %collective-permute-start.10 = (f32[136,128]{1,0:T(8,128)S(1)}, f32[136,128]{1,0:T(8,128)S(1)}, u32[]{:S(2)}, u32[]{:S(2)}) collective-permute-start(f32[136,128]{1,0:T(8,128)S(1)} %add.31.refs_0_), channel_id=1, source_target_pairs={{0,3},{1,2},{2,1},{3,0},{4,7},{5,6},{6,5},{7,4},{8,11},{9,10},{10,... | collective-permute-start | bytes 208904 | tf_op jit(solution)/shard_map/ppermute | solution.py:174
  42.3 2.0 %collective-permute-start.12 = (bf16[1,512,512]{2,1,0:T(8,128)(2,1)S(1)}, bf16[1,512,512]{2,1,0:T(8,128)(2,1)S(1)}, u32[]{:S(2)}, u32[]{:S(2)}) collective-permute-start(bf16[1,512,512]{2,1,0:T(8,128)(2,1)S(1)} %update.1.value_ref), channel_id=1, source_target_pairs={{0,16},{16,0},{1,17},{17,1},{2,18},{18,2},{3,19},{19,3},{4,20},{20... | collective-permute-start | bytes 1572872 | tf_op jit(solution)/shard_map/ppermute | solution.py:227

commit v8 on v7

--- a/solution.py
+++ b/solution.py
@@ -31,9 +31,10 @@
 LONE = (3, 7)
 TWICE = (2, 1)
 BLOCKS = (0, *[block for partner in TWICE for block in (partner, partner ^ RELAY)], *LONE, RELAY)
-OUT_TWICE = (2,)
-OUT_LONE = (7, 5, 3, 1)
-OUT_BLOCKS = (0, *[block for partner in OUT_TWICE for block in (partner, partner ^ RELAY)], *OUT_LONE, RELAY)
+OUT_RELAY = 2
+OUT_TWICE = (1,)
+OUT_LONE = (7, 6, 5, 4)
+OUT_BLOCKS = (0, *[block for partner in OUT_TWICE for block in (partner, partner ^ OUT_RELAY)], *OUT_LONE, OUT_RELAY)
 
 
 def split(value):
@@ -188,7 +189,7 @@
     twice, lone = arrived[: len(OUT_TWICE)], arrived[len(OUT_TWICE) :]
     relayed = functools.reduce(jnp.add, [value[length:] for value in twice], relayed)
     owned = functools.reduce(jnp.add, [value[:length] for value in twice] + lone, keep)
-    owned = owned + swap(relayed, RELAY)
+    owned = owned + swap(relayed, OUT_RELAY)
     step = GROUP
     while step < size:
         owned = owned + swap(owned, step)

time: 45.3 us -> 45.2 us (level)
  transfers between devices with their start and end apart: 13 -> 13, of which waited for: 9 -> 8; matrix products, arithmetic and copies ran while one was open for 0% -> 0% of each run, Pallas kernels for 2% -> 2%
where the time goes in v8:
time: 45.2 us; the launch traced here: 45.1 us
  starting transfers between devices  21.4 us (47%)
  waiting for transfers between devices  12.4 us (27%)
  Pallas kernels  9.91 us (22%)
  local copies, waits for them, and re-layouts  1.23 us (3%)
    ppermute x12, starting transfers between devices, swap(): lax.ppermute(value, 'tensor', [(i, i ^ partner) for i in range(size)])  21.4 us
    ppermute x12, waiting for transfers between devices, swap(): lax.ppermute(value, 'tensor', [(i, i ^ partner) for i in range(size)])  11.3 us
    pallas_call x1, Pallas kernels, on_device(): pl.pallas_call(functools.partial(update_kernel, gain), out_shape=jax.Shap...  7.44 us
    pallas_call x2, Pallas kernels, place(): pl.pallas_call(functools.partial(place_kernel, flipped), out_shape=jax.Sh...  1.61 us
    unnamed x4, local copies, waits for them, and re-layouts  1.23 us
    ppermute x1, waiting for transfers between devices, on_device(): other = lax.ppermute(update, 'dp', [(0, 1), (1, 0)])  1.08 us
  transfers between devices with their start and end apart: 13, of which 8 were waited for; matrix products, arithmetic and copies ran while one was open for 0% of the time, Pallas kernels for 2%

profile of v8, /device:TPU:0, one launch (start us, length us, event | category | flops | bytes accessed | tf_op | source)
XLA Modules:
  0.0 45.1 jit_solution(11226922481159116867)
XLA Ops:
  0.0 1.2 %copy-done = f32[1,512,512]{2,1,0:T(8,128)S(1)} copy-done((f32[1,512,512]{2,1,0:T(8,128)S(1)}, f32[1,512,512]{2,1,0:T(8,128)}, u32[]{:S(2)}) %copy-start) | copy-done | bytes 1048600
  1.2 0.9 %gram.1 = (f32[136,128]{1,0:T(8,128)S(1)}, f32[272,128]{1,0:T(8,128)S(1)}, f32[136,128]{1,0:T(8,128)S(1)}, f32[136,128]{1,0:T(8,128)S(1)}, f32[136,128]{1,0:T(8,...) custom-call(f32[1,512,512]{2,1,0:T(8,128)S(1)} %copy-done), custom_call_target="tpu_custom_call" | custom-call | tf_op jit(solution)/shard_map/gram/pallas_call | solution.py:179
  2.1 3.0 %collective-permute-start = (f32[272,128]{1,0:T(8,128)S(1)}, f32[272,128]{1,0:T(8,128)S(1)}, u32[]{:S(2)}, u32[]{:S(2)}) collective-permute-start(f32[272,128]{1,0:T(8,128)S(1)} %get-tuple-element.13), channel_id=1, source_target_pairs={{0,1},{1,0},{2,3},{3,2},{4,5},{5,4},{6,7},{7,6},{8,9},{9,8},{10,11... | collective-permute-start | bytes 417800 | tf_op jit(solution)/shard_map/ppermute | solution.py:175
  5.1 2.5 %collective-permute-start.1 = (f32[136,128]{1,0:T(8,128)S(1)}, f32[136,128]{1,0:T(8,128)S(1)}, u32[]{:S(2)}, u32[]{:S(2)}) collective-permute-start(f32[136,128]{1,0:T(8,128)S(1)} %get-tuple-element.14), channel_id=1, source_target_pairs={{0,7},{1,6},{2,5},{3,4},{4,3},{5,2},{6,1},{7,0},{8,15},{9,14},{10,... | collective-permute-start | bytes 208904 | tf_op jit(solution)/shard_map/ppermute | solution.py:175
  7.7 2.9 %collective-permute-start.3 = (f32[136,128]{1,0:T(8,128)S(1)}, f32[136,128]{1,0:T(8,128)S(1)}, u32[]{:S(2)}, u32[]{:S(2)}) collective-permute-start(f32[136,128]{1,0:T(8,128)S(1)} %get-tuple-element.16), channel_id=1, source_target_pairs={{0,5},{1,4},{2,7},{3,6},{4,1},{5,0},{6,3},{7,2},{8,13},{9,12},{10,... | collective-permute-start | bytes 208904 | tf_op jit(solution)/shard_map/ppermute | solution.py:175
  10.5 0.4 collective-permute-start.4
  11.0 1.6 %collective-permute-start.5 = (f32[136,128]{1,0:T(8,128)S(1)}, f32[136,128]{1,0:T(8,128)S(1)}, u32[]{:S(2)}, u32[]{:S(2)}) collective-permute-start(f32[136,128]{1,0:T(8,128)S(1)} %slice_add_fusion), channel_id=1, source_target_pairs={{0,2},{1,3},{2,0},{3,1},{4,6},{5,7},{6,4},{7,5},{8,10},{9,11},{10,... | collective-permute-start | bytes 208904 | tf_op jit(solution)/shard_map/ppermute | solution.py:175
  12.6 0.6 %collective-permute-done.2 = f32[136,128]{1,0:T(8,128)S(1)} collective-permute-done((f32[136,128]{1,0:T(8,128)S(1)}, f32[136,128]{1,0:T(8,128)S(1)}, u32[]{:S(2)}, u32[]{:S(2)}) %collective-permute-start.2) | collective-permute-done | bytes 69664 | tf_op jit(solution)/shard_map/ppermute | solution.py:175
  13.2 1.7 %collective-permute-done.3 = f32[136,128]{1,0:T(8,128)S(1)} collective-permute-done((f32[136,128]{1,0:T(8,128)S(1)}, f32[136,128]{1,0:T(8,128)S(1)}, u32[]{:S(2)}, u32[]{:S(2)}) %collective-permute-start.3) | collective-permute-done | bytes 69664 | tf_op jit(solution)/shard_map/ppermute | solution.py:175
  14.8 0.5 %collective-permute-done.5 = f32[136,128]{1,0:T(8,128)S(1)} collective-permute-done((f32[136,128]{1,0:T(8,128)S(1)}, f32[136,128]{1,0:T(8,128)S(1)}, u32[]{:S(2)}, u32[]{:S(2)}) %collective-permute-start.5) | collective-permute-done | bytes 69664 | tf_op jit(solution)/shard_map/ppermute | solution.py:175
  15.4 2.7 %collective-permute-start.6 = (f32[136,128]{1,0:T(8,128)S(1)}, f32[136,128]{1,0:T(8,128)S(1)}, u32[]{:S(2)}, u32[]{:S(2)}) collective-permute-start(f32[136,128]{1,0:T(8,128)S(1)} %fusion.4), channel_id=1, source_target_pairs={{0,8},{1,9},{2,10},{3,11},{4,12},{5,13},{6,14},{7,15},{8,0},{9,1},... | collective-permute-start | bytes 208904 | tf_op jit(solution)/shard_map/ppermute | solution.py:175
  18.1 2.6 %collective-permute-done.6 = f32[136,128]{1,0:T(8,128)S(1)} collective-permute-done((f32[136,128]{1,0:T(8,128)S(1)}, f32[136,128]{1,0:T(8,128)S(1)}, u32[]{:S(2)}, u32[]{:S(2)}) %collective-permute-start.6) | collective-permute-done | bytes 69664 | tf_op jit(solution)/shard_map/ppermute | solution.py:175
  20.7 1.6 %collective-permute-start.7 = (f32[136,128]{1,0:T(8,128)S(1)}, f32[136,128]{1,0:T(8,128)S(1)}, u32[]{:S(2)}, u32[]{:S(2)}) collective-permute-start(f32[136,128]{1,0:T(8,128)S(1)} %add.31.refs_0_), channel_id=1, source_target_pairs={{0,4},{1,5},{2,6},{3,7},{4,0},{5,1},{6,2},{7,3},{8,12},{9,13},{10,... | collective-permute-start | bytes 208904 | tf_op jit(solution)/shard_map/ppermute | solution.py:175
  22.3 2.7 %collective-permute-done.7.refs_5_ = f32[136,128]{1,0:T(8,128)S(1)} collective-permute-done((f32[136,128]{1,0:T(8,128)S(1)}, f32[136,128]{1,0:T(8,128)S(1)}, u32[]{:S(2)}, u32[]{:S(2)}) %collective-permute-start.7) | collective-permute-done | bytes 69664 | tf_op jit(solution)/shard_map/ppermute | solution.py:175
  25.1 0.9 %collective-permute-start.9 = (f32[272,128]{1,0:T(8,128)S(1)}, f32[272,128]{1,0:T(8,128)S(1)}, u32[]{:S(2)}, u32[]{:S(2)}) collective-permute-start(f32[272,128]{1,0:T(8,128)S(1)} %pad_maximum_fusion), channel_id=1, source_target_pairs={{0,1},{1,0},{2,3},{3,2},{4,5},{5,4},{6,7},{7,6},{8,9},{9,8},{10,11... | collective-permute-start | bytes 417800 | tf_op jit(solution)/shard_map/ppermute | solution.py:175
  25.9 1.8 %collective-permute-start.8 = (f32[272,128]{1,0:T(8,128)S(1)}, f32[272,128]{1,0:T(8,128)S(1)}, u32[]{:S(2)}, u32[]{:S(2)}) collective-permute-start(f32[272,128]{1,0:T(8,128)S(1)} %pad_maximum_fusion), channel_id=1, source_target_pairs={{0,2},{1,3},{2,0},{3,1},{4,6},{5,7},{6,4},{7,5},{8,10},{9,11},{10,... | collective-permute-start | bytes 417800 | tf_op jit(solution)/shard_map/ppermute | solution.py:175
  27.7 1.9 %collective-permute-start.11 = (f32[136,128]{1,0:T(8,128)S(1)}, f32[136,128]{1,0:T(8,128)S(1)}, u32[]{:S(2)}, u32[]{:S(2)}) collective-permute-start(f32[136,128]{1,0:T(8,128)S(1)} %add.31.refs_0_), channel_id=1, source_target_pairs={{0,7},{1,6},{2,5},{3,4},{4,3},{5,2},{6,1},{7,0},{8,15},{9,14},{10,... | collective-permute-start | bytes 208904 | tf_op jit(solution)/shard_map/ppermute | solution.py:175
  29.6 2.0 %collective-permute-start.10 = (f32[136,128]{1,0:T(8,128)S(1)}, f32[136,128]{1,0:T(8,128)S(1)}, u32[]{:S(2)}, u32[]{:S(2)}) collective-permute-start(f32[136,128]{1,0:T(8,128)S(1)} %add.31.refs_0_), channel_id=1, source_target_pairs={{0,3},{1,2},{2,1},{3,0},{4,7},{5,6},{6,5},{7,4},{8,11},{9,10},{10,... | collective-permute-start | bytes 208904 | tf_op jit(solution)/shard_map/ppermute | solution.py:175
  31.7 2.2 %collective-permute-done.11.refs_4_ = f32[136,128]{1,0:T(8,128)S(1)} collective-permute-done((f32[136,128]{1,0:T(8,128)S(1)}, f32[136,128]{1,0:T(8,128)S(1)}, u32[]{:S(2)}, u32[]{:S(2)}) %collective-permute-start.11) | collective-permute-done | bytes 69664 | tf_op jit(solution)/shard_map/ppermute | solution.py:175
  33.8 1.0 %collective-permute-done.10.refs_3_ = f32[136,128]{1,0:T(8,128)S(1)} collective-permute-done((f32[136,128]{1,0:T(8,128)S(1)}, f32[136,128]{1,0:T(8,128)S(1)}, u32[]{:S(2)}, u32[]{:S(2)}) %collective-permute-start.10) | collective-permute-done | bytes 69664 | tf_op jit(solution)/shard_map/ppermute | solution.py:175
  34.9 7.4 %update.1.value_ref = bf16[1,512,512]{2,1,0:T(8,128)(2,1)S(1)} custom-call(f32[136,128]{1,0:T(8,128)S(1)} %add.31.refs_0_, f32[272,128]{1,0:T(8,128)S(1)} %collective-permute-done.8.refs_1_, f32[272,128]{1,0:T(8,128)S(1)} %collective-permute-done.9.refs_2_, f32[136,128]{1,0:T(8,128)S(1)} %collective-permute-done.10.refs_3_, ...), custom_call_target="tpu_custom_call" | custom-call | tf_op jit(solution)/shard_map/update/pallas_call | solution.py:203
  42.4 0.8 %place.2.refs_0_ = bf16[2,512,512]{2,1,0:T(8,128)(2,1)} custom-call(bf16[1,512,512]{2,1,0:T(8,128)(2,1)S(1)} %update.1.value_ref), custom_call_target="tpu_custom_call" | custom-call | flops 1048576 | bytes 524288 | tf_op jit(solution)/shard_map/place/pallas_call | solution.py:216
  43.2 1.1 %collective-permute-done.12.value_ref = bf16[1,512,512]{2,1,0:T(8,128)(2,1)S(1)} collective-permute-done((bf16[1,512,512]{2,1,0:T(8,128)(2,1)S(1)}, bf16[1,512,512]{2,1,0:T(8,128)(2,1)S(1)}, u32[]{:S(2)}, u32[]{:S(2)}) %collective-permute-start.12) | collective-permute-done | bytes 524320 | tf_op jit(solution)/shard_map/ppermute | solution.py:228
  44.3 0.8 %place.3 = bf16[2,512,512]{2,1,0:T(8,128)(2,1)} custom-call(bf16[1,512,512]{2,1,0:T(8,128)(2,1)S(1)} %collective-permute-done.12.value_ref, bf16[2,512,512]{2,1,0:T(8,128)(2,1)} %place.2.refs_0_), custom_call_target="tpu_custom_call", output_to_operand_aliasing={{}: (1, {})} | custom-call | flops 1048576 | bytes 524288 | tf_op jit(solution)/shard_map/place/pallas_call | solution.py:216
  (14 shorter events, 0.2 us)
Async XLA Ops:
  0.0 1.2 %copy-start = (f32[1,512,512]{2,1,0:T(8,128)S(1)}, f32[1,512,512]{2,1,0:T(8,128)}, u32[]{:S(2)}) copy-start(f32[1,512,512]{2,1,0:T(8,128)} %refs_6_.1) | copy-start | bytes 3145732
  1.2 33.6 %copy-start.1 = (f32[1,512,512]{2,1,0:T(8,128)S(1)}, f32[1,512,512]{2,1,0:T(8,128)}, u32[]{:S(2)}) copy-start(f32[1,512,512]{2,1,0:T(8,128)} %refs_6_.1) | copy-start | bytes 3145732
  2.1 8.9 %collective-permute-start = (f32[272,128]{1,0:T(8,128)S(1)}, f32[272,128]{1,0:T(8,128)S(1)}, u32[]{:S(2)}, u32[]{:S(2)}) collective-permute-start(f32[272,128]{1,0:T(8,128)S(1)} %get-tuple-element.13), channel_id=1, source_target_pairs={{0,1},{1,0},{2,3},{3,2},{4,5},{5,4},{6,7},{7,6},{8,9},{9,8},{10,11... | collective-permute-start | bytes 417800 | tf_op jit(solution)/shard_map/ppermute | solution.py:175
  5.1 7.5 %collective-permute-start.1 = (f32[136,128]{1,0:T(8,128)S(1)}, f32[136,128]{1,0:T(8,128)S(1)}, u32[]{:S(2)}, u32[]{:S(2)}) collective-permute-start(f32[136,128]{1,0:T(8,128)S(1)} %get-tuple-element.14), channel_id=1, source_target_pairs={{0,7},{1,6},{2,5},{3,4},{4,3},{5,2},{6,1},{7,0},{8,15},{9,14},{10,... | collective-permute-start | bytes 208904 | tf_op jit(solution)/shard_map/ppermute | solution.py:175
  7.6 5.5 %collective-permute-start.2 = (f32[136,128]{1,0:T(8,128)S(1)}, f32[136,128]{1,0:T(8,128)S(1)}, u32[]{:S(2)}, u32[]{:S(2)}) collective-permute-start(f32[136,128]{1,0:T(8,128)S(1)} %get-tuple-element.15), channel_id=1, source_target_pairs={{0,6},{1,7},{2,4},{3,5},{4,2},{5,3},{6,0},{7,1},{8,14},{9,15},{10,... | collective-permute-start | bytes 208904 | tf_op jit(solution)/shard_map/ppermute | solution.py:175
  7.7 7.2 %collective-permute-start.3 = (f32[136,128]{1,0:T(8,128)S(1)}, f32[136,128]{1,0:T(8,128)S(1)}, u32[]{:S(2)}, u32[]{:S(2)}) collective-permute-start(f32[136,128]{1,0:T(8,128)S(1)} %get-tuple-element.16), channel_id=1, source_target_pairs={{0,5},{1,4},{2,7},{3,6},{4,1},{5,0},{6,3},{7,2},{8,13},{9,12},{10,... | collective-permute-start | bytes 208904 | tf_op jit(solution)/shard_map/ppermute | solution.py:175
  10.5 4.3 %collective-permute-start.4 = (f32[136,128]{1,0:T(8,128)S(1)}, f32[136,128]{1,0:T(8,128)S(1)}, u32[]{:S(2)}, u32[]{:S(2)}) collective-permute-start(f32[136,128]{1,0:T(8,128)S(1)} %get-tuple-element.17), channel_id=1, source_target_pairs={{0,4},{1,5},{2,6},{3,7},{4,0},{5,1},{6,2},{7,3},{8,12},{9,13},{10,... | collective-permute-start | bytes 208904 | tf_op jit(solution)/shard_map/ppermute | solution.py:175
  11.0 4.4 %collective-permute-start.5 = (f32[136,128]{1,0:T(8,128)S(1)}, f32[136,128]{1,0:T(8,128)S(1)}, u32[]{:S(2)}, u32[]{:S(2)}) collective-permute-start(f32[136,128]{1,0:T(8,128)S(1)} %slice_add_fusion), channel_id=1, source_target_pairs={{0,2},{1,3},{2,0},{3,1},{4,6},{5,7},{6,4},{7,5},{8,10},{9,11},{10,... | collective-permute-start | bytes 208904 | tf_op jit(solution)/shard_map/ppermute | solution.py:175
  15.4 5.3 %collective-permute-start.6 = (f32[136,128]{1,0:T(8,128)S(1)}, f32[136,128]{1,0:T(8,128)S(1)}, u32[]{:S(2)}, u32[]{:S(2)}) collective-permute-start(f32[136,128]{1,0:T(8,128)S(1)} %fusion.4), channel_id=1, source_target_pairs={{0,8},{1,9},{2,10},{3,11},{4,12},{5,13},{6,14},{7,15},{8,0},{9,1},... | collective-permute-start | bytes 208904 | tf_op jit(solution)/shard_map/ppermute | solution.py:175
  20.7 4.4 %collective-permute-start.7 = (f32[136,128]{1,0:T(8,128)S(1)}, f32[136,128]{1,0:T(8,128)S(1)}, u32[]{:S(2)}, u32[]{:S(2)}) collective-permute-start(f32[136,128]{1,0:T(8,128)S(1)} %add.31.refs_0_), channel_id=1, source_target_pairs={{0,4},{1,5},{2,6},{3,7},{4,0},{5,1},{6,2},{7,3},{8,12},{9,13},{10,... | collective-permute-start | bytes 208904 | tf_op jit(solution)/shard_map/ppermute | solution.py:175
  25.1 9.8 %collective-permute-start.9 = (f32[272,128]{1,0:T(8,128)S(1)}, f32[272,128]{1,0:T(8,128)S(1)}, u32[]{:S(2)}, u32[]{:S(2)}) collective-permute-start(f32[272,128]{1,0:T(8,128)S(1)} %pad_maximum_fusion), channel_id=1, source_target_pairs={{0,1},{1,0},{2,3},{3,2},{4,5},{5,4},{6,7},{7,6},{8,9},{9,8},{10,11... | collective-permute-start | bytes 417800 | tf_op jit(solution)/shard_map/ppermute | solution.py:175
  25.9 8.9 %collective-permute-start.8 = (f32[272,128]{1,0:T(8,128)S(1)}, f32[272,128]{1,0:T(8,128)S(1)}, u32[]{:S(2)}, u32[]{:S(2)}) collective-permute-start(f32[272,128]{1,0:T(8,128)S(1)} %pad_maximum_fusion), channel_id=1, source_target_pairs={{0,2},{1,3},{2,0},{3,1},{4,6},{5,7},{6,4},{7,5},{8,10},{9,11},{10,... | collective-permute-start | bytes 417800 | tf_op jit(solution)/shard_map/ppermute | solution.py:175
  27.7 6.1 %collective-permute-start.11 = (f32[136,128]{1,0:T(8,128)S(1)}, f32[136,128]{1,0:T(8,128)S(1)}, u32[]{:S(2)}, u32[]{:S(2)}) collective-permute-start(f32[136,128]{1,0:T(8,128)S(1)} %add.31.refs_0_), channel_id=1, source_target_pairs={{0,7},{1,6},{2,5},{3,4},{4,3},{5,2},{6,1},{7,0},{8,15},{9,14},{10,... | collective-permute-start | bytes 208904 | tf_op jit(solution)/shard_map/ppermute | solution.py:175
  29.6 5.2 %collective-permute-start.10 = (f32[136,128]{1,0:T(8,128)S(1)}, f32[136,128]{1,0:T(8,128)S(1)}, u32[]{:S(2)}, u32[]{:S(2)}) collective-permute-start(f32[136,128]{1,0:T(8,128)S(1)} %add.31.refs_0_), channel_id=1, source_target_pairs={{0,3},{1,2},{2,1},{3,0},{4,7},{5,6},{6,5},{7,4},{8,11},{9,10},{10,... | collective-permute-start | bytes 208904 | tf_op jit(solution)/shard_map/ppermute | solution.py:175
  42.3 2.0 %collective-permute-start.12 = (bf16[1,512,512]{2,1,0:T(8,128)(2,1)S(1)}, bf16[1,512,512]{2,1,0:T(8,128)(2,1)S(1)}, u32[]{:S(2)}, u32[]{:S(2)}) collective-permute-start(bf16[1,512,512]{2,1,0:T(8,128)(2,1)S(1)} %update.1.value_ref), channel_id=1, source_target_pairs={{0,16},{16,0},{1,17},{17,1},{2,18},{18,2},{3,19},{19,3},{4,20},{20... | collective-permute-start | bytes 1572872 | tf_op jit(solution)/shard_map/ppermute | solution.py:228
